TPU v7x, 32 devices: a whole 2x2x4 slice. The times are simulated.
32 devices in a mesh: seq: 8 (over y, x, core), head: 4 (over z).
Axes of the slice: x: 2, y: 2, z: 4, core: 2. Of those that a mesh axis runs over, the one named last changes fastest.
Arguments:
- queries: bfloat16 [1024, 1024], P('seq', 'head'), may hold values from -24 to 24
- keys_values: bfloat16 [2, 1024, 128], P(None, 'seq'), may hold values from -6 to 6
- out_weight: bfloat16 [2560, 8, 128], P('head'), may hold values from -0.125 to 0.125
- out_grad: bfloat16 [1024, 2560], P('seq'), may hold values from -6 to 6
- positions: int32 [1024], replicated, may hold values from 0 to 1023, as said below
Outputs:
- d_query: bfloat16 [1024, 1024], P('seq', 'head')
- d_out_weight: float32 [2560, 8, 128], P('seq', 'head')
Inputs may be any that keep to these rules, and one draw needn't show every extreme that they name: positions holds each of 0 to 1023 once, in runs of 64 consecutive rows with consecutive positions, each run starting at a row and a position that are multiples of 64.
All inputs are finite; a program needn't handle non-finite values.
Results may differ from a plain program's by a relative error of at most 0.007.
Values may be sent and summed in bfloat16 or wider, within the bound.
No kernel may reach another device: no remote copies, remote signals or barrier semaphores. Data moves between devices by JAX's collectives and lax.ppermute only.
A program may use at most 64 MiB of HBM per device.

v0:
```python
import math

import jax
import jax.numpy as jnp
from jax import lax
from jax.sharding import PartitionSpec as P

HD = 128
GROUP = 8


big_negative = -1e30


def attend_block(query_rows, query_pos, block_kv, key_pos, scale):
    scores = (
        lax.dot_general(
            query_rows, block_kv[0], (((1,), (1,)), ((), ())), preferred_element_type=jnp.float32
        )
        * scale
    )
    visible = key_pos[None, :] <= query_pos[:, None]
    return (jnp.where(visible, scores, big_negative), visible)


def sweep(step_fn, states, key_piece, offset, positions):
    span_size = key_piece.shape[1]
    block_size = math.gcd(span_size, 1024)

    def step(step_index, inner):
        block_kv = lax.dynamic_slice_in_dim(key_piece, step_index * block_size, block_size, 1)
        key_pos = lax.dynamic_slice_in_dim(
            positions, offset + step_index * block_size, block_size, 0
        )
        return step_fn(inner, block_kv, key_pos)

    return lax.fori_loop(0, span_size // block_size, step, states)


def body(queries, keys_values, out_weight, out_grad, positions):
    token_count = queries.shape[0]
    head_count = queries.shape[1] // HD
    scale = HD ** (-0.5)
    seq_index = lax.axis_index("seq")
    head_index = lax.axis_index("head")
    kv_group = head_index * head_count // GROUP
    own_kv = lax.dynamic_slice_in_dim(keys_values, kv_group * HD, HD, 2)
    own_pos = lax.dynamic_slice_in_dim(positions, seq_index * token_count, token_count, 0)
    query_pos = jnp.repeat(own_pos, head_count)
    query_rows = queries.reshape(token_count * head_count, HD)
    d_attn = jnp.einsum(
        "td,dhc->thc",
        out_grad,
        lax.all_to_all(out_weight, "head", split_axis=1, concat_axis=0, tiled=True),
        preferred_element_type=jnp.float32,
    )
    d_attn = d_attn.astype(jnp.bfloat16).reshape(token_count * head_count, HD)
    row_total = token_count * head_count
    zeros_col = jnp.zeros((row_total, 1), jnp.float32)
    zeros_rows = jnp.zeros((row_total, HD), jnp.float32)
    lowest_col = jnp.full((row_total, 1), big_negative, jnp.float32)
    all_kv = lax.all_gather(own_kv, "seq", axis=1, tiled=True)

    def run_sweep(step_fn, init):
        return sweep(step_fn, init, all_kv, 0, positions)

    def stats_step(states, block_kv, key_pos):
        top, norm = states
        scores, visible = attend_block(query_rows, query_pos, block_kv, key_pos, scale)
        new_top = jnp.maximum(top, jnp.max(scores, axis=1, keepdims=True))
        weights = jnp.where(visible, jnp.exp(scores - new_top), 0.0)
        norm = jnp.exp(top - new_top) * norm + jnp.sum(weights, axis=1, keepdims=True)
        return (new_top, norm)

    top, norm = run_sweep(stats_step, (lowest_col, zeros_col))

    def block_probs(block_kv, key_pos):
        scores, visible = attend_block(query_rows, query_pos, block_kv, key_pos, scale)
        return jnp.where(visible, jnp.exp(scores - top), 0.0) / norm

    def out_step(acc_out, block_kv, key_pos):
        probs = block_probs(block_kv, key_pos)
        return acc_out + jnp.dot(
            probs.astype(jnp.bfloat16), block_kv[1], preferred_element_type=jnp.float32
        )

    attn_full = run_sweep(out_step, zeros_rows)
    delta = jnp.sum(d_attn.astype(jnp.float32) * attn_full, axis=1, keepdims=True)

    def grad_step(acc_grad, block_kv, key_pos):
        probs = block_probs(block_kv, key_pos)
        dprob = lax.dot_general(
            d_attn, block_kv[1], (((1,), (1,)), ((), ())), preferred_element_type=jnp.float32
        )
        dscore = (probs * (dprob - delta)).astype(jnp.bfloat16)
        return acc_grad + jnp.dot(dscore, block_kv[0], preferred_element_type=jnp.float32)

    d_rows = run_sweep(grad_step, zeros_rows) * scale
    attn = attn_full.astype(jnp.bfloat16).reshape(token_count, head_count, HD)
    d_query = d_rows.astype(jnp.bfloat16).reshape(token_count, head_count * HD)
    d_out_weight = lax.psum_scatter(
        jnp.einsum("td,thc->dhc", out_grad, attn, preferred_element_type=jnp.float32),
        "seq",
        scatter_dimension=0,
        tiled=True,
    )
    return (d_query, d_out_weight)


def solution(mesh):
    return jax.shard_map(
        body,
        mesh=mesh,
        in_specs=(
            P("seq", "head"),
            P(None, "seq", None),
            P("head", None, None),
            P("seq", None),
            P(),
        ),
        out_specs=(P("seq", "head"), P("seq", "head", None)),
        check_vma=False,
    )
```

profile of v0, /device:TPU:0, one launch (start us, length us, event | category | flops | bytes accessed | tf_op | source)
XLA Modules:
  0.0 125.0 jit_solution(11164809730574350599)
XLA Ops:
  7.2 0.0 copy-start
  7.2 2.6 %copy.14 = bf16[640,8,128]{2,0,1:T(8,128)(2,1)} copy(bf16[640,8,128]{2,1,0:T(8,128)(2,1)} %param.7) | data formatting | bytes 2621440 | tf_op args[2]
  9.8 0.0 copy-start.8
  9.8 0.0 copy-start.9
  9.8 0.0 copy-start.7
  9.8 6.5 %all-to-all-start = ((bf16[640,8,128]{2,0,1:T(8,128)(2,1)}), bf16[640,8,128]{2,0,1:T(8,128)(2,1)S(1)}, u32[]{:S(2)}, u32[]{:S(2)}) async-start(bf16[640,8,128]{2,0,1:T(8,128)(2,1)} %copy.14), calls=%async_computation | async-start | bytes 2621440 | tf_op jit(solution)/shard_map/all_to_all | solution.py:54
  16.3 0.0 all-reduce.3.cloned.1.call-start
  16.3 0.0 copy-done.8
  16.3 0.0 copy-done.9
  16.3 0.1 dynamic_slice.16
  16.4 0.1 broadcast_in_dim.38
  16.5 0.1 le.51
  16.7 0.0 copy-done.7
  16.7 9.9 %all_gather.3 = bf16[2,1024,128]{2,1,0:T(8,128)(2,1)S(1)} all-gather(bf16[2,128,128]{2,1,0:T(8,128)(2,1)S(1)} %copy-done.7), channel_id=1, replica_groups=mesh['seq'=8,'head'=4] {'seq'}, dimensions={1}, use_global_device_ids=true | all-gather | bytes 589824 | tf_op jit(solution)/shard_map/all_gather | solution.py:62
  26.5 0.0 copy-start.3
  26.5 0.4 fusion.15
  26.9 0.4 fusion.7
  27.3 0.3 fusion.6
  27.6 0.0 copy-start.1
  27.6 20.0 %all-to-all-done = bf16[640,8,128]{2,0,1:T(8,128)(2,1)S(1)} async-done(((bf16[640,8,128]{2,0,1:T(8,128)(2,1)}), bf16[640,8,128]{2,0,1:T(8,128)(2,1)S(1)}, u32[]{:S(2)}, u32[]{:S(2)}) %all-to-all-start) | async-done | bytes 1310752 | tf_op jit(solution)/shard_map/all_to_all | solution.py:54
  47.6 0.1 copy.15
  47.7 0.0 copy-done
  47.7 0.4 convolution_convert_fusion
  48.1 0.1 copy.16
  48.2 0.0 copy-start.5
  48.2 0.0 copy-done.3
  48.2 0.0 copy-done.1
  48.2 0.4 fusion.14
  48.6 0.2 copy-done.5
  48.8 0.5 convolution_bitcast_fusion
  49.3 3.1 %copy.18 = f32[2560,2,128]{2,1,0:T(2,128)} copy(f32[2560,2,128]{0,2,1:T(8,128)S(1)} %convolution_bitcast_fusion) | data formatting | bytes 5242880 | tf_op jit(solution)/shard_map/td,thc->dhc/dot_general | solution.py:102
  52.5 0.0 copy-start.10
  52.5 0.0 copy-start.2
  52.5 0.0 copy-start.4
  52.5 0.0 copy-start.6
  52.5 0.0 all-reduce.3.cloned.1.call-update
  52.5 0.6 copy-done.10
  53.1 0.6 dynamic-slice
  54.4 0.0 copy-done.2
  54.4 0.0 copy-done.4
  54.4 0.0 copy-done.6
  54.4 0.4 fusion.5
  54.8 0.7 reshape.37
  55.5 60.9 %all-reduce.3.cloned.1.call-done = f32[2560,2,128]{2,1,0:T(2,128)} async-done(((f32[2560,2,128]{2,1,0:T(2,128)}), f32[2560,2,128]{2,1,0:T(2,128)}) %all-reduce.3.cloned.1.call-update) | async-done | bytes 2621456
  116.4 1.7 %constant_dynamic-slice_fusion = f32[320,2,128]{2,1,0:T(2,128)} fusion(f32[2560,2,128]{2,1,0:T(2,128)} %all-reduce.3.cloned.1.call-done, u32[]{:T(128)S(6)} %multiply.1), kind=kLoop, calls=%fused_computation.23 | loop fusion | bytes 655364
  (3 shorter events, 0.0 us)
Async XLA Ops:
  7.2 40.6 %copy-start = (bf16[128,2560]{1,0:T(8,128)(2,1)S(1)}, bf16[128,2560]{1,0:T(8,128)(2,1)}, u32[]{:S(2)}) copy-start(bf16[128,2560]{1,0:T(8,128)(2,1)} %param.8) | copy-start | bytes 1966084
  9.8 6.5 %copy-start.8 = (bf16[128,256]{1,0:T(8,128)(2,1)S(1)}, bf16[128,256]{1,0:T(8,128)(2,1)}, u32[]{:S(2)}) copy-start(bf16[128,256]{1,0:T(8,128)(2,1)} %param.5) | copy-start | bytes 196612
  9.8 6.5 %copy-start.9 = (s32[1024]{0:T(1024)S(1)}, s32[1024]{0:T(1024)}, u32[]{:S(2)}) copy-start(s32[1024]{0:T(1024)} %param.9) | copy-start | bytes 12292
  9.8 6.8 %copy-start.7 = (bf16[2,128,128]{2,1,0:T(8,128)(2,1)S(1)}, bf16[2,128,128]{2,1,0:T(8,128)(2,1)}, u32[]{:S(2)}) copy-start(bf16[2,128,128]{2,1,0:T(8,128)(2,1)} %param.6) | copy-start | bytes 196612
  9.8 37.8 %all-to-all-start = ((bf16[640,8,128]{2,0,1:T(8,128)(2,1)}), bf16[640,8,128]{2,0,1:T(8,128)(2,1)S(1)}, u32[]{:S(2)}, u32[]{:S(2)}) async-start(bf16[640,8,128]{2,0,1:T(8,128)(2,1)} %copy.14), calls=%async_computation | async-start | bytes 2621440 | tf_op jit(solution)/shard_map/all_to_all | solution.py:54
  16.3 100.1 %all-reduce.3.cloned.1.call-start = ((), (), s32[]{:S(2)}) async-start(), calls=%async_computation.1 | async-start | bytes 5242880
  26.5 21.7 %copy-start.3 = (bf16[2,1024,128]{2,1,0:T(8,128)(2,1)}, bf16[2,1024,128]{2,1,0:T(8,128)(2,1)S(1)}, u32[]{:S(2)}) copy-start(bf16[2,1024,128]{2,1,0:T(8,128)(2,1)S(1)} %all_gather.3) | copy-start | bytes 1572868
  27.6 20.6 %copy-start.1 = (f32[256,1024]{1,0:T(8,128)}, f32[256,1024]{1,0:T(8,128)S(1)}, u32[]{:S(2)}) copy-start(f32[256,1024]{1,0:T(8,128)S(1)} %fusion.6) | copy-start | bytes 3145732
  48.2 0.6 copy-start.5
  52.5 0.7 copy-start.10
  52.5 1.9 %copy-start.2 = (f32[256,1024]{1,0:T(8,128)S(1)}, f32[256,1024]{1,0:T(8,128)}, u32[]{:S(2)}) copy-start(f32[256,1024]{1,0:T(8,128)} %copy-done.1) | copy-start | bytes 3145732
  52.5 1.9 %copy-start.4 = (bf16[2,1024,128]{2,1,0:T(8,128)(2,1)S(1)}, bf16[2,1024,128]{2,1,0:T(8,128)(2,1)}, u32[]{:S(2)}) copy-start(bf16[2,1024,128]{2,1,0:T(8,128)(2,1)} %copy-done.3) | copy-start | bytes 1572868
  52.5 1.9 %copy-start.6 = (bf16[128,2,128]{2,1,0:T(2,128)(2,1)S(1)}, bf16[128,2,128]{2,1,0:T(2,128)(2,1)}, u32[]{:S(2)}) copy-start(bf16[128,2,128]{2,1,0:T(2,128)(2,1)} %copy-done.5) | copy-start | bytes 196612
Sparse Core Ops, SparseCore 0:
  52.6 63.7 all-reduce.2
where the time goes:
time: 125 us
  waiting for transfers between devices  80.9 us (65%)
  between operations  14.8 us (12%)
  local copies, waits for them, and re-layouts  10.1 us (8%)
  blocking collectives  9.86 us (8%)
  starting transfers between devices  6.48 us (5%)
  matrix products  2.08 us (2%)
    unnamed x2, waiting for transfers between devices  60.9 us
    all_to_all x1, waiting for transfers between devices, body(): lax.all_to_all(out_weight, 'head', split_axis=1, concat_axis=0, tiled=True)  20 us
    all_gather x1, blocking collectives, body(): all_kv = lax.all_gather(own_kv, 'seq', axis=1, tiled=True)  9.86 us
    all_to_all x1, starting transfers between devices, body(): lax.all_to_all(out_weight, 'head', split_axis=1, concat_axis=0, tiled=True)  6.48 us
    unnamed x25, local copies, waits for them, and re-layouts  5.83 us
    dot_general x1, local copies, waits for them, and re-layouts, body(): jnp.einsum('td,thc->dhc', out_grad, attn, preferred_element_type=jnp.floa...  3.14 us
  transfers between devices with their start and end apart: 2, of which 2 were waited for; matrix products, arithmetic and copies ran while one was open for 2% of the time, Pallas kernels for 0%

commit v1 on v0

--- a/solution.py
+++ b/solution.py
@@ -3,7 +3,10 @@
 import jax
 import jax.numpy as jnp
 from jax import lax
+from jax.experimental import pallas as pl
+from jax.experimental.pallas import tpu as pltpu
 from jax.sharding import PartitionSpec as P
+
 
 HD = 128
 GROUP = 8
@@ -37,7 +40,7 @@
     return lax.fori_loop(0, span_size // block_size, step, states)
 
 
-def body(queries, keys_values, out_weight, out_grad, positions):
+def wide_body(queries, keys_values, out_weight, out_grad, positions):
     token_count = queries.shape[0]
     head_count = queries.shape[1] // HD
     scale = HD ** (-0.5)
@@ -107,7 +110,206 @@
     return (d_query, d_out_weight)
 
 
+bf16, f32 = jnp.bfloat16, jnp.float32
+ROWS = (((1,), (1,)), ((), ()))
+COLS = (((0,), (0,)), ((), ()))
+
+
+def dot(left, right, dims=(((1,), (0,)), ((), ()))):
+    return lax.dot_general(left, right, dims, preferred_element_type=f32)
+
+
+def xor_pairs(size, mask):
+    return [(index, index ^ mask) for index in range(size)]
+
+
+def vmem_call(kernel, outs, flops, *args):
+    return pl.pallas_call(
+        kernel,
+        out_shape=[pltpu.VMEM(shape, dtype) for shape, dtype in outs],
+        in_specs=[pl.BlockSpec(memory_space=pltpu.VMEM)] * len(args),
+        out_specs=[pl.BlockSpec(memory_space=pltpu.VMEM)] * len(outs),
+        cost_estimate=pl.CostEstimate(flops=flops, bytes_accessed=1 << 16, transcendentals=0),
+    )(*args)
+
+
+def pack_kernel(kv_ref, query_ref, out_ref):
+    out_ref[:, :HD] = kv_ref[0]
+    out_ref[:, HD : 2 * HD] = kv_ref[1]
+    out_ref[:, 2 * HD :] = query_ref[...]
+
+
+def slice_kernel(grad_ref, *out_refs):
+    pair = lax.axis_index("seq") // 2
+    span = out_refs[0].shape[1]
+    for mask, out_ref in enumerate(out_refs):
+        start = pl.multiple_of((pair ^ mask) * span, 128)
+        out_ref[...] = grad_ref[:, pl.ds(start, span)]
+
+
+def parts_kernel(grad_ref, weight_ref, own_ref, *rest):
+    out_refs, flat = rest[:-1], rest[-1]
+    rows, heads, _ = weight_ref.shape
+    head = lax.axis_index("head")
+    flat[...] = weight_ref[...].reshape(rows * heads, HD).astype(f32)
+    cols = grad_ref[:, pl.ds(pl.multiple_of(head * rows, 128), rows)]
+    per = own_ref.shape[1] // HD
+    for mask, out_ref in enumerate((own_ref, *out_refs)):
+        for h in range(per):
+            weight = flat[pl.ds((head ^ mask) * per + h, rows, stride=heads), :].astype(bf16)
+            out_ref[:, h * HD : (h + 1) * HD] = dot(cols, weight).astype(out_ref.dtype)
+
+
+def join_kernel(*refs):
+    token_refs, out_ref = refs[:-1], refs[-1]
+    rows = token_refs[0].shape[0]
+    for block, ref in enumerate(token_refs):
+        out_ref[block * rows : (block + 1) * rows, :] = ref[:, : 2 * HD]
+
+
+def attention_kernel(pos_ref, near_ref, far_ref, *refs):
+    token_refs, (attn_ref, full_ref, prob_ref) = refs[:-3], refs[-3:]
+    rows = token_refs[0].shape[0]
+    blocks = len(token_refs)
+    seq = lax.axis_index("seq")
+    pair, low = seq // 2, seq % 2
+    places = [
+        pos_ref[pl.ds(2 * (pair ^ mask) + side, 1), :]
+        for side in (low, 1 - low)
+        for mask in range(blocks)
+    ]
+    key_pos = jnp.concatenate(places, axis=1)
+    row_id = lax.broadcasted_iota(jnp.int32, (rows, rows), 0)
+    col_id = lax.broadcasted_iota(jnp.int32, (rows, rows), 1)
+    keys = jnp.concatenate([near_ref[:, :HD], far_ref[:, :HD]], axis=0)
+    values = jnp.concatenate([near_ref[:, HD:], far_ref[:, HD:]], axis=0)
+    scale = HD ** (-0.5)
+    for block, ref in enumerate(token_refs):
+        query_pos = jnp.sum(jnp.where(row_id == col_id, places[block], 0), axis=1, keepdims=True)
+        visible = key_pos <= query_pos
+        for h in range(full_ref.shape[1] // HD):
+            scores = dot(ref[:, (2 + h) * HD : (3 + h) * HD], keys, ROWS) * scale
+            scores = jnp.where(visible, scores, big_negative)
+            top = jnp.max(scores, axis=1, keepdims=True)
+            weights = jnp.exp(scores - top)
+            share = 1.0 / jnp.sum(weights, axis=1, keepdims=True)
+            full = dot(weights.astype(bf16), values) * share
+            attn_ref[block * rows : (block + 1) * rows, h * HD : (h + 1) * HD] = full.astype(bf16)
+            if block == 0:
+                full_ref[:, h * HD : (h + 1) * HD] = full
+                prob_ref[h] = weights * share
+
+
+def query_kernel(near_ref, far_ref, full_ref, prob_ref, own_ref, *refs):
+    part_refs, out_ref = refs[:-1], refs[-1]
+    total = own_ref[...]
+    for ref in part_refs:
+        total = total + ref[...].astype(f32)
+    d_attn = total.astype(bf16)
+    half = near_ref.shape[0]
+    for h in range(prob_ref.shape[0]):
+        cols = slice(h * HD, (h + 1) * HD)
+        grad = d_attn[:, cols]
+        delta = jnp.sum(grad.astype(f32) * full_ref[:, cols], axis=1, keepdims=True)
+        acc = 0.0
+        for side, ref in enumerate((near_ref, far_ref)):
+            dprob = dot(grad, ref[:, HD:], ROWS)
+            prob = prob_ref[h, :, side * half : (side + 1) * half]
+            acc = acc + dot((prob * (dprob - delta)).astype(bf16), ref[:, :HD])
+        out_ref[:, cols] = (acc * HD ** (-0.5)).astype(bf16)
+
+
+def sums_kernel(attn_ref, *refs):
+    grad_refs, (mine_ref, theirs_ref) = refs[:-2], refs[-2:]
+    low = lax.axis_index("seq") % 2
+    grads = jnp.concatenate([ref[...] for ref in grad_refs], axis=0)
+    sums = dot(grads, attn_ref[...], COLS)
+    half = sums.shape[0] // 2
+    mine_ref[pl.ds(0, half), :] = jnp.where(low == 0, sums[:half], sums[half:])
+    theirs_ref[pl.ds(0, half), :] = jnp.where(low == 0, sums[half:], sums[:half])
+
+
+def add_kernel(mine_ref, theirs_ref, out_ref):
+    for h in range(out_ref.shape[1]):
+        cols = slice(h * HD, (h + 1) * HD)
+        out_ref[:, h, :] = mine_ref[:, cols] + theirs_ref[:, cols]
+
+
+def narrow_body(queries, keys_values, out_weight, out_grad, positions, seq_size, head_size):
+    token_count = queries.shape[0]
+    head_count = queries.shape[1] // HD
+    width = head_count * HD
+    head_index = lax.axis_index("head")
+    pair_count = seq_size // 2
+    span = out_grad.shape[1] // pair_count
+    rows_in = out_weight.shape[0]
+    tokens_near = pair_count * token_count
+    if keys_values.shape[2] == HD:
+        own_kv = keys_values
+    else:
+        own_kv = lax.dynamic_slice_in_dim(keys_values, head_index * head_count // GROUP * HD, HD, 2)
+
+    def move(array, axis, size, mask):
+        return lax.ppermute(array, axis, xor_pairs(size, mask))
+
+    masks = range(1, pair_count)
+    (own_tokens,) = vmem_call(
+        pack_kernel, [((token_count, 2 * HD + width), bf16)], 1 << 20, own_kv, queries
+    )
+    tokens = [own_tokens] + [move(own_tokens, "seq", seq_size, 2 * m) for m in masks]
+    grads = vmem_call(slice_kernel, [((token_count, span), bf16)] * pair_count, 1 << 20, out_grad)
+    grads = [grads[0]] + [move(grads[m], "seq", seq_size, 2 * m) for m in masks]
+
+    kinds = [f32] + [bf16] * (head_size - 1)
+    parts = pl.pallas_call(
+        parts_kernel,
+        out_shape=[pltpu.VMEM((token_count, width), kind) for kind in kinds],
+        in_specs=[pl.BlockSpec(memory_space=pltpu.VMEM)] * 2,
+        out_specs=[pl.BlockSpec(memory_space=pltpu.VMEM)] * head_size,
+        scratch_shapes=[pltpu.VMEM((rows_in * out_weight.shape[1], HD), f32)],
+        cost_estimate=pl.CostEstimate(flops=1 << 28, bytes_accessed=1 << 20, transcendentals=0),
+    )(out_grad, out_weight)
+    parts = [parts[0]] + [move(parts[m], "head", head_size, m) for m in range(1, head_size)]
+
+    (near,) = vmem_call(join_kernel, [((tokens_near, 2 * HD), bf16)], 1 << 20, *tokens)
+    far = move(near, "seq", seq_size, 1)
+    attn, full, prob = vmem_call(
+        attention_kernel,
+        [
+            ((tokens_near, width), bf16),
+            ((token_count, width), f32),
+            ((head_count, token_count, 2 * tokens_near), f32),
+        ],
+        1 << 29,
+        positions.reshape(seq_size, token_count),
+        near,
+        far,
+        *tokens,
+    )
+    mine, theirs = vmem_call(sums_kernel, [((span // 2, width), f32)] * 2, 1 << 28, attn, *grads)
+    theirs = move(theirs, "seq", seq_size, 1)
+    d_query = pl.pallas_call(
+        query_kernel,
+        out_shape=jax.ShapeDtypeStruct((token_count, width), bf16),
+        cost_estimate=pl.CostEstimate(flops=1 << 28, bytes_accessed=1 << 20, transcendentals=0),
+    )(near, far, full, prob, *parts)
+    d_out_weight = pl.pallas_call(
+        add_kernel,
+        out_shape=jax.ShapeDtypeStruct((span // 2, head_count, HD), f32),
+        cost_estimate=pl.CostEstimate(flops=1 << 20, bytes_accessed=1 << 20, transcendentals=0),
+    )(mine, theirs)
+    return (d_query, d_out_weight)
+
+
 def solution(mesh):
+    seq_size, head_size = mesh.shape["seq"], mesh.shape["head"]
+    narrow = seq_size in (4, 8) and head_size in (2, 4, 8)
+
+    def body(*arrays):
+        if not narrow:
+            return wide_body(*arrays)
+        return narrow_body(*arrays, seq_size, head_size)
+
     return jax.shard_map(
         body,
         mesh=mesh,

time: 125 us -> 50.6 us (0.40)
  waiting for transfers between devices: 80.9 us -> 12.3 us
  Pallas kernels: 0 us -> 16.3 us
  between operations: 14.8 us -> 0.77 us
  blocking collectives: 9.86 us -> 0 us
  starting transfers between devices: 6.48 us -> 12.5 us
  matrix products: 2.08 us -> 0 us
  local copies, waits for them, and re-layouts: 10.1 us -> 8.39 us
    unnamed x2 -> x0, waiting for transfers between devices: 60.9 us -> none
    all_to_all x1 -> x0, waiting for transfers between devices: 20 us -> none  [body(): lax.all_to_all(out_weight, 'head', split_axis=1, concat_axis=0, tiled=True)]
    pallas_call x0 -> x8, Pallas kernels: none -> 16.3 us  [the longest x5 9.02 us: vmem_call(): pl.pallas_call(kernel, out_shape=[pltpu.VMEM(shape, dtype) for shape, dty...]
    ppermute x0 -> x11, starting transfers between devices: none -> 12.5 us  [move(): return lax.ppermute(array, axis, xor_pairs(size, mask))]
    ppermute x0 -> x11, waiting for transfers between devices: none -> 12.3 us  [move(): return lax.ppermute(array, axis, xor_pairs(size, mask))]
    all_gather x1 -> x0, blocking collectives: 9.86 us -> none  [body(): all_kv = lax.all_gather(own_kv, 'seq', axis=1, tiled=True)]
    all_to_all x1 -> x0, starting transfers between devices: 6.48 us -> none  [body(): lax.all_to_all(out_weight, 'head', split_axis=1, concat_axis=0, tiled=True)]
    dot_general x1 -> x0, local copies, waits for them, and re-layouts: 3.14 us -> none  [body(): jnp.einsum('td,thc->dhc', out_grad, attn, preferred_element_type=jnp.floa...]
  transfers between devices with their start and end apart: 2 -> 11, of which waited for: 2 -> 6; matrix products, arithmetic and copies ran while one was open for 2% -> 0% of each run, Pallas kernels for 0% -> 21%
where the time goes in v1:
time: 50.6 us; the launch traced here: 50.3 us
  Pallas kernels  16.3 us (32%)
  starting transfers between devices  12.5 us (25%)
  waiting for transfers between devices  12.3 us (24%)
  local copies, waits for them, and re-layouts  8.39 us (17%)
  between operations  0.77 us (2%)
    ppermute x11, starting transfers between devices, move(): return lax.ppermute(array, axis, xor_pairs(size, mask))  12.5 us
    ppermute x11, waiting for transfers between devices, move(): return lax.ppermute(array, axis, xor_pairs(size, mask))  12.3 us
    pallas_call x5, Pallas kernels, vmem_call(): pl.pallas_call(kernel, out_shape=[pltpu.VMEM(shape, dtype) for shape, dty...  9.02 us
    unnamed x38, local copies, waits for them, and re-layouts  8.39 us
    pallas_call x1, Pallas kernels, narrow_body(): pl.pallas_call(query_kernel, out_shape=jax.ShapeDtypeStruct((token_count,...  2.72 us
    pallas_call x1, Pallas kernels, narrow_body(): pl.pallas_call(parts_kernel, out_shape=[pltpu.VMEM((token_count, width),...  2.61 us
    pallas_call x1, Pallas kernels, narrow_body(): pl.pallas_call(add_kernel, out_shape=jax.ShapeDtypeStruct((span // 2, hea...  1.99 us
  transfers between devices with their start and end apart: 11, of which 6 were waited for; matrix products, arithmetic and copies ran while one was open for 0% of the time, Pallas kernels for 21%

profile of v1, /device:TPU:0, one launch (start us, length us, event | category | flops | bytes accessed | tf_op | source)
XLA Modules:
  0.0 50.3 jit_solution(879152168889699601)
XLA Ops:
  0.6 0.9 %shard_map.68.refs_0_ = bf16[128,512]{1,0:T(8,128)(2,1)S(1)} custom-call(bf16[2,128,128]{2,1,0:T(8,128)(2,1)} %kv_ref.1, bf16[128,256]{1,0:T(8,128)(2,1)} %query_ref.1), custom_call_target="tpu_custom_call" | custom-call | flops 1048576 | bytes 65536 | tf_op jit(solution)/shard_map/pallas_call | solution.py:127
  1.5 0.0 copy-start.2
  1.5 3.0 %collective-permute-start = (bf16[128,512]{1,0:T(8,128)(2,1)S(1)}, bf16[128,512]{1,0:T(8,128)(2,1)S(1)}, u32[]{:S(2)}, u32[]{:S(2)}) collective-permute-start(bf16[128,512]{1,0:T(8,128)(2,1)S(1)} %shard_map.68.refs_0_), channel_id=1, source_target_pairs={{0,8},{4,12},{8,0},{12,4},{16,24},{20,28},{24,16},{28,20},{1,9},{5... | collective-permute-start | bytes 393224 | tf_op jit(solution)/shard_map/ppermute | solution.py:253
  4.6 1.5 %collective-permute-start.1 = (bf16[128,512]{1,0:T(8,128)(2,1)S(1)}, bf16[128,512]{1,0:T(8,128)(2,1)S(1)}, u32[]{:S(2)}, u32[]{:S(2)}) collective-permute-start(bf16[128,512]{1,0:T(8,128)(2,1)S(1)} %shard_map.68.refs_0_), channel_id=1, source_target_pairs={{0,16},{4,20},{8,24},{12,28},{16,0},{20,4},{24,8},{28,12},{1,17},{... | collective-permute-start | bytes 393224 | tf_op jit(solution)/shard_map/ppermute | solution.py:253
  6.1 0.0 collective-permute-start.2
  6.1 2.3 %collective-permute-done.refs_1_ = bf16[128,512]{1,0:T(8,128)(2,1)S(1)} collective-permute-done((bf16[128,512]{1,0:T(8,128)(2,1)S(1)}, bf16[128,512]{1,0:T(8,128)(2,1)S(1)}, u32[]{:S(2)}, u32[]{:S(2)}) %collective-permute-start) | collective-permute-done | bytes 131104 | tf_op jit(solution)/shard_map/ppermute | solution.py:253
  8.5 3.9 %collective-permute-done.1.refs_2_ = bf16[128,512]{1,0:T(8,128)(2,1)S(1)} collective-permute-done((bf16[128,512]{1,0:T(8,128)(2,1)S(1)}, bf16[128,512]{1,0:T(8,128)(2,1)S(1)}, u32[]{:S(2)}, u32[]{:S(2)}) %collective-permute-start.1) | collective-permute-done | bytes 131104 | tf_op jit(solution)/shard_map/ppermute | solution.py:253
  12.3 0.0 collective-permute-done.2.refs_3_
  12.3 0.0 copy-done.2
  12.4 0.0 copy-done.10
  12.4 0.6 %copy-done.11 = bf16[128,512]{1,0:T(8,128)(2,1)} copy-done((bf16[128,512]{1,0:T(8,128)(2,1)}, bf16[128,512]{1,0:T(8,128)(2,1)S(1)}, u32[]{:S(2)}) %copy-start.11) | copy-done | bytes 131096
  13.0 0.7 %copy-done.12 = bf16[128,512]{1,0:T(8,128)(2,1)} copy-done((bf16[128,512]{1,0:T(8,128)(2,1)}, bf16[128,512]{1,0:T(8,128)(2,1)S(1)}, u32[]{:S(2)}) %copy-start.12) | copy-done | bytes 131096
  13.6 1.1 %shard_map.69.near_ref = bf16[512,256]{1,0:T(8,128)(2,1)S(1)} custom-call(bf16[128,512]{1,0:T(8,128)(2,1)} %copy-done.2, bf16[128,512]{1,0:T(8,128)(2,1)} %copy-done.10, bf16[128,512]{1,0:T(8,128)(2,1)} %copy-done.11, bf16[128,512]{1,0:T(8,128)(2,1)} %copy-done.12), custom_call_target="tpu_custom_call" | custom-call | flops 1048576 | bytes 65536 | tf_op jit(solution)/shard_map/pallas_call | solution.py:127
  14.8 0.0 copy-start.1
  14.8 0.1 collective-permute-start.3
  14.9 1.2 %shard_map.73 = (bf16[128,640]{1,0:T(8,128)(2,1)S(1)}, bf16[128,640]{1,0:T(8,128)(2,1)S(1)}, bf16[128,640]{1,0:T(8,128)(2,1)S(1)}, bf16[128,640]{1,0:T(8,128)(2,1)S(1)}) custom-call(bf16[128,2560]{1,0:T(8,128)(2,1)} %grad_ref.3), custom_call_target="tpu_custom_call" | custom-call | flops 1048576 | bytes 65536 | tf_op jit(solution)/shard_map/pallas_call | solution.py:127
  16.0 0.6 %copy-done.6 = bf16[128,640]{1,0:T(8,128)(2,1)} copy-done((bf16[128,640]{1,0:T(8,128)(2,1)}, bf16[128,640]{1,0:T(8,128)(2,1)S(1)}, u32[]{:S(2)}) %copy-start.6) | copy-done | bytes 163864
  16.7 0.6 %collective-permute-start.7 = (bf16[128,640]{1,0:T(8,128)(2,1)S(1)}, bf16[128,640]{1,0:T(8,128)(2,1)S(1)}, u32[]{:S(2)}, u32[]{:S(2)}) collective-permute-start(bf16[128,640]{1,0:T(8,128)(2,1)S(1)} %get-tuple-element.23), channel_id=1, source_target_pairs={{0,8},{4,12},{8,0},{12,4},{16,24},{20,28},{24,16},{28,20},{1,9},{5... | collective-permute-start | bytes 491528 | tf_op jit(solution)/shard_map/ppermute | solution.py:253
  17.3 1.5 %collective-permute-start.8 = (bf16[128,640]{1,0:T(8,128)(2,1)S(1)}, bf16[128,640]{1,0:T(8,128)(2,1)S(1)}, u32[]{:S(2)}, u32[]{:S(2)}) collective-permute-start(bf16[128,640]{1,0:T(8,128)(2,1)S(1)} %get-tuple-element.24), channel_id=1, source_target_pairs={{0,16},{4,20},{8,24},{12,28},{16,0},{20,4},{24,8},{28,12},{1,17},{... | collective-permute-start | bytes 491528 | tf_op jit(solution)/shard_map/ppermute | solution.py:253
  18.7 1.4 %collective-permute-start.9 = (bf16[128,640]{1,0:T(8,128)(2,1)S(1)}, bf16[128,640]{1,0:T(8,128)(2,1)S(1)}, u32[]{:S(2)}, u32[]{:S(2)}) collective-permute-start(bf16[128,640]{1,0:T(8,128)(2,1)S(1)} %get-tuple-element.25), channel_id=1, source_target_pairs={{0,24},{4,28},{8,16},{12,20},{16,8},{20,12},{24,0},{28,4},{1,25},{... | collective-permute-start | bytes 491528 | tf_op jit(solution)/shard_map/ppermute | solution.py:253
  20.2 0.0 collective-permute-done.3.far_ref
  20.2 0.7 %copy-done.9 = bf16[512,256]{1,0:T(8,128)(2,1)} copy-done((bf16[512,256]{1,0:T(8,128)(2,1)}, bf16[512,256]{1,0:T(8,128)(2,1)S(1)}, u32[]{:S(2)}) %copy-start.9) | copy-done | bytes 262168
  20.9 4.3 %shard_map.70 = (bf16[512,256]{1,0:T(8,128)(2,1)S(1)}, f32[128,256]{1,0:T(8,128)S(1)}, f32[2,128,1024]{2,1,0:T(8,128)S(1)}) custom-call(s32[8,128]{1,0:T(8,128)} %bitcast.1, bf16[512,256]{1,0:T(8,128)(2,1)} %copy-done.1, bf16[512,256]{1,0:T(8,128)(2,1)} %copy-done.9, bf16[128,512]{1,0:T(8,128)(2,1)} %copy-done.2, bf16[128,512]{1,0:T(8,128)(2,1)} %copy-done.10, ...), custom_call_target="tpu_custom_call" | custom-call | flops 536870912 | bytes 65536 | tf_op jit(solution)/shard_map/pallas_call | solution.py:127
  25.1 1.0 %copy-done = f32[2,128,1024]{2,1,0:T(8,128)} copy-done((f32[2,128,1024]{2,1,0:T(8,128)}, f32[2,128,1024]{2,1,0:T(8,128)S(1)}, u32[]{:S(2)}) %copy-start) | copy-done | bytes 1048600
  26.1 0.6 %copy-done.4 = f32[128,256]{1,0:T(8,128)} copy-done((f32[128,256]{1,0:T(8,128)}, f32[128,256]{1,0:T(8,128)S(1)}, u32[]{:S(2)}) %copy-start.4) | copy-done | bytes 131096
  26.8 0.7 %copy-done.7 = bf16[512,256]{1,0:T(8,128)(2,1)} copy-done((bf16[512,256]{1,0:T(8,128)(2,1)}, bf16[512,256]{1,0:T(8,128)(2,1)S(1)}, u32[]{:S(2)}) %copy-start.7) | copy-done | bytes 262168
  27.5 0.0 collective-permute-done.7.refs_1_
  27.5 0.0 collective-permute-done.8.refs_2_
  27.5 0.2 collective-permute-done.9.refs_3_
  27.7 0.5 copy-done.16
  28.2 0.1 copy-done.17
  28.2 0.1 copy-done.18
  28.4 1.6 %shard_map.74 = (f32[320,256]{1,0:T(8,128)S(1)}, f32[320,256]{1,0:T(8,128)S(1)}) custom-call(bf16[512,256]{1,0:T(8,128)(2,1)} %copy-done.7, bf16[128,640]{1,0:T(8,128)(2,1)} %copy-done.6, bf16[128,640]{1,0:T(8,128)(2,1)} %copy-done.16, bf16[128,640]{1,0:T(8,128)(2,1)} %copy-done.17, bf16[128,640]{1,0:T(8,128)(2,1)} %copy-done.18), custom_call_target="tpu_custom_call" | custom-call | flops 268435456 | bytes 65536 | tf_op jit(solution)/shard_map/pallas_call | solution.py:127
  30.0 0.7 %copy-done.3 = f32[320,256]{1,0:T(8,128)} copy-done((f32[320,256]{1,0:T(8,128)}, f32[320,256]{1,0:T(8,128)S(1)}, u32[]{:S(2)}) %copy-start.3) | copy-done | bytes 327704
  30.7 0.0 collective-permute-start.10
  30.7 2.6 %shard_map.71 = (f32[128,256]{1,0:T(8,128)S(1)}, bf16[128,256]{1,0:T(8,128)(2,1)S(1)}, bf16[128,256]{1,0:T(8,128)(2,1)S(1)}, bf16[128,256]{1,0:T(8,128)(2,1)S(1)}) custom-call(bf16[128,2560]{1,0:T(8,128)(2,1)} %grad_ref.3, bf16[640,8,128]{2,1,0:T(8,128)(2,1)} %weight_ref.1), custom_call_target="tpu_custom_call" | custom-call | flops 268435456 | bytes 1048576 | tf_op jit(solution)/shard_map/pallas_call | solution.py:264
  33.4 0.6 %copy-done.5 = f32[128,256]{1,0:T(8,128)} copy-done((f32[128,256]{1,0:T(8,128)}, f32[128,256]{1,0:T(8,128)S(1)}, u32[]{:S(2)}) %copy-start.5) | copy-done | bytes 131096
  34.0 1.6 %collective-permute-start.4 = (bf16[128,256]{1,0:T(8,128)(2,1)S(1)}, bf16[128,256]{1,0:T(8,128)(2,1)S(1)}, u32[]{:S(2)}, u32[]{:S(2)}) collective-permute-start(bf16[128,256]{1,0:T(8,128)(2,1)S(1)} %get-tuple-element.18), channel_id=1, source_target_pairs={{0,1},{1,0},{2,3},{3,2},{4,5},{5,4},{6,7},{7,6},{8,9},{9,8},{10,11... | collective-permute-start | bytes 196616 | tf_op jit(solution)/shard_map/ppermute | solution.py:253
  35.6 2.6 %collective-permute-start.5 = (bf16[128,256]{1,0:T(8,128)(2,1)S(1)}, bf16[128,256]{1,0:T(8,128)(2,1)S(1)}, u32[]{:S(2)}, u32[]{:S(2)}) collective-permute-start(bf16[128,256]{1,0:T(8,128)(2,1)S(1)} %get-tuple-element.19), channel_id=1, source_target_pairs={{0,2},{1,3},{2,0},{3,1},{4,6},{5,7},{6,4},{7,5},{8,10},{9,11},{10,... | collective-permute-start | bytes 196616 | tf_op jit(solution)/shard_map/ppermute | solution.py:253
  38.2 0.2 collective-permute-start.6
  38.4 0.1 collective-permute-done.4.refs_0_
  38.5 4.1 %collective-permute-done.5.refs_1_ = bf16[128,256]{1,0:T(8,128)(2,1)S(1)} collective-permute-done((bf16[128,256]{1,0:T(8,128)(2,1)S(1)}, bf16[128,256]{1,0:T(8,128)(2,1)S(1)}, u32[]{:S(2)}, u32[]{:S(2)}) %collective-permute-start.5) | collective-permute-done | bytes 65568 | tf_op jit(solution)/shard_map/ppermute | solution.py:253
  42.6 1.7 %collective-permute-done.6.refs_2_ = bf16[128,256]{1,0:T(8,128)(2,1)S(1)} collective-permute-done((bf16[128,256]{1,0:T(8,128)(2,1)S(1)}, bf16[128,256]{1,0:T(8,128)(2,1)S(1)}, u32[]{:S(2)}, u32[]{:S(2)}) %collective-permute-start.6) | collective-permute-done | bytes 65568 | tf_op jit(solution)/shard_map/ppermute | solution.py:253
  44.2 0.6 %copy-done.15 = bf16[128,256]{1,0:T(8,128)(2,1)} copy-done((bf16[128,256]{1,0:T(8,128)(2,1)}, bf16[128,256]{1,0:T(8,128)(2,1)S(1)}, u32[]{:S(2)}) %copy-start.15) | copy-done | bytes 65560
  44.9 2.7 %shard_map.72 = bf16[128,256]{1,0:T(8,128)(2,1)} custom-call(bf16[512,256]{1,0:T(8,128)(2,1)} %copy-done.1, bf16[512,256]{1,0:T(8,128)(2,1)} %copy-done.9, f32[128,256]{1,0:T(8,128)} %copy-done.4, f32[2,128,1024]{2,1,0:T(8,128)} %copy-done, f32[128,256]{1,0:T(8,128)} %copy-done.5, bf16[128,256]{1,0:T(8,128)(2,1)} %copy-done.13, bf16[128,256]{1,0:T(8,128)(2,1)} %copy-done.14, ...), custom_call_target="tpu_custom_call" | custom-call | flops 268435456 | bytes 1048576 | tf_op jit(solution)/shard_map/pallas_call | solution.py:291
  47.6 0.0 collective-permute-done.10.theirs_ref
  47.6 0.7 %copy-done.8 = f32[320,256]{1,0:T(8,128)} copy-done((f32[320,256]{1,0:T(8,128)}, f32[320,256]{1,0:T(8,128)S(1)}, u32[]{:S(2)}) %copy-start.8) | copy-done | bytes 327704
  48.3 2.0 %shard_map.75 = f32[320,2,128]{2,1,0:T(2,128)} custom-call(f32[320,256]{1,0:T(8,128)} %copy-done.3, f32[320,256]{1,0:T(8,128)} %copy-done.8), custom_call_target="tpu_custom_call" | custom-call | flops 1048576 | bytes 1048576 | tf_op jit(solution)/shard_map/pallas_call | solution.py:296
  (20 shorter events, 0.0 us)
Async XLA Ops:
  1.5 10.8 %copy-start.2 = (bf16[128,512]{1,0:T(8,128)(2,1)}, bf16[128,512]{1,0:T(8,128)(2,1)S(1)}, u32[]{:S(2)}) copy-start(bf16[128,512]{1,0:T(8,128)(2,1)S(1)} %shard_map.68.refs_0_) | copy-start | bytes 393220
  1.5 6.9 %collective-permute-start = (bf16[128,512]{1,0:T(8,128)(2,1)S(1)}, bf16[128,512]{1,0:T(8,128)(2,1)S(1)}, u32[]{:S(2)}, u32[]{:S(2)}) collective-permute-start(bf16[128,512]{1,0:T(8,128)(2,1)S(1)} %shard_map.68.refs_0_), channel_id=1, source_target_pairs={{0,8},{4,12},{8,0},{12,4},{16,24},{20,28},{24,16},{28,20},{1,9},{5... | collective-permute-start | bytes 393224 | tf_op jit(solution)/shard_map/ppermute | solution.py:253
  4.6 7.8 %collective-permute-start.1 = (bf16[128,512]{1,0:T(8,128)(2,1)S(1)}, bf16[128,512]{1,0:T(8,128)(2,1)S(1)}, u32[]{:S(2)}, u32[]{:S(2)}) collective-permute-start(bf16[128,512]{1,0:T(8,128)(2,1)S(1)} %shard_map.68.refs_0_), channel_id=1, source_target_pairs={{0,16},{4,20},{8,24},{12,28},{16,0},{20,4},{24,8},{28,12},{1,17},{... | collective-permute-start | bytes 393224 | tf_op jit(solution)/shard_map/ppermute | solution.py:253
  6.1 6.3 %collective-permute-start.2 = (bf16[128,512]{1,0:T(8,128)(2,1)S(1)}, bf16[128,512]{1,0:T(8,128)(2,1)S(1)}, u32[]{:S(2)}, u32[]{:S(2)}) collective-permute-start(bf16[128,512]{1,0:T(8,128)(2,1)S(1)} %shard_map.68.refs_0_), channel_id=1, source_target_pairs={{0,24},{4,28},{8,16},{12,20},{16,8},{20,12},{24,0},{28,4},{1,25},{... | collective-permute-start | bytes 393224 | tf_op jit(solution)/shard_map/ppermute | solution.py:253
  8.4 3.9 %copy-start.10 = (bf16[128,512]{1,0:T(8,128)(2,1)}, bf16[128,512]{1,0:T(8,128)(2,1)S(1)}, u32[]{:S(2)}) copy-start(bf16[128,512]{1,0:T(8,128)(2,1)S(1)} %collective-permute-done.refs_1_) | copy-start | bytes 393220
  12.3 0.6 %copy-start.11 = (bf16[128,512]{1,0:T(8,128)(2,1)}, bf16[128,512]{1,0:T(8,128)(2,1)S(1)}, u32[]{:S(2)}) copy-start(bf16[128,512]{1,0:T(8,128)(2,1)S(1)} %collective-permute-done.1.refs_2_) | copy-start | bytes 393220
  13.0 0.7 %copy-start.12 = (bf16[128,512]{1,0:T(8,128)(2,1)}, bf16[128,512]{1,0:T(8,128)(2,1)S(1)}, u32[]{:S(2)}) copy-start(bf16[128,512]{1,0:T(8,128)(2,1)S(1)} %collective-permute-done.2.refs_3_) | copy-start | bytes 393220
  14.8 5.4 %copy-start.1 = (bf16[512,256]{1,0:T(8,128)(2,1)}, bf16[512,256]{1,0:T(8,128)(2,1)S(1)}, u32[]{:S(2)}) copy-start(bf16[512,256]{1,0:T(8,128)(2,1)S(1)} %shard_map.69.near_ref) | copy-start | bytes 786436
  14.8 5.4 %collective-permute-start.3 = (bf16[512,256]{1,0:T(8,128)(2,1)S(1)}, bf16[512,256]{1,0:T(8,128)(2,1)S(1)}, u32[]{:S(2)}, u32[]{:S(2)}) collective-permute-start(bf16[512,256]{1,0:T(8,128)(2,1)S(1)} %shard_map.69.near_ref), channel_id=1, source_target_pairs={{0,4},{4,0},{8,12},{12,8},{16,20},{20,16},{24,28},{28,24},{1,5},{5... | collective-permute-start | bytes 786440 | tf_op jit(solution)/shard_map/ppermute | solution.py:253
  16.0 0.7 %copy-start.6 = (bf16[128,640]{1,0:T(8,128)(2,1)}, bf16[128,640]{1,0:T(8,128)(2,1)S(1)}, u32[]{:S(2)}) copy-start(bf16[128,640]{1,0:T(8,128)(2,1)S(1)} %get-tuple-element.22.refs_0_) | copy-start | bytes 491524
  16.7 10.8 %collective-permute-start.7 = (bf16[128,640]{1,0:T(8,128)(2,1)S(1)}, bf16[128,640]{1,0:T(8,128)(2,1)S(1)}, u32[]{:S(2)}, u32[]{:S(2)}) collective-permute-start(bf16[128,640]{1,0:T(8,128)(2,1)S(1)} %get-tuple-element.23), channel_id=1, source_target_pairs={{0,8},{4,12},{8,0},{12,4},{16,24},{20,28},{24,16},{28,20},{1,9},{5... | collective-permute-start | bytes 491528 | tf_op jit(solution)/shard_map/ppermute | solution.py:253
  17.3 10.2 %collective-permute-start.8 = (bf16[128,640]{1,0:T(8,128)(2,1)S(1)}, bf16[128,640]{1,0:T(8,128)(2,1)S(1)}, u32[]{:S(2)}, u32[]{:S(2)}) collective-permute-start(bf16[128,640]{1,0:T(8,128)(2,1)S(1)} %get-tuple-element.24), channel_id=1, source_target_pairs={{0,16},{4,20},{8,24},{12,28},{16,0},{20,4},{24,8},{28,12},{1,17},{... | collective-permute-start | bytes 491528 | tf_op jit(solution)/shard_map/ppermute | solution.py:253
  18.7 9.0 %collective-permute-start.9 = (bf16[128,640]{1,0:T(8,128)(2,1)S(1)}, bf16[128,640]{1,0:T(8,128)(2,1)S(1)}, u32[]{:S(2)}, u32[]{:S(2)}) collective-permute-start(bf16[128,640]{1,0:T(8,128)(2,1)S(1)} %get-tuple-element.25), channel_id=1, source_target_pairs={{0,24},{4,28},{8,16},{12,20},{16,8},{20,12},{24,0},{28,4},{1,25},{... | collective-permute-start | bytes 491528 | tf_op jit(solution)/shard_map/ppermute | solution.py:253
  20.2 0.7 %copy-start.9 = (bf16[512,256]{1,0:T(8,128)(2,1)}, bf16[512,256]{1,0:T(8,128)(2,1)S(1)}, u32[]{:S(2)}) copy-start(bf16[512,256]{1,0:T(8,128)(2,1)S(1)} %collective-permute-done.3.far_ref) | copy-start | bytes 786436
  25.1 1.0 %copy-start = (f32[2,128,1024]{2,1,0:T(8,128)}, f32[2,128,1024]{2,1,0:T(8,128)S(1)}, u32[]{:S(2)}) copy-start(f32[2,128,1024]{2,1,0:T(8,128)S(1)} %get-tuple-element.16.prob_ref) | copy-start | bytes 3145732
  26.1 0.6 %copy-start.4 = (f32[128,256]{1,0:T(8,128)}, f32[128,256]{1,0:T(8,128)S(1)}, u32[]{:S(2)}) copy-start(f32[128,256]{1,0:T(8,128)S(1)} %get-tuple-element.15.full_ref) | copy-start | bytes 393220
  26.8 0.7 %copy-start.7 = (bf16[512,256]{1,0:T(8,128)(2,1)}, bf16[512,256]{1,0:T(8,128)(2,1)S(1)}, u32[]{:S(2)}) copy-start(bf16[512,256]{1,0:T(8,128)(2,1)S(1)} %get-tuple-element.21.attn_ref) | copy-start | bytes 786436
  27.5 0.7 %copy-start.16 = (bf16[128,640]{1,0:T(8,128)(2,1)}, bf16[128,640]{1,0:T(8,128)(2,1)S(1)}, u32[]{:S(2)}) copy-start(bf16[128,640]{1,0:T(8,128)(2,1)S(1)} %collective-permute-done.7.refs_1_) | copy-start | bytes 491524
  27.5 0.7 %copy-start.17 = (bf16[128,640]{1,0:T(8,128)(2,1)}, bf16[128,640]{1,0:T(8,128)(2,1)S(1)}, u32[]{:S(2)}) copy-start(bf16[128,640]{1,0:T(8,128)(2,1)S(1)} %collective-permute-done.8.refs_2_) | copy-start | bytes 491524
  27.7 0.7 %copy-start.18 = (bf16[128,640]{1,0:T(8,128)(2,1)}, bf16[128,640]{1,0:T(8,128)(2,1)S(1)}, u32[]{:S(2)}) copy-start(bf16[128,640]{1,0:T(8,128)(2,1)S(1)} %collective-permute-done.9.refs_3_) | copy-start | bytes 491524
  30.0 0.7 %copy-start.3 = (f32[320,256]{1,0:T(8,128)}, f32[320,256]{1,0:T(8,128)S(1)}, u32[]{:S(2)}) copy-start(f32[320,256]{1,0:T(8,128)S(1)} %get-tuple-element.26.mine_ref) | copy-start | bytes 983044
  30.7 16.9 %collective-permute-start.10 = (f32[320,256]{1,0:T(8,128)S(1)}, f32[320,256]{1,0:T(8,128)S(1)}, u32[]{:S(2)}, u32[]{:S(2)}) collective-permute-start(f32[320,256]{1,0:T(8,128)S(1)} %get-tuple-element.27), channel_id=1, source_target_pairs={{0,4},{4,0},{8,12},{12,8},{16,20},{20,16},{24,28},{28,24},{1,5},{5... | collective-permute-start | bytes 983048 | tf_op jit(solution)/shard_map/ppermute | solution.py:253
  33.3 0.6 %copy-start.5 = (f32[128,256]{1,0:T(8,128)}, f32[128,256]{1,0:T(8,128)S(1)}, u32[]{:S(2)}) copy-start(f32[128,256]{1,0:T(8,128)S(1)} %get-tuple-element.17.own_ref) | copy-start | bytes 393220
  34.0 4.5 %collective-permute-start.4 = (bf16[128,256]{1,0:T(8,128)(2,1)S(1)}, bf16[128,256]{1,0:T(8,128)(2,1)S(1)}, u32[]{:S(2)}, u32[]{:S(2)}) collective-permute-start(bf16[128,256]{1,0:T(8,128)(2,1)S(1)} %get-tuple-element.18), channel_id=1, source_target_pairs={{0,1},{1,0},{2,3},{3,2},{4,5},{5,4},{6,7},{7,6},{8,9},{9,8},{10,11... | collective-permute-start | bytes 196616 | tf_op jit(solution)/shard_map/ppermute | solution.py:253
  35.6 7.0 %collective-permute-start.5 = (bf16[128,256]{1,0:T(8,128)(2,1)S(1)}, bf16[128,256]{1,0:T(8,128)(2,1)S(1)}, u32[]{:S(2)}, u32[]{:S(2)}) collective-permute-start(bf16[128,256]{1,0:T(8,128)(2,1)S(1)} %get-tuple-element.19), channel_id=1, source_target_pairs={{0,2},{1,3},{2,0},{3,1},{4,6},{5,7},{6,4},{7,5},{8,10},{9,11},{10,... | collective-permute-start | bytes 196616 | tf_op jit(solution)/shard_map/ppermute | solution.py:253
  38.2 6.1 %collective-permute-start.6 = (bf16[128,256]{1,0:T(8,128)(2,1)S(1)}, bf16[128,256]{1,0:T(8,128)(2,1)S(1)}, u32[]{:S(2)}, u32[]{:S(2)}) collective-permute-start(bf16[128,256]{1,0:T(8,128)(2,1)S(1)} %get-tuple-element.20), channel_id=1, source_target_pairs={{0,3},{1,2},{2,1},{3,0},{4,7},{5,6},{6,5},{7,4},{8,11},{9,10},{10,... | collective-permute-start | bytes 196616 | tf_op jit(solution)/shard_map/ppermute | solution.py:253
  38.5 5.7 %copy-start.13 = (bf16[128,256]{1,0:T(8,128)(2,1)}, bf16[128,256]{1,0:T(8,128)(2,1)S(1)}, u32[]{:S(2)}) copy-start(bf16[128,256]{1,0:T(8,128)(2,1)S(1)} %collective-permute-done.4.refs_0_) | copy-start | bytes 196612
  42.6 1.7 %copy-start.14 = (bf16[128,256]{1,0:T(8,128)(2,1)}, bf16[128,256]{1,0:T(8,128)(2,1)S(1)}, u32[]{:S(2)}) copy-start(bf16[128,256]{1,0:T(8,128)(2,1)S(1)} %collective-permute-done.5.refs_1_) | copy-start | bytes 196612
  44.2 0.6 %copy-start.15 = (bf16[128,256]{1,0:T(8,128)(2,1)}, bf16[128,256]{1,0:T(8,128)(2,1)S(1)}, u32[]{:S(2)}) copy-start(bf16[128,256]{1,0:T(8,128)(2,1)S(1)} %collective-permute-done.6.refs_2_) | copy-start | bytes 196612
  47.6 0.7 %copy-start.8 = (f32[320,256]{1,0:T(8,128)}, f32[320,256]{1,0:T(8,128)S(1)}, u32[]{:S(2)}) copy-start(f32[320,256]{1,0:T(8,128)S(1)} %collective-permute-done.10.theirs_ref) | copy-start | bytes 983044

commit v2 on v1

--- a/solution.py
+++ b/solution.py
@@ -123,20 +123,32 @@
     return [(index, index ^ mask) for index in range(size)]
 
 
-def vmem_call(kernel, outs, flops, *args):
+def vmem_call(kernel, outs, flops, limit, *args):
     return pl.pallas_call(
         kernel,
         out_shape=[pltpu.VMEM(shape, dtype) for shape, dtype in outs],
         in_specs=[pl.BlockSpec(memory_space=pltpu.VMEM)] * len(args),
         out_specs=[pl.BlockSpec(memory_space=pltpu.VMEM)] * len(outs),
         cost_estimate=pl.CostEstimate(flops=flops, bytes_accessed=1 << 16, transcendentals=0),
+        compiler_params=pltpu.CompilerParams(vmem_limit_bytes=limit << 20),
     )(*args)
 
 
-def pack_kernel(kv_ref, query_ref, out_ref):
-    out_ref[:, :HD] = kv_ref[0]
-    out_ref[:, HD : 2 * HD] = kv_ref[1]
-    out_ref[:, 2 * HD :] = query_ref[...]
+def pack_kernel(kv_ref, query_ref, out_ref, sems):
+    copies = [
+        pltpu.make_async_copy(source, out_ref.at[:, cols], sems.at[index])
+        for index, (source, cols) in enumerate(
+            (
+                (kv_ref.at[0], slice(0, HD)),
+                (kv_ref.at[1], slice(HD, 2 * HD)),
+                (query_ref, slice(2 * HD, out_ref.shape[1])),
+            )
+        )
+    ]
+    for copy in copies:
+        copy.start()
+    for copy in copies:
+        copy.wait()
 
 
 def slice_kernel(grad_ref, *out_refs):
@@ -253,11 +265,22 @@
         return lax.ppermute(array, axis, xor_pairs(size, mask))
 
     masks = range(1, pair_count)
-    (own_tokens,) = vmem_call(
-        pack_kernel, [((token_count, 2 * HD + width), bf16)], 1 << 20, own_kv, queries
+    own_tokens = pl.pallas_call(
+        pack_kernel,
+        out_shape=pltpu.VMEM((token_count, 2 * HD + width), bf16),
+        in_specs=[pl.BlockSpec(memory_space=pltpu.HBM)] * 2,
+        out_specs=pl.BlockSpec(memory_space=pltpu.VMEM),
+        scratch_shapes=[pltpu.SemaphoreType.DMA((3,))],
+        cost_estimate=pl.CostEstimate(flops=1 << 32, bytes_accessed=1 << 18, transcendentals=0),
+        compiler_params=pltpu.CompilerParams(vmem_limit_bytes=2 << 20),
+    )(
+        pltpu.with_memory_space_constraint(own_kv, pltpu.HBM),
+        pltpu.with_memory_space_constraint(queries, pltpu.HBM),
     )
     tokens = [own_tokens] + [move(own_tokens, "seq", seq_size, 2 * m) for m in masks]
-    grads = vmem_call(slice_kernel, [((token_count, span), bf16)] * pair_count, 1 << 20, out_grad)
+    grads = vmem_call(
+        slice_kernel, [((token_count, span), bf16)] * pair_count, 1 << 32, 4, out_grad
+    )
     grads = [grads[0]] + [move(grads[m], "seq", seq_size, 2 * m) for m in masks]
 
     kinds = [f32] + [bf16] * (head_size - 1)
@@ -268,10 +291,11 @@
         out_specs=[pl.BlockSpec(memory_space=pltpu.VMEM)] * head_size,
         scratch_shapes=[pltpu.VMEM((rows_in * out_weight.shape[1], HD), f32)],
         cost_estimate=pl.CostEstimate(flops=1 << 28, bytes_accessed=1 << 20, transcendentals=0),
+        compiler_params=pltpu.CompilerParams(vmem_limit_bytes=16 << 20),
     )(out_grad, out_weight)
     parts = [parts[0]] + [move(parts[m], "head", head_size, m) for m in range(1, head_size)]
 
-    (near,) = vmem_call(join_kernel, [((tokens_near, 2 * HD), bf16)], 1 << 20, *tokens)
+    (near,) = vmem_call(join_kernel, [((tokens_near, 2 * HD), bf16)], 1 << 20, 2, *tokens)
     far = move(near, "seq", seq_size, 1)
     attn, full, prob = vmem_call(
         attention_kernel,
@@ -281,22 +305,27 @@
             ((head_count, token_count, 2 * tokens_near), f32),
         ],
         1 << 29,
+        24,
         positions.reshape(seq_size, token_count),
         near,
         far,
         *tokens,
     )
-    mine, theirs = vmem_call(sums_kernel, [((span // 2, width), f32)] * 2, 1 << 28, attn, *grads)
+    mine, theirs = vmem_call(
+        sums_kernel, [((span // 2, width), f32)] * 2, 1 << 28, 12, attn, *grads
+    )
     theirs = move(theirs, "seq", seq_size, 1)
     d_query = pl.pallas_call(
         query_kernel,
         out_shape=jax.ShapeDtypeStruct((token_count, width), bf16),
         cost_estimate=pl.CostEstimate(flops=1 << 28, bytes_accessed=1 << 20, transcendentals=0),
+        compiler_params=pltpu.CompilerParams(vmem_limit_bytes=8 << 20),
     )(near, far, full, prob, *parts)
     d_out_weight = pl.pallas_call(
         add_kernel,
         out_shape=jax.ShapeDtypeStruct((span // 2, head_count, HD), f32),
         cost_estimate=pl.CostEstimate(flops=1 << 20, bytes_accessed=1 << 20, transcendentals=0),
+        compiler_params=pltpu.CompilerParams(vmem_limit_bytes=4 << 20),
     )(mine, theirs)
     return (d_query, d_out_weight)
 

time: 50.6 us -> 38 us (0.75)
  Pallas kernels: 16.3 us -> 7.8 us
  local copies, waits for them, and re-layouts: 8.39 us -> 0.01 us
  waiting for transfers between devices: 12.3 us -> 16.6 us
    unnamed x38 -> x6, local copies, waits for them, and re-layouts: 8.39 us -> 0.01 us
    pallas_call x5 -> x4, Pallas kernels: 9.02 us -> 3.52 us  [vmem_call(): pl.pallas_call(kernel, out_shape=[pltpu.VMEM(shape, dtype) for shape, dty...]
    ppermute x11, waiting for transfers between devices: 12.3 us -> 16.6 us  [move(): return lax.ppermute(array, axis, xor_pairs(size, mask))]
    pallas_call x1, Pallas kernels: 2.61 us -> 1.1 us  [narrow_body(): pl.pallas_call(parts_kernel, out_shape=[pltpu.VMEM((token_count, width),...]
    pallas_call x1, Pallas kernels: 2.72 us -> 1.29 us  [narrow_body(): pl.pallas_call(query_kernel, out_shape=jax.ShapeDtypeStruct((token_count,...]
    pallas_call x1, Pallas kernels: 1.99 us -> 0.92 us  [narrow_body(): pl.pallas_call(add_kernel, out_shape=jax.ShapeDtypeStruct((span // 2, hea...]
    pallas_call x0 -> x1, Pallas kernels: none -> 0.96 us  [narrow_body(): pl.pallas_call(pack_kernel, out_shape=pltpu.VMEM((token_count, 2 * HD + w...]
  transfers between devices with their start and end apart: 11 -> 11, of which waited for: 6 -> 8; matrix products, arithmetic and copies ran while one was open for 0% -> 0% of each run, Pallas kernels for 21% -> 15%
where the time goes in v2:
time: 38 us; the launch traced here: 37.8 us
  waiting for transfers between devices  16.6 us (44%)
  starting transfers between devices  12.7 us (33%)
  Pallas kernels  7.8 us (21%)
  between operations  0.73 us (2%)
    ppermute x11, waiting for transfers between devices, move(): return lax.ppermute(array, axis, xor_pairs(size, mask))  16.6 us
    ppermute x11, starting transfers between devices, move(): return lax.ppermute(array, axis, xor_pairs(size, mask))  12.7 us
    pallas_call x4, Pallas kernels, vmem_call(): pl.pallas_call(kernel, out_shape=[pltpu.VMEM(shape, dtype) for shape, dty...  3.52 us
    pallas_call x1, Pallas kernels, narrow_body(): pl.pallas_call(query_kernel, out_shape=jax.ShapeDtypeStruct((token_count,...  1.29 us
    pallas_call x1, Pallas kernels, narrow_body(): pl.pallas_call(parts_kernel, out_shape=[pltpu.VMEM((token_count, width),...  1.1 us
    pallas_call x1, Pallas kernels, narrow_body(): pl.pallas_call(pack_kernel, out_shape=pltpu.VMEM((token_count, 2 * HD + w...  0.96 us
    pallas_call x1, Pallas kernels, narrow_body(): pl.pallas_call(add_kernel, out_shape=jax.ShapeDtypeStruct((span // 2, hea...  0.92 us
  transfers between devices with their start and end apart: 11, of which 8 were waited for; matrix products, arithmetic and copies ran while one was open for 0% of the time, Pallas kernels for 15%

profile of v2, /device:TPU:0, one launch (start us, length us, event | category | flops | bytes accessed | tf_op | source)
XLA Modules:
  0.0 37.8 jit_solution(2678114328959461024)
XLA Ops:
  0.6 0.0 copy-start.1
  0.6 1.0 %shard_map.68.refs_0_ = bf16[128,512]{1,0:T(8,128)(2,1)S(1)} custom-call(bf16[2,128,128]{2,1,0:T(8,128)(2,1)} %kv_ref.1, bf16[128,256]{1,0:T(8,128)(2,1)} %query_ref.1), custom_call_target="tpu_custom_call" | custom-call | flops 4294967296 | bytes 262144 | tf_op jit(solution)/shard_map/pallas_call | solution.py:268
  1.6 3.0 %collective-permute-start = (bf16[128,512]{1,0:T(8,128)(2,1)S(1)}, bf16[128,512]{1,0:T(8,128)(2,1)S(1)}, u32[]{:S(2)}, u32[]{:S(2)}) collective-permute-start(bf16[128,512]{1,0:T(8,128)(2,1)S(1)} %shard_map.68.refs_0_), channel_id=1, source_target_pairs={{0,8},{4,12},{8,0},{12,4},{16,24},{20,28},{24,16},{28,20},{1,9},{5... | collective-permute-start | bytes 393224 | tf_op jit(solution)/shard_map/ppermute | solution.py:265
  4.6 1.5 %collective-permute-start.1 = (bf16[128,512]{1,0:T(8,128)(2,1)S(1)}, bf16[128,512]{1,0:T(8,128)(2,1)S(1)}, u32[]{:S(2)}, u32[]{:S(2)}) collective-permute-start(bf16[128,512]{1,0:T(8,128)(2,1)S(1)} %shard_map.68.refs_0_), channel_id=1, source_target_pairs={{0,16},{4,20},{8,24},{12,28},{16,0},{20,4},{24,8},{28,12},{1,17},{... | collective-permute-start | bytes 393224 | tf_op jit(solution)/shard_map/ppermute | solution.py:265
  6.2 0.0 collective-permute-start.2
  6.2 2.3 %collective-permute-done.refs_1_ = bf16[128,512]{1,0:T(8,128)(2,1)S(1)} collective-permute-done((bf16[128,512]{1,0:T(8,128)(2,1)S(1)}, bf16[128,512]{1,0:T(8,128)(2,1)S(1)}, u32[]{:S(2)}, u32[]{:S(2)}) %collective-permute-start) | collective-permute-done | bytes 131104 | tf_op jit(solution)/shard_map/ppermute | solution.py:265
  8.5 3.9 %collective-permute-done.1.refs_2_ = bf16[128,512]{1,0:T(8,128)(2,1)S(1)} collective-permute-done((bf16[128,512]{1,0:T(8,128)(2,1)S(1)}, bf16[128,512]{1,0:T(8,128)(2,1)S(1)}, u32[]{:S(2)}, u32[]{:S(2)}) %collective-permute-start.1) | collective-permute-done | bytes 131104 | tf_op jit(solution)/shard_map/ppermute | solution.py:265
  12.4 0.0 collective-permute-done.2.refs_3_
  12.4 0.0 copy-start.2
  12.5 0.1 collective-permute-start.3
  12.5 0.0 copy-done.1
  12.5 0.1 shard_map.73
  12.6 1.3 %collective-permute-start.7 = (bf16[128,640]{1,0:T(8,128)(2,1)S(1)}, bf16[128,640]{1,0:T(8,128)(2,1)S(1)}, u32[]{:S(2)}, u32[]{:S(2)}) collective-permute-start(bf16[128,640]{1,0:T(8,128)(2,1)S(1)} %get-tuple-element.23), channel_id=1, source_target_pairs={{0,8},{4,12},{8,0},{12,4},{16,24},{20,28},{24,16},{28,20},{1,9},{5... | collective-permute-start | bytes 491528 | tf_op jit(solution)/shard_map/ppermute | solution.py:265
  13.9 0.8 %collective-permute-start.8 = (bf16[128,640]{1,0:T(8,128)(2,1)S(1)}, bf16[128,640]{1,0:T(8,128)(2,1)S(1)}, u32[]{:S(2)}, u32[]{:S(2)}) collective-permute-start(bf16[128,640]{1,0:T(8,128)(2,1)S(1)} %get-tuple-element.24), channel_id=1, source_target_pairs={{0,16},{4,20},{8,24},{12,28},{16,0},{20,4},{24,8},{28,12},{1,17},{... | collective-permute-start | bytes 491528 | tf_op jit(solution)/shard_map/ppermute | solution.py:265
  14.7 1.4 %collective-permute-start.9 = (bf16[128,640]{1,0:T(8,128)(2,1)S(1)}, bf16[128,640]{1,0:T(8,128)(2,1)S(1)}, u32[]{:S(2)}, u32[]{:S(2)}) collective-permute-start(bf16[128,640]{1,0:T(8,128)(2,1)S(1)} %get-tuple-element.25), channel_id=1, source_target_pairs={{0,24},{4,28},{8,16},{12,20},{16,8},{20,12},{24,0},{28,4},{1,25},{... | collective-permute-start | bytes 491528 | tf_op jit(solution)/shard_map/ppermute | solution.py:265
  16.2 0.0 collective-permute-done.3.far_ref
  16.2 0.0 copy-done.2
  16.2 0.0 copy-start
  16.2 3.1 %shard_map.70 = (bf16[512,256]{1,0:T(8,128)(2,1)S(1)}, f32[128,256]{1,0:T(8,128)S(1)}, f32[2,128,1024]{2,1,0:T(8,128)S(1)}) custom-call(s32[8,128]{1,0:T(8,128)S(1)} %bitcast.1, bf16[512,256]{1,0:T(8,128)(2,1)S(1)} %shard_map.69.near_ref, bf16[512,256]{1,0:T(8,128)(2,1)S(1)} %collective-permute-done.3.far_ref, bf16[128,512]{1,0:T(8,128)(2,1)S(1)} %shard_map.68.refs_0_, ...), custom_call_target="tpu_custom_call" | custom-call | flops 536870912 | bytes 65536 | tf_op jit(solution)/shard_map/pallas_call | solution.py:127
  19.3 0.5 %collective-permute-done.7.refs_1_ = bf16[128,640]{1,0:T(8,128)(2,1)S(1)} collective-permute-done((bf16[128,640]{1,0:T(8,128)(2,1)S(1)}, bf16[128,640]{1,0:T(8,128)(2,1)S(1)}, u32[]{:S(2)}, u32[]{:S(2)}) %collective-permute-start.7) | collective-permute-done | bytes 163872 | tf_op jit(solution)/shard_map/ppermute | solution.py:265
  19.8 2.3 %collective-permute-done.8.refs_2_ = bf16[128,640]{1,0:T(8,128)(2,1)S(1)} collective-permute-done((bf16[128,640]{1,0:T(8,128)(2,1)S(1)}, bf16[128,640]{1,0:T(8,128)(2,1)S(1)}, u32[]{:S(2)}, u32[]{:S(2)}) %collective-permute-start.8) | collective-permute-done | bytes 163872 | tf_op jit(solution)/shard_map/ppermute | solution.py:265
  22.1 1.6 %collective-permute-done.9.refs_3_ = bf16[128,640]{1,0:T(8,128)(2,1)S(1)} collective-permute-done((bf16[128,640]{1,0:T(8,128)(2,1)S(1)}, bf16[128,640]{1,0:T(8,128)(2,1)S(1)}, u32[]{:S(2)}, u32[]{:S(2)}) %collective-permute-start.9) | collective-permute-done | bytes 163872 | tf_op jit(solution)/shard_map/ppermute | solution.py:265
  23.7 0.4 shard_map.74
  24.1 0.1 collective-permute-start.10
  24.2 0.0 copy-done
  24.2 1.1 %shard_map.71 = (f32[128,256]{1,0:T(8,128)S(1)}, bf16[128,256]{1,0:T(8,128)(2,1)S(1)}, bf16[128,256]{1,0:T(8,128)(2,1)S(1)}, bf16[128,256]{1,0:T(8,128)(2,1)S(1)}) custom-call(bf16[128,2560]{1,0:T(8,128)(2,1)S(1)} %copy-done.1, bf16[640,8,128]{2,1,0:T(8,128)(2,1)S(1)} %copy-done), custom_call_target="tpu_custom_call" | custom-call | flops 268435456 | bytes 1048576 | tf_op jit(solution)/shard_map/pallas_call | solution.py:287
  25.3 1.6 %collective-permute-start.4 = (bf16[128,256]{1,0:T(8,128)(2,1)S(1)}, bf16[128,256]{1,0:T(8,128)(2,1)S(1)}, u32[]{:S(2)}, u32[]{:S(2)}) collective-permute-start(bf16[128,256]{1,0:T(8,128)(2,1)S(1)} %get-tuple-element.18), channel_id=1, source_target_pairs={{0,1},{1,0},{2,3},{3,2},{4,5},{5,4},{6,7},{7,6},{8,9},{9,8},{10,11... | collective-permute-start | bytes 196616 | tf_op jit(solution)/shard_map/ppermute | solution.py:265
  26.9 2.6 %collective-permute-start.5 = (bf16[128,256]{1,0:T(8,128)(2,1)S(1)}, bf16[128,256]{1,0:T(8,128)(2,1)S(1)}, u32[]{:S(2)}, u32[]{:S(2)}) collective-permute-start(bf16[128,256]{1,0:T(8,128)(2,1)S(1)} %get-tuple-element.19), channel_id=1, source_target_pairs={{0,2},{1,3},{2,0},{3,1},{4,6},{5,7},{6,4},{7,5},{8,10},{9,11},{10,... | collective-permute-start | bytes 196616 | tf_op jit(solution)/shard_map/ppermute | solution.py:265
  29.5 0.2 collective-permute-start.6
  29.8 0.1 collective-permute-done.4.refs_0_
  29.9 4.1 %collective-permute-done.5.refs_1_ = bf16[128,256]{1,0:T(8,128)(2,1)S(1)} collective-permute-done((bf16[128,256]{1,0:T(8,128)(2,1)S(1)}, bf16[128,256]{1,0:T(8,128)(2,1)S(1)}, u32[]{:S(2)}, u32[]{:S(2)}) %collective-permute-start.5) | collective-permute-done | bytes 65568 | tf_op jit(solution)/shard_map/ppermute | solution.py:265
  33.9 1.7 %collective-permute-done.6.refs_2_ = bf16[128,256]{1,0:T(8,128)(2,1)S(1)} collective-permute-done((bf16[128,256]{1,0:T(8,128)(2,1)S(1)}, bf16[128,256]{1,0:T(8,128)(2,1)S(1)}, u32[]{:S(2)}, u32[]{:S(2)}) %collective-permute-start.6) | collective-permute-done | bytes 65568 | tf_op jit(solution)/shard_map/ppermute | solution.py:265
  35.6 1.3 %shard_map.72 = bf16[128,256]{1,0:T(8,128)(2,1)} custom-call(bf16[512,256]{1,0:T(8,128)(2,1)S(1)} %shard_map.69.near_ref, bf16[512,256]{1,0:T(8,128)(2,1)S(1)} %collective-permute-done.3.far_ref, f32[128,256]{1,0:T(8,128)S(1)} %get-tuple-element.15.full_ref, f32[2,128,1024]{2,1,0:T(8,128)S(1)} %get-tuple-element.16.prob_ref, ...), custom_call_target="tpu_custom_call" | custom-call | flops 268435456 | bytes 1048576 | tf_op jit(solution)/shard_map/pallas_call | solution.py:318
  36.9 0.0 collective-permute-done.10.theirs_ref
  36.9 0.9 %shard_map.75 = f32[320,2,128]{2,1,0:T(2,128)} custom-call(f32[320,256]{1,0:T(8,128)S(1)} %get-tuple-element.26.mine_ref, f32[320,256]{1,0:T(8,128)S(1)} %collective-permute-done.10.theirs_ref), custom_call_target="tpu_custom_call" | custom-call | flops 1048576 | bytes 1048576 | tf_op jit(solution)/shard_map/pallas_call | solution.py:324
  (1 shorter events, 0.0 us)
Async XLA Ops:
  0.6 11.9 %copy-start.1 = (bf16[128,2560]{1,0:T(8,128)(2,1)S(1)}, bf16[128,2560]{1,0:T(8,128)(2,1)}, u32[]{:S(2)}) copy-start(bf16[128,2560]{1,0:T(8,128)(2,1)} %grad_ref.3) | copy-start | bytes 1966084
  1.6 6.9 %collective-permute-start = (bf16[128,512]{1,0:T(8,128)(2,1)S(1)}, bf16[128,512]{1,0:T(8,128)(2,1)S(1)}, u32[]{:S(2)}, u32[]{:S(2)}) collective-permute-start(bf16[128,512]{1,0:T(8,128)(2,1)S(1)} %shard_map.68.refs_0_), channel_id=1, source_target_pairs={{0,8},{4,12},{8,0},{12,4},{16,24},{20,28},{24,16},{28,20},{1,9},{5... | collective-permute-start | bytes 393224 | tf_op jit(solution)/shard_map/ppermute | solution.py:265
  4.6 7.8 %collective-permute-start.1 = (bf16[128,512]{1,0:T(8,128)(2,1)S(1)}, bf16[128,512]{1,0:T(8,128)(2,1)S(1)}, u32[]{:S(2)}, u32[]{:S(2)}) collective-permute-start(bf16[128,512]{1,0:T(8,128)(2,1)S(1)} %shard_map.68.refs_0_), channel_id=1, source_target_pairs={{0,16},{4,20},{8,24},{12,28},{16,0},{20,4},{24,8},{28,12},{1,17},{... | collective-permute-start | bytes 393224 | tf_op jit(solution)/shard_map/ppermute | solution.py:265
  6.2 6.3 %collective-permute-start.2 = (bf16[128,512]{1,0:T(8,128)(2,1)S(1)}, bf16[128,512]{1,0:T(8,128)(2,1)S(1)}, u32[]{:S(2)}, u32[]{:S(2)}) collective-permute-start(bf16[128,512]{1,0:T(8,128)(2,1)S(1)} %shard_map.68.refs_0_), channel_id=1, source_target_pairs={{0,24},{4,28},{8,16},{12,20},{16,8},{20,12},{24,0},{28,4},{1,25},{... | collective-permute-start | bytes 393224 | tf_op jit(solution)/shard_map/ppermute | solution.py:265
  12.4 3.7 %copy-start.2 = (s32[1024]{0:T(1024)S(1)}, s32[1024]{0:T(1024)}, u32[]{:S(2)}) copy-start(s32[1024]{0:T(1024)} %param.9) | copy-start | bytes 12292
  12.5 3.7 %collective-permute-start.3 = (bf16[512,256]{1,0:T(8,128)(2,1)S(1)}, bf16[512,256]{1,0:T(8,128)(2,1)S(1)}, u32[]{:S(2)}, u32[]{:S(2)}) collective-permute-start(bf16[512,256]{1,0:T(8,128)(2,1)S(1)} %shard_map.69.near_ref), channel_id=1, source_target_pairs={{0,4},{4,0},{8,12},{12,8},{16,20},{20,16},{24,28},{28,24},{1,5},{5... | collective-permute-start | bytes 786440 | tf_op jit(solution)/shard_map/ppermute | solution.py:265
  12.6 7.1 %collective-permute-start.7 = (bf16[128,640]{1,0:T(8,128)(2,1)S(1)}, bf16[128,640]{1,0:T(8,128)(2,1)S(1)}, u32[]{:S(2)}, u32[]{:S(2)}) collective-permute-start(bf16[128,640]{1,0:T(8,128)(2,1)S(1)} %get-tuple-element.23), channel_id=1, source_target_pairs={{0,8},{4,12},{8,0},{12,4},{16,24},{20,28},{24,16},{28,20},{1,9},{5... | collective-permute-start | bytes 491528 | tf_op jit(solution)/shard_map/ppermute | solution.py:265
  13.9 8.2 %collective-permute-start.8 = (bf16[128,640]{1,0:T(8,128)(2,1)S(1)}, bf16[128,640]{1,0:T(8,128)(2,1)S(1)}, u32[]{:S(2)}, u32[]{:S(2)}) collective-permute-start(bf16[128,640]{1,0:T(8,128)(2,1)S(1)} %get-tuple-element.24), channel_id=1, source_target_pairs={{0,16},{4,20},{8,24},{12,28},{16,0},{20,4},{24,8},{28,12},{1,17},{... | collective-permute-start | bytes 491528 | tf_op jit(solution)/shard_map/ppermute | solution.py:265
  14.7 9.0 %collective-permute-start.9 = (bf16[128,640]{1,0:T(8,128)(2,1)S(1)}, bf16[128,640]{1,0:T(8,128)(2,1)S(1)}, u32[]{:S(2)}, u32[]{:S(2)}) collective-permute-start(bf16[128,640]{1,0:T(8,128)(2,1)S(1)} %get-tuple-element.25), channel_id=1, source_target_pairs={{0,24},{4,28},{8,16},{12,20},{16,8},{20,12},{24,0},{28,4},{1,25},{... | collective-permute-start | bytes 491528 | tf_op jit(solution)/shard_map/ppermute | solution.py:265
  16.2 8.0 %copy-start = (bf16[640,8,128]{2,1,0:T(8,128)(2,1)S(1)}, bf16[640,8,128]{2,1,0:T(8,128)(2,1)}, u32[]{:S(2)}) copy-start(bf16[640,8,128]{2,1,0:T(8,128)(2,1)} %weight_ref.1) | copy-start | bytes 3932164
  24.1 12.8 %collective-permute-start.10 = (f32[320,256]{1,0:T(8,128)S(1)}, f32[320,256]{1,0:T(8,128)S(1)}, u32[]{:S(2)}, u32[]{:S(2)}) collective-permute-start(f32[320,256]{1,0:T(8,128)S(1)} %get-tuple-element.27), channel_id=1, source_target_pairs={{0,4},{4,0},{8,12},{12,8},{16,20},{20,16},{24,28},{28,24},{1,5},{5... | collective-permute-start | bytes 983048 | tf_op jit(solution)/shard_map/ppermute | solution.py:265
  25.3 4.5 %collective-permute-start.4 = (bf16[128,256]{1,0:T(8,128)(2,1)S(1)}, bf16[128,256]{1,0:T(8,128)(2,1)S(1)}, u32[]{:S(2)}, u32[]{:S(2)}) collective-permute-start(bf16[128,256]{1,0:T(8,128)(2,1)S(1)} %get-tuple-element.18), channel_id=1, source_target_pairs={{0,1},{1,0},{2,3},{3,2},{4,5},{5,4},{6,7},{7,6},{8,9},{9,8},{10,11... | collective-permute-start | bytes 196616 | tf_op jit(solution)/shard_map/ppermute | solution.py:265
  26.9 7.0 %collective-permute-start.5 = (bf16[128,256]{1,0:T(8,128)(2,1)S(1)}, bf16[128,256]{1,0:T(8,128)(2,1)S(1)}, u32[]{:S(2)}, u32[]{:S(2)}) collective-permute-start(bf16[128,256]{1,0:T(8,128)(2,1)S(1)} %get-tuple-element.19), channel_id=1, source_target_pairs={{0,2},{1,3},{2,0},{3,1},{4,6},{5,7},{6,4},{7,5},{8,10},{9,11},{10,... | collective-permute-start | bytes 196616 | tf_op jit(solution)/shard_map/ppermute | solution.py:265
  29.5 6.1 %collective-permute-start.6 = (bf16[128,256]{1,0:T(8,128)(2,1)S(1)}, bf16[128,256]{1,0:T(8,128)(2,1)S(1)}, u32[]{:S(2)}, u32[]{:S(2)}) collective-permute-start(bf16[128,256]{1,0:T(8,128)(2,1)S(1)} %get-tuple-element.20), channel_id=1, source_target_pairs={{0,3},{1,2},{2,1},{3,0},{4,7},{5,6},{6,5},{7,4},{8,11},{9,10},{10,... | collective-permute-start | bytes 196616 | tf_op jit(solution)/shard_map/ppermute | solution.py:265

commit v3 on v2

--- a/solution.py
+++ b/solution.py
@@ -1,3 +1,4 @@
+import functools
 import math
 
 import jax
@@ -123,12 +124,13 @@
     return [(index, index ^ mask) for index in range(size)]
 
 
-def vmem_call(kernel, outs, flops, limit, *args):
+def vmem_call(kernel, outs, flops, limit, *args, scratch=()):
     return pl.pallas_call(
         kernel,
         out_shape=[pltpu.VMEM(shape, dtype) for shape, dtype in outs],
         in_specs=[pl.BlockSpec(memory_space=pltpu.VMEM)] * len(args),
         out_specs=[pl.BlockSpec(memory_space=pltpu.VMEM)] * len(outs),
+        scratch_shapes=[pltpu.VMEM(shape, dtype) for shape, dtype in scratch],
         cost_estimate=pl.CostEstimate(flops=flops, bytes_accessed=1 << 16, transcendentals=0),
         compiler_params=pltpu.CompilerParams(vmem_limit_bytes=limit << 20),
     )(*args)
@@ -159,17 +161,33 @@
         out_ref[...] = grad_ref[:, pl.ds(start, span)]
 
 
-def parts_kernel(grad_ref, weight_ref, own_ref, *rest):
-    out_refs, flat = rest[:-1], rest[-1]
+def split_masks(masks, bit):
+    kept = [mask for mask in masks if not mask & bit]
+    return kept, [mask | bit for mask in kept]
+
+
+def parts_kernel(grad_ref, weight_ref, kept_ref, sent_ref, flat):
     rows, heads, _ = weight_ref.shape
     head = lax.axis_index("head")
     flat[...] = weight_ref[...].reshape(rows * heads, HD).astype(f32)
     cols = grad_ref[:, pl.ds(pl.multiple_of(head * rows, 128), rows)]
-    per = own_ref.shape[1] // HD
-    for mask, out_ref in enumerate((own_ref, *out_refs)):
-        for h in range(per):
-            weight = flat[pl.ds((head ^ mask) * per + h, rows, stride=heads), :].astype(bf16)
-            out_ref[:, h * HD : (h + 1) * HD] = dot(cols, weight).astype(out_ref.dtype)
+    size = lax.axis_size("head")
+    per = heads // size
+    for out_ref, masks in zip((kept_ref, sent_ref), split_masks(range(size), 1)):
+        for place, mask in enumerate(masks):
+            for h in range(per):
+                weight = flat[pl.ds((head ^ mask) * per + h, rows, stride=heads), :].astype(bf16)
+                start = (place * per + h) * HD
+                out_ref[:, start : start + HD] = dot(cols, weight).astype(out_ref.dtype)
+
+
+def blend_kernel(width, bit, kept_ref, got_ref, next_ref, sent_ref):
+    masks = [mask for mask in range(lax.axis_size("head")) if not mask & (bit - 1)]
+    for out_ref, chosen in zip((next_ref, sent_ref), split_masks(masks, bit)):
+        for place, mask in enumerate(chosen):
+            cols = slice(masks.index(mask) * width, (masks.index(mask) + 1) * width)
+            total = kept_ref[:, cols] + got_ref[:, cols].astype(f32)
+            out_ref[:, place * width : (place + 1) * width] = total.astype(out_ref.dtype)
 
 
 def join_kernel(*refs):
@@ -180,9 +198,10 @@
 
 
 def attention_kernel(pos_ref, near_ref, far_ref, *refs):
-    token_refs, (attn_ref, full_ref, prob_ref) = refs[:-3], refs[-3:]
+    token_refs, (attn_ref, full_ref, prob_ref, score_ref, weight_ref) = refs[:-5], refs[-5:]
     rows = token_refs[0].shape[0]
     blocks = len(token_refs)
+    half = blocks * rows
     seq = lax.axis_index("seq")
     pair, low = seq // 2, seq % 2
     places = [
@@ -193,31 +212,35 @@
     key_pos = jnp.concatenate(places, axis=1)
     row_id = lax.broadcasted_iota(jnp.int32, (rows, rows), 0)
     col_id = lax.broadcasted_iota(jnp.int32, (rows, rows), 1)
-    keys = jnp.concatenate([near_ref[:, :HD], far_ref[:, :HD]], axis=0)
-    values = jnp.concatenate([near_ref[:, HD:], far_ref[:, HD:]], axis=0)
-    scale = HD ** (-0.5)
-    for block, ref in enumerate(token_refs):
-        query_pos = jnp.sum(jnp.where(row_id == col_id, places[block], 0), axis=1, keepdims=True)
-        visible = key_pos <= query_pos
-        for h in range(full_ref.shape[1] // HD):
-            scores = dot(ref[:, (2 + h) * HD : (3 + h) * HD], keys, ROWS) * scale
-            scores = jnp.where(visible, scores, big_negative)
+    heads = range(score_ref.shape[0])
+    for h in heads:
+        query = jnp.concatenate([ref[:, (2 + h) * HD : (3 + h) * HD] for ref in token_refs], axis=0)
+        score_ref[h, :, :half] = dot(query, near_ref[:, :HD], ROWS)
+        score_ref[h, :, half:] = dot(query, far_ref[:, :HD], ROWS)
+    for h in heads:
+        cols = slice(h * HD, (h + 1) * HD)
+        shares = []
+        for block in range(blocks):
+            span = slice(block * rows, (block + 1) * rows)
+            query_pos = jnp.sum(
+                jnp.where(row_id == col_id, places[block], 0), axis=1, keepdims=True
+            )
+            scores = jnp.where(key_pos <= query_pos, score_ref[h, span, :], big_negative)
             top = jnp.max(scores, axis=1, keepdims=True)
-            weights = jnp.exp(scores - top)
-            share = 1.0 / jnp.sum(weights, axis=1, keepdims=True)
-            full = dot(weights.astype(bf16), values) * share
-            attn_ref[block * rows : (block + 1) * rows, h * HD : (h + 1) * HD] = full.astype(bf16)
+            weights = jnp.exp2((scores - top) * (HD ** (-0.5) * math.log2(math.e)))
+            shares.append(1.0 / jnp.sum(weights, axis=1, keepdims=True))
+            weight_ref[h, span, :] = weights.astype(bf16)
             if block == 0:
-                full_ref[:, h * HD : (h + 1) * HD] = full
-                prob_ref[h] = weights * share
-
-
-def query_kernel(near_ref, far_ref, full_ref, prob_ref, own_ref, *refs):
-    part_refs, out_ref = refs[:-1], refs[-1]
-    total = own_ref[...]
-    for ref in part_refs:
-        total = total + ref[...].astype(f32)
-    d_attn = total.astype(bf16)
+                prob_ref[h] = weights * shares[0]
+        full = dot(weight_ref[h, :, :half], near_ref[:, HD:])
+        full = full + dot(weight_ref[h, :, half:], far_ref[:, HD:])
+        full = full * jnp.concatenate(shares, axis=0)
+        attn_ref[:, cols] = full.astype(bf16)
+        full_ref[:, cols] = full[:rows]
+
+
+def query_kernel(near_ref, far_ref, full_ref, prob_ref, kept_ref, got_ref, out_ref):
+    d_attn = (kept_ref[...] + got_ref[...].astype(f32)).astype(bf16)
     half = near_ref.shape[0]
     for h in range(prob_ref.shape[0]):
         cols = slice(h * HD, (h + 1) * HD)
@@ -283,17 +306,30 @@
     )
     grads = [grads[0]] + [move(grads[m], "seq", seq_size, 2 * m) for m in masks]
 
-    kinds = [f32] + [bf16] * (head_size - 1)
-    parts = pl.pallas_call(
+    half = (token_count, head_size // 2 * width)
+    kept, sent = vmem_call(
         parts_kernel,
-        out_shape=[pltpu.VMEM((token_count, width), kind) for kind in kinds],
-        in_specs=[pl.BlockSpec(memory_space=pltpu.VMEM)] * 2,
-        out_specs=[pl.BlockSpec(memory_space=pltpu.VMEM)] * head_size,
-        scratch_shapes=[pltpu.VMEM((rows_in * out_weight.shape[1], HD), f32)],
-        cost_estimate=pl.CostEstimate(flops=1 << 28, bytes_accessed=1 << 20, transcendentals=0),
-        compiler_params=pltpu.CompilerParams(vmem_limit_bytes=16 << 20),
-    )(out_grad, out_weight)
-    parts = [parts[0]] + [move(parts[m], "head", head_size, m) for m in range(1, head_size)]
+        [(half, f32), (half, bf16)],
+        1 << 28,
+        16,
+        out_grad,
+        out_weight,
+        scratch=[((rows_in * out_weight.shape[1], HD), f32)],
+    )
+    got = move(sent, "head", head_size, 1)
+    bit = 2
+    while bit < head_size:
+        half = (token_count, kept.shape[1] // 2)
+        kept, sent = vmem_call(
+            functools.partial(blend_kernel, width, bit),
+            [(half, f32), (half, bf16)],
+            1 << 20,
+            2,
+            kept,
+            got,
+        )
+        got = move(sent, "head", head_size, bit)
+        bit *= 2
 
     (near,) = vmem_call(join_kernel, [((tokens_near, 2 * HD), bf16)], 1 << 20, 2, *tokens)
     far = move(near, "seq", seq_size, 1)
@@ -310,6 +346,9 @@
         near,
         far,
         *tokens,
+        scratch=[
+            ((head_count, tokens_near, 2 * tokens_near), kind) for kind in (f32, bf16)
+        ],
     )
     mine, theirs = vmem_call(
         sums_kernel, [((span // 2, width), f32)] * 2, 1 << 28, 12, attn, *grads
@@ -320,7 +359,7 @@
         out_shape=jax.ShapeDtypeStruct((token_count, width), bf16),
         cost_estimate=pl.CostEstimate(flops=1 << 28, bytes_accessed=1 << 20, transcendentals=0),
         compiler_params=pltpu.CompilerParams(vmem_limit_bytes=8 << 20),
-    )(near, far, full, prob, *parts)
+    )(near, far, full, prob, kept, got)
     d_out_weight = pl.pallas_call(
         add_kernel,
         out_shape=jax.ShapeDtypeStruct((span // 2, head_count, HD), f32),

time: 38 us -> 39.3 us (1.034)
  waiting for transfers between devices: 16.6 us -> 19.1 us
  Pallas kernels: 7.8 us -> 6.67 us
    ppermute x11 -> x10, waiting for transfers between devices: 16.6 us -> 19.1 us  [move(): return lax.ppermute(array, axis, xor_pairs(size, mask))]
    pallas_call x1 -> x0, Pallas kernels: 1.1 us -> none  [narrow_body(): pl.pallas_call(parts_kernel, out_shape=[pltpu.VMEM((token_count, width),...]
    ppermute x11 -> x10, starting transfers between devices: 12.7 us -> 12.6 us  [move(): return lax.ppermute(array, axis, xor_pairs(size, mask))]
    pallas_call x4 -> x6, Pallas kernels: 3.52 us -> 3.5 us  [vmem_call(): pl.pallas_call(kernel, out_shape=[pltpu.VMEM(shape, dtype) for shape, dty...]
  transfers between devices with their start and end apart: 11 -> 10, of which waited for: 8 -> 7; matrix products, arithmetic and copies ran while one was open for 0% -> 0% of each run, Pallas kernels for 15% -> 11%
where the time goes in v3:
time: 39.3 us; the launch traced here: 39.1 us
  waiting for transfers between devices  19.1 us (49%)
  starting transfers between devices  12.6 us (32%)
  Pallas kernels  6.67 us (17%)
  between operations  0.73 us (2%)
    ppermute x10, waiting for transfers between devices, move(): return lax.ppermute(array, axis, xor_pairs(size, mask))  19.1 us
    ppermute x10, starting transfers between devices, move(): return lax.ppermute(array, axis, xor_pairs(size, mask))  12.6 us
    pallas_call x6, Pallas kernels, vmem_call(): pl.pallas_call(kernel, out_shape=[pltpu.VMEM(shape, dtype) for shape, dty...  3.5 us
    pallas_call x1, Pallas kernels, narrow_body(): pl.pallas_call(query_kernel, out_shape=jax.ShapeDtypeStruct((token_count,...  1.29 us
    pallas_call x1, Pallas kernels, narrow_body(): pl.pallas_call(pack_kernel, out_shape=pltpu.VMEM((token_count, 2 * HD + w...  0.96 us
    pallas_call x1, Pallas kernels, narrow_body(): pl.pallas_call(add_kernel, out_shape=jax.ShapeDtypeStruct((span // 2, hea...  0.92 us
  transfers between devices with their start and end apart: 10, of which 7 were waited for; matrix products, arithmetic and copies ran while one was open for 0% of the time, Pallas kernels for 11%

profile of v3, /device:TPU:0, one launch (start us, length us, event | category | flops | bytes accessed | tf_op | source)
XLA Modules:
  0.0 39.1 jit_solution(6744314809339264883)
XLA Ops:
  0.6 0.0 copy-start.1
  0.6 1.0 %shard_map.68.refs_0_ = bf16[128,512]{1,0:T(8,128)(2,1)S(1)} custom-call(bf16[2,128,128]{2,1,0:T(8,128)(2,1)} %kv_ref.1, bf16[128,256]{1,0:T(8,128)(2,1)} %query_ref.1), custom_call_target="tpu_custom_call" | custom-call | flops 4294967296 | bytes 262144 | tf_op jit(solution)/shard_map/pallas_call | solution.py:291
  1.6 3.0 %collective-permute-start = (bf16[128,512]{1,0:T(8,128)(2,1)S(1)}, bf16[128,512]{1,0:T(8,128)(2,1)S(1)}, u32[]{:S(2)}, u32[]{:S(2)}) collective-permute-start(bf16[128,512]{1,0:T(8,128)(2,1)S(1)} %shard_map.68.refs_0_), channel_id=1, source_target_pairs={{0,8},{4,12},{8,0},{12,4},{16,24},{20,28},{24,16},{28,20},{1,9},{5... | collective-permute-start | bytes 393224 | tf_op jit(solution)/shard_map/ppermute | solution.py:288
  4.6 1.5 %collective-permute-start.1 = (bf16[128,512]{1,0:T(8,128)(2,1)S(1)}, bf16[128,512]{1,0:T(8,128)(2,1)S(1)}, u32[]{:S(2)}, u32[]{:S(2)}) collective-permute-start(bf16[128,512]{1,0:T(8,128)(2,1)S(1)} %shard_map.68.refs_0_), channel_id=1, source_target_pairs={{0,16},{4,20},{8,24},{12,28},{16,0},{20,4},{24,8},{28,12},{1,17},{... | collective-permute-start | bytes 393224 | tf_op jit(solution)/shard_map/ppermute | solution.py:288
  6.2 0.0 collective-permute-start.2
  6.2 2.3 %collective-permute-done.refs_1_ = bf16[128,512]{1,0:T(8,128)(2,1)S(1)} collective-permute-done((bf16[128,512]{1,0:T(8,128)(2,1)S(1)}, bf16[128,512]{1,0:T(8,128)(2,1)S(1)}, u32[]{:S(2)}, u32[]{:S(2)}) %collective-permute-start) | collective-permute-done | bytes 131104 | tf_op jit(solution)/shard_map/ppermute | solution.py:288
  8.5 3.9 %collective-permute-done.1.refs_2_ = bf16[128,512]{1,0:T(8,128)(2,1)S(1)} collective-permute-done((bf16[128,512]{1,0:T(8,128)(2,1)S(1)}, bf16[128,512]{1,0:T(8,128)(2,1)S(1)}, u32[]{:S(2)}, u32[]{:S(2)}) %collective-permute-start.1) | collective-permute-done | bytes 131104 | tf_op jit(solution)/shard_map/ppermute | solution.py:288
  12.4 0.0 collective-permute-done.2.refs_3_
  12.4 0.0 copy-start.2
  12.5 0.1 collective-permute-start.3
  12.5 0.0 copy-done.1
  12.5 0.1 shard_map.74
  12.6 1.3 %collective-permute-start.6 = (bf16[128,640]{1,0:T(8,128)(2,1)S(1)}, bf16[128,640]{1,0:T(8,128)(2,1)S(1)}, u32[]{:S(2)}, u32[]{:S(2)}) collective-permute-start(bf16[128,640]{1,0:T(8,128)(2,1)S(1)} %get-tuple-element.23), channel_id=1, source_target_pairs={{0,8},{4,12},{8,0},{12,4},{16,24},{20,28},{24,16},{28,20},{1,9},{5... | collective-permute-start | bytes 491528 | tf_op jit(solution)/shard_map/ppermute | solution.py:288
  13.9 0.8 %collective-permute-start.7 = (bf16[128,640]{1,0:T(8,128)(2,1)S(1)}, bf16[128,640]{1,0:T(8,128)(2,1)S(1)}, u32[]{:S(2)}, u32[]{:S(2)}) collective-permute-start(bf16[128,640]{1,0:T(8,128)(2,1)S(1)} %get-tuple-element.24), channel_id=1, source_target_pairs={{0,16},{4,20},{8,24},{12,28},{16,0},{20,4},{24,8},{28,12},{1,17},{... | collective-permute-start | bytes 491528 | tf_op jit(solution)/shard_map/ppermute | solution.py:288
  14.7 1.4 %collective-permute-start.8 = (bf16[128,640]{1,0:T(8,128)(2,1)S(1)}, bf16[128,640]{1,0:T(8,128)(2,1)S(1)}, u32[]{:S(2)}, u32[]{:S(2)}) collective-permute-start(bf16[128,640]{1,0:T(8,128)(2,1)S(1)} %get-tuple-element.25), channel_id=1, source_target_pairs={{0,24},{4,28},{8,16},{12,20},{16,8},{20,12},{24,0},{28,4},{1,25},{... | collective-permute-start | bytes 491528 | tf_op jit(solution)/shard_map/ppermute | solution.py:288
  16.2 0.0 collective-permute-done.3.far_ref
  16.2 0.0 copy-done.2
  16.2 0.0 copy-start
  16.2 1.9 %shard_map.70 = (bf16[512,256]{1,0:T(8,128)(2,1)S(1)}, f32[128,256]{1,0:T(8,128)S(1)}, f32[2,128,1024]{2,1,0:T(8,128)S(1)}) custom-call(s32[8,128]{1,0:T(8,128)S(1)} %bitcast.1, bf16[512,256]{1,0:T(8,128)(2,1)S(1)} %shard_map.69.near_ref, bf16[512,256]{1,0:T(8,128)(2,1)S(1)} %collective-permute-done.3.far_ref, bf16[128,512]{1,0:T(8,128)(2,1)S(1)} %shard_map.68.refs_0_, ...), custom_call_target="tpu_custom_call" | custom-call | flops 536870912 | bytes 65536 | tf_op jit(solution)/shard_map/pallas_call | solution.py:128
  18.1 1.7 %collective-permute-done.6.refs_1_ = bf16[128,640]{1,0:T(8,128)(2,1)S(1)} collective-permute-done((bf16[128,640]{1,0:T(8,128)(2,1)S(1)}, bf16[128,640]{1,0:T(8,128)(2,1)S(1)}, u32[]{:S(2)}, u32[]{:S(2)}) %collective-permute-start.6) | collective-permute-done | bytes 163872 | tf_op jit(solution)/shard_map/ppermute | solution.py:288
  19.8 2.3 %collective-permute-done.7.refs_2_ = bf16[128,640]{1,0:T(8,128)(2,1)S(1)} collective-permute-done((bf16[128,640]{1,0:T(8,128)(2,1)S(1)}, bf16[128,640]{1,0:T(8,128)(2,1)S(1)}, u32[]{:S(2)}, u32[]{:S(2)}) %collective-permute-start.7) | collective-permute-done | bytes 163872 | tf_op jit(solution)/shard_map/ppermute | solution.py:288
  22.1 1.6 %collective-permute-done.8.refs_3_ = bf16[128,640]{1,0:T(8,128)(2,1)S(1)} collective-permute-done((bf16[128,640]{1,0:T(8,128)(2,1)S(1)}, bf16[128,640]{1,0:T(8,128)(2,1)S(1)}, u32[]{:S(2)}, u32[]{:S(2)}) %collective-permute-start.8) | collective-permute-done | bytes 163872 | tf_op jit(solution)/shard_map/ppermute | solution.py:288
  23.7 0.4 shard_map.75
  24.1 0.1 collective-permute-start.9
  24.2 0.0 copy-done
  24.2 1.1 %shard_map.71 = (f32[128,512]{1,0:T(8,128)S(1)}, bf16[128,512]{1,0:T(8,128)(2,1)S(1)}) custom-call(bf16[128,2560]{1,0:T(8,128)(2,1)S(1)} %copy-done.1, bf16[640,8,128]{2,1,0:T(8,128)(2,1)S(1)} %copy-done), custom_call_target="tpu_custom_call" | custom-call | flops 268435456 | bytes 65536 | tf_op jit(solution)/shard_map/pallas_call | solution.py:128
  25.3 1.6 %collective-permute-start.4 = (bf16[128,512]{1,0:T(8,128)(2,1)S(1)}, bf16[128,512]{1,0:T(8,128)(2,1)S(1)}, u32[]{:S(2)}, u32[]{:S(2)}) collective-permute-start(bf16[128,512]{1,0:T(8,128)(2,1)S(1)} %get-tuple-element.18), channel_id=1, source_target_pairs={{0,1},{1,0},{2,3},{3,2},{4,5},{5,4},{6,7},{7,6},{8,9},{9,8},{10,11... | collective-permute-start | bytes 393224 | tf_op jit(solution)/shard_map/ppermute | solution.py:288
  26.9 4.3 %collective-permute-done.4.got_ref = bf16[128,512]{1,0:T(8,128)(2,1)S(1)} collective-permute-done((bf16[128,512]{1,0:T(8,128)(2,1)S(1)}, bf16[128,512]{1,0:T(8,128)(2,1)S(1)}, u32[]{:S(2)}, u32[]{:S(2)}) %collective-permute-start.4) | collective-permute-done | bytes 131104 | tf_op jit(solution)/shard_map/ppermute | solution.py:288
  31.3 2.7 %collective-permute-start.5 = (bf16[128,256]{1,0:T(8,128)(2,1)S(1)}, bf16[128,256]{1,0:T(8,128)(2,1)S(1)}, u32[]{:S(2)}, u32[]{:S(2)}) collective-permute-start(bf16[128,256]{1,0:T(8,128)(2,1)S(1)} %get-tuple-element.20), channel_id=1, source_target_pairs={{0,2},{1,3},{2,0},{3,1},{4,6},{5,7},{6,4},{7,5},{8,10},{9,11},{10,... | collective-permute-start | bytes 196616 | tf_op jit(solution)/shard_map/ppermute | solution.py:288
  33.9 3.0 %collective-permute-done.5.got_ref = bf16[128,256]{1,0:T(8,128)(2,1)S(1)} collective-permute-done((bf16[128,256]{1,0:T(8,128)(2,1)S(1)}, bf16[128,256]{1,0:T(8,128)(2,1)S(1)}, u32[]{:S(2)}, u32[]{:S(2)}) %collective-permute-start.5) | collective-permute-done | bytes 65568 | tf_op jit(solution)/shard_map/ppermute | solution.py:288
  36.9 1.3 %shard_map.73 = bf16[128,256]{1,0:T(8,128)(2,1)} custom-call(bf16[512,256]{1,0:T(8,128)(2,1)S(1)} %shard_map.69.near_ref, bf16[512,256]{1,0:T(8,128)(2,1)S(1)} %collective-permute-done.3.far_ref, f32[128,256]{1,0:T(8,128)S(1)} %get-tuple-element.15.full_ref, f32[2,128,1024]{2,1,0:T(8,128)S(1)} %get-tuple-element.16.prob_ref, ...), custom_call_target="tpu_custom_call" | custom-call | flops 268435456 | bytes 1048576 | tf_op jit(solution)/shard_map/pallas_call | solution.py:357
  38.2 0.0 collective-permute-done.9.theirs_ref
  38.2 0.9 %shard_map.76 = f32[320,2,128]{2,1,0:T(2,128)} custom-call(f32[320,256]{1,0:T(8,128)S(1)} %get-tuple-element.26.mine_ref, f32[320,256]{1,0:T(8,128)S(1)} %collective-permute-done.9.theirs_ref), custom_call_target="tpu_custom_call" | custom-call | flops 1048576 | bytes 1048576 | tf_op jit(solution)/shard_map/pallas_call | solution.py:363
  (2 shorter events, 0.0 us)
Async XLA Ops:
  0.6 11.9 %copy-start.1 = (bf16[128,2560]{1,0:T(8,128)(2,1)S(1)}, bf16[128,2560]{1,0:T(8,128)(2,1)}, u32[]{:S(2)}) copy-start(bf16[128,2560]{1,0:T(8,128)(2,1)} %grad_ref.3) | copy-start | bytes 1966084
  1.6 6.9 %collective-permute-start = (bf16[128,512]{1,0:T(8,128)(2,1)S(1)}, bf16[128,512]{1,0:T(8,128)(2,1)S(1)}, u32[]{:S(2)}, u32[]{:S(2)}) collective-permute-start(bf16[128,512]{1,0:T(8,128)(2,1)S(1)} %shard_map.68.refs_0_), channel_id=1, source_target_pairs={{0,8},{4,12},{8,0},{12,4},{16,24},{20,28},{24,16},{28,20},{1,9},{5... | collective-permute-start | bytes 393224 | tf_op jit(solution)/shard_map/ppermute | solution.py:288
  4.6 7.8 %collective-permute-start.1 = (bf16[128,512]{1,0:T(8,128)(2,1)S(1)}, bf16[128,512]{1,0:T(8,128)(2,1)S(1)}, u32[]{:S(2)}, u32[]{:S(2)}) collective-permute-start(bf16[128,512]{1,0:T(8,128)(2,1)S(1)} %shard_map.68.refs_0_), channel_id=1, source_target_pairs={{0,16},{4,20},{8,24},{12,28},{16,0},{20,4},{24,8},{28,12},{1,17},{... | collective-permute-start | bytes 393224 | tf_op jit(solution)/shard_map/ppermute | solution.py:288
  6.2 6.3 %collective-permute-start.2 = (bf16[128,512]{1,0:T(8,128)(2,1)S(1)}, bf16[128,512]{1,0:T(8,128)(2,1)S(1)}, u32[]{:S(2)}, u32[]{:S(2)}) collective-permute-start(bf16[128,512]{1,0:T(8,128)(2,1)S(1)} %shard_map.68.refs_0_), channel_id=1, source_target_pairs={{0,24},{4,28},{8,16},{12,20},{16,8},{20,12},{24,0},{28,4},{1,25},{... | collective-permute-start | bytes 393224 | tf_op jit(solution)/shard_map/ppermute | solution.py:288
  12.4 3.7 %copy-start.2 = (s32[1024]{0:T(1024)S(1)}, s32[1024]{0:T(1024)}, u32[]{:S(2)}) copy-start(s32[1024]{0:T(1024)} %param.9) | copy-start | bytes 12292
  12.5 3.7 %collective-permute-start.3 = (bf16[512,256]{1,0:T(8,128)(2,1)S(1)}, bf16[512,256]{1,0:T(8,128)(2,1)S(1)}, u32[]{:S(2)}, u32[]{:S(2)}) collective-permute-start(bf16[512,256]{1,0:T(8,128)(2,1)S(1)} %shard_map.69.near_ref), channel_id=1, source_target_pairs={{0,4},{4,0},{8,12},{12,8},{16,20},{20,16},{24,28},{28,24},{1,5},{5... | collective-permute-start | bytes 786440 | tf_op jit(solution)/shard_map/ppermute | solution.py:288
  12.6 7.1 %collective-permute-start.6 = (bf16[128,640]{1,0:T(8,128)(2,1)S(1)}, bf16[128,640]{1,0:T(8,128)(2,1)S(1)}, u32[]{:S(2)}, u32[]{:S(2)}) collective-permute-start(bf16[128,640]{1,0:T(8,128)(2,1)S(1)} %get-tuple-element.23), channel_id=1, source_target_pairs={{0,8},{4,12},{8,0},{12,4},{16,24},{20,28},{24,16},{28,20},{1,9},{5... | collective-permute-start | bytes 491528 | tf_op jit(solution)/shard_map/ppermute | solution.py:288
  13.9 8.2 %collective-permute-start.7 = (bf16[128,640]{1,0:T(8,128)(2,1)S(1)}, bf16[128,640]{1,0:T(8,128)(2,1)S(1)}, u32[]{:S(2)}, u32[]{:S(2)}) collective-permute-start(bf16[128,640]{1,0:T(8,128)(2,1)S(1)} %get-tuple-element.24), channel_id=1, source_target_pairs={{0,16},{4,20},{8,24},{12,28},{16,0},{20,4},{24,8},{28,12},{1,17},{... | collective-permute-start | bytes 491528 | tf_op jit(solution)/shard_map/ppermute | solution.py:288
  14.7 9.0 %collective-permute-start.8 = (bf16[128,640]{1,0:T(8,128)(2,1)S(1)}, bf16[128,640]{1,0:T(8,128)(2,1)S(1)}, u32[]{:S(2)}, u32[]{:S(2)}) collective-permute-start(bf16[128,640]{1,0:T(8,128)(2,1)S(1)} %get-tuple-element.25), channel_id=1, source_target_pairs={{0,24},{4,28},{8,16},{12,20},{16,8},{20,12},{24,0},{28,4},{1,25},{... | collective-permute-start | bytes 491528 | tf_op jit(solution)/shard_map/ppermute | solution.py:288
  16.2 8.0 %copy-start = (bf16[640,8,128]{2,1,0:T(8,128)(2,1)S(1)}, bf16[640,8,128]{2,1,0:T(8,128)(2,1)}, u32[]{:S(2)}) copy-start(bf16[640,8,128]{2,1,0:T(8,128)(2,1)} %weight_ref.1) | copy-start | bytes 3932164
  24.1 14.1 %collective-permute-start.9 = (f32[320,256]{1,0:T(8,128)S(1)}, f32[320,256]{1,0:T(8,128)S(1)}, u32[]{:S(2)}, u32[]{:S(2)}) collective-permute-start(f32[320,256]{1,0:T(8,128)S(1)} %get-tuple-element.27), channel_id=1, source_target_pairs={{0,4},{4,0},{8,12},{12,8},{16,20},{20,16},{24,28},{28,24},{1,5},{5... | collective-permute-start | bytes 983048 | tf_op jit(solution)/shard_map/ppermute | solution.py:288
  25.3 6.0 %collective-permute-start.4 = (bf16[128,512]{1,0:T(8,128)(2,1)S(1)}, bf16[128,512]{1,0:T(8,128)(2,1)S(1)}, u32[]{:S(2)}, u32[]{:S(2)}) collective-permute-start(bf16[128,512]{1,0:T(8,128)(2,1)S(1)} %get-tuple-element.18), channel_id=1, source_target_pairs={{0,1},{1,0},{2,3},{3,2},{4,5},{5,4},{6,7},{7,6},{8,9},{9,8},{10,11... | collective-permute-start | bytes 393224 | tf_op jit(solution)/shard_map/ppermute | solution.py:288
  31.3 5.6 %collective-permute-start.5 = (bf16[128,256]{1,0:T(8,128)(2,1)S(1)}, bf16[128,256]{1,0:T(8,128)(2,1)S(1)}, u32[]{:S(2)}, u32[]{:S(2)}) collective-permute-start(bf16[128,256]{1,0:T(8,128)(2,1)S(1)} %get-tuple-element.20), channel_id=1, source_target_pairs={{0,2},{1,3},{2,0},{3,1},{4,6},{5,7},{6,4},{7,5},{8,10},{9,11},{10,... | collective-permute-start | bytes 196616 | tf_op jit(solution)/shard_map/ppermute | solution.py:288

commit v4 on v3

--- a/solution.py
+++ b/solution.py
@@ -260,14 +260,15 @@
     grads = jnp.concatenate([ref[...] for ref in grad_refs], axis=0)
     sums = dot(grads, attn_ref[...], COLS)
     half = sums.shape[0] // 2
-    mine_ref[pl.ds(0, half), :] = jnp.where(low == 0, sums[:half], sums[half:])
-    theirs_ref[pl.ds(0, half), :] = jnp.where(low == 0, sums[half:], sums[:half])
+    mine_ref[...] = jnp.where(low == 0, sums[:half], sums[half:])
+    theirs = jnp.where(low == 0, sums[half:], sums[:half])
+    theirs_ref[...] = theirs.astype(theirs_ref.dtype)
 
 
 def add_kernel(mine_ref, theirs_ref, out_ref):
     for h in range(out_ref.shape[1]):
         cols = slice(h * HD, (h + 1) * HD)
-        out_ref[:, h, :] = mine_ref[:, cols] + theirs_ref[:, cols]
+        out_ref[:, h, :] = mine_ref[:, cols] + theirs_ref[:, cols].astype(f32)
 
 
 def narrow_body(queries, keys_values, out_weight, out_grad, positions, seq_size, head_size):
@@ -351,15 +352,26 @@
         ],
     )
     mine, theirs = vmem_call(
-        sums_kernel, [((span // 2, width), f32)] * 2, 1 << 28, 12, attn, *grads
+        sums_kernel,
+        [((span // 2, width), kind) for kind in (f32, bf16)],
+        1 << 28,
+        12,
+        attn,
+        *grads,
     )
     theirs = move(theirs, "seq", seq_size, 1)
-    d_query = pl.pallas_call(
+    (d_query,) = vmem_call(
         query_kernel,
-        out_shape=jax.ShapeDtypeStruct((token_count, width), bf16),
-        cost_estimate=pl.CostEstimate(flops=1 << 28, bytes_accessed=1 << 20, transcendentals=0),
-        compiler_params=pltpu.CompilerParams(vmem_limit_bytes=8 << 20),
-    )(near, far, full, prob, kept, got)
+        [((token_count, width), bf16)],
+        1 << 28,
+        8,
+        near,
+        far,
+        full,
+        prob,
+        kept,
+        got,
+    )
     d_out_weight = pl.pallas_call(
         add_kernel,
         out_shape=jax.ShapeDtypeStruct((span // 2, head_count, HD), f32),
@@ -371,7 +383,7 @@
 
 def solution(mesh):
     seq_size, head_size = mesh.shape["seq"], mesh.shape["head"]
-    narrow = seq_size in (4, 8) and head_size in (2, 4, 8)
+    narrow = seq_size == 8 and head_size in (2, 4, 8)
 
     def body(*arrays):
         if not narrow:

time: 39.3 us -> 33.5 us (0.85)
  waiting for transfers between devices: 19.1 us -> 13.3 us
  local copies, waits for them, and re-layouts: 0.01 us -> 0.65 us
  Pallas kernels: 6.67 us -> 6.04 us
    ppermute x10, waiting for transfers between devices: 19.1 us -> 13.3 us  [move(): return lax.ppermute(array, axis, xor_pairs(size, mask))]
    pallas_call x1 -> x0, Pallas kernels: 1.29 us -> none  [narrow_body(): pl.pallas_call(query_kernel, out_shape=jax.ShapeDtypeStruct((token_count,...]
    pallas_call x6 -> x7, Pallas kernels: 3.5 us -> 4.16 us  [vmem_call(): pl.pallas_call(kernel, out_shape=[pltpu.VMEM(shape, dtype) for shape, dty...]
    unnamed x6 -> x7, local copies, waits for them, and re-layouts: 0.01 us -> 0.65 us
  transfers between devices with their start and end apart: 10 -> 10, of which waited for: 7 -> 5; matrix products, arithmetic and copies ran while one was open for 0% -> 2% of each run, Pallas kernels for 11% -> 12%
where the time goes in v4:
time: 33.5 us; the launch traced here: 33.3 us
  waiting for transfers between devices  13.3 us (40%)
  starting transfers between devices  12.6 us (38%)
  Pallas kernels  6.04 us (18%)
  between operations  0.74 us (2%)
  local copies, waits for them, and re-layouts  0.65 us (2%)
    ppermute x10, waiting for transfers between devices, move(): return lax.ppermute(array, axis, xor_pairs(size, mask))  13.3 us
    ppermute x10, starting transfers between devices, move(): return lax.ppermute(array, axis, xor_pairs(size, mask))  12.6 us
    pallas_call x7, Pallas kernels, vmem_call(): pl.pallas_call(kernel, out_shape=[pltpu.VMEM(shape, dtype) for shape, dty...  4.16 us
    pallas_call x1, Pallas kernels, narrow_body(): pl.pallas_call(pack_kernel, out_shape=pltpu.VMEM((token_count, 2 * HD + w...  0.96 us
    pallas_call x1, Pallas kernels, narrow_body(): pl.pallas_call(add_kernel, out_shape=jax.ShapeDtypeStruct((span // 2, hea...  0.92 us
  transfers between devices with their start and end apart: 10, of which 5 were waited for; matrix products, arithmetic and copies ran while one was open for 2% of the time, Pallas kernels for 12%

profile of v4, /device:TPU:0, one launch (start us, length us, event | category | flops | bytes accessed | tf_op | source)
XLA Modules:
  0.0 33.3 jit_solution(8476323005589198779)
XLA Ops:
  0.6 0.0 copy-start.1
  0.6 1.0 %shard_map.68.refs_0_ = bf16[128,512]{1,0:T(8,128)(2,1)S(1)} custom-call(bf16[2,128,128]{2,1,0:T(8,128)(2,1)} %kv_ref.1, bf16[128,256]{1,0:T(8,128)(2,1)} %query_ref.1), custom_call_target="tpu_custom_call" | custom-call | flops 4294967296 | bytes 262144 | tf_op jit(solution)/shard_map/pallas_call | solution.py:292
  1.6 3.0 %collective-permute-start = (bf16[128,512]{1,0:T(8,128)(2,1)S(1)}, bf16[128,512]{1,0:T(8,128)(2,1)S(1)}, u32[]{:S(2)}, u32[]{:S(2)}) collective-permute-start(bf16[128,512]{1,0:T(8,128)(2,1)S(1)} %shard_map.68.refs_0_), channel_id=1, source_target_pairs={{0,8},{4,12},{8,0},{12,4},{16,24},{20,28},{24,16},{28,20},{1,9},{5... | collective-permute-start | bytes 393224 | tf_op jit(solution)/shard_map/ppermute | solution.py:289
  4.6 1.5 %collective-permute-start.1 = (bf16[128,512]{1,0:T(8,128)(2,1)S(1)}, bf16[128,512]{1,0:T(8,128)(2,1)S(1)}, u32[]{:S(2)}, u32[]{:S(2)}) collective-permute-start(bf16[128,512]{1,0:T(8,128)(2,1)S(1)} %shard_map.68.refs_0_), channel_id=1, source_target_pairs={{0,16},{4,20},{8,24},{12,28},{16,0},{20,4},{24,8},{28,12},{1,17},{... | collective-permute-start | bytes 393224 | tf_op jit(solution)/shard_map/ppermute | solution.py:289
  6.2 0.0 collective-permute-start.2
  6.2 2.3 %collective-permute-done.refs_1_ = bf16[128,512]{1,0:T(8,128)(2,1)S(1)} collective-permute-done((bf16[128,512]{1,0:T(8,128)(2,1)S(1)}, bf16[128,512]{1,0:T(8,128)(2,1)S(1)}, u32[]{:S(2)}, u32[]{:S(2)}) %collective-permute-start) | collective-permute-done | bytes 131104 | tf_op jit(solution)/shard_map/ppermute | solution.py:289
  8.5 3.9 %collective-permute-done.1.refs_2_ = bf16[128,512]{1,0:T(8,128)(2,1)S(1)} collective-permute-done((bf16[128,512]{1,0:T(8,128)(2,1)S(1)}, bf16[128,512]{1,0:T(8,128)(2,1)S(1)}, u32[]{:S(2)}, u32[]{:S(2)}) %collective-permute-start.1) | collective-permute-done | bytes 131104 | tf_op jit(solution)/shard_map/ppermute | solution.py:289
  12.4 0.0 collective-permute-done.2.refs_3_
  12.4 0.0 copy-start
  12.5 0.1 collective-permute-start.3
  12.5 0.0 copy-done.1
  12.5 0.1 shard_map.74
  12.6 0.0 copy-start.2
  12.6 1.3 %collective-permute-start.6 = (bf16[128,640]{1,0:T(8,128)(2,1)S(1)}, bf16[128,640]{1,0:T(8,128)(2,1)S(1)}, u32[]{:S(2)}, u32[]{:S(2)}) collective-permute-start(bf16[128,640]{1,0:T(8,128)(2,1)S(1)} %get-tuple-element.23), channel_id=1, source_target_pairs={{0,8},{4,12},{8,0},{12,4},{16,24},{20,28},{24,16},{28,20},{1,9},{5... | collective-permute-start | bytes 491528 | tf_op jit(solution)/shard_map/ppermute | solution.py:289
  13.9 0.8 %collective-permute-start.7 = (bf16[128,640]{1,0:T(8,128)(2,1)S(1)}, bf16[128,640]{1,0:T(8,128)(2,1)S(1)}, u32[]{:S(2)}, u32[]{:S(2)}) collective-permute-start(bf16[128,640]{1,0:T(8,128)(2,1)S(1)} %get-tuple-element.24), channel_id=1, source_target_pairs={{0,16},{4,20},{8,24},{12,28},{16,0},{20,4},{24,8},{28,12},{1,17},{... | collective-permute-start | bytes 491528 | tf_op jit(solution)/shard_map/ppermute | solution.py:289
  14.7 1.4 %collective-permute-start.8 = (bf16[128,640]{1,0:T(8,128)(2,1)S(1)}, bf16[128,640]{1,0:T(8,128)(2,1)S(1)}, u32[]{:S(2)}, u32[]{:S(2)}) collective-permute-start(bf16[128,640]{1,0:T(8,128)(2,1)S(1)} %get-tuple-element.25), channel_id=1, source_target_pairs={{0,24},{4,28},{8,16},{12,20},{16,8},{20,12},{24,0},{28,4},{1,25},{... | collective-permute-start | bytes 491528 | tf_op jit(solution)/shard_map/ppermute | solution.py:289
  16.2 0.0 copy-done
  16.2 1.1 %shard_map.71 = (f32[128,512]{1,0:T(8,128)S(1)}, bf16[128,512]{1,0:T(8,128)(2,1)S(1)}) custom-call(bf16[128,2560]{1,0:T(8,128)(2,1)S(1)} %copy-done.1, bf16[640,8,128]{2,1,0:T(8,128)(2,1)S(1)} %copy-done), custom_call_target="tpu_custom_call" | custom-call | flops 268435456 | bytes 65536 | tf_op jit(solution)/shard_map/pallas_call | solution.py:128
  17.3 1.6 %collective-permute-start.4 = (bf16[128,512]{1,0:T(8,128)(2,1)S(1)}, bf16[128,512]{1,0:T(8,128)(2,1)S(1)}, u32[]{:S(2)}, u32[]{:S(2)}) collective-permute-start(bf16[128,512]{1,0:T(8,128)(2,1)S(1)} %get-tuple-element.18), channel_id=1, source_target_pairs={{0,1},{1,0},{2,3},{3,2},{4,5},{5,4},{6,7},{7,6},{8,9},{9,8},{10,11... | collective-permute-start | bytes 393224 | tf_op jit(solution)/shard_map/ppermute | solution.py:289
  18.9 0.0 collective-permute-done.3.far_ref
  18.9 0.0 copy-done.2
  18.9 1.9 %shard_map.70 = (bf16[512,256]{1,0:T(8,128)(2,1)S(1)}, f32[128,256]{1,0:T(8,128)S(1)}, f32[2,128,1024]{2,1,0:T(8,128)S(1)}) custom-call(s32[8,128]{1,0:T(8,128)S(1)} %bitcast.1, bf16[512,256]{1,0:T(8,128)(2,1)S(1)} %shard_map.69.near_ref, bf16[512,256]{1,0:T(8,128)(2,1)S(1)} %collective-permute-done.3.far_ref, bf16[128,512]{1,0:T(8,128)(2,1)S(1)} %shard_map.68.refs_0_, ...), custom_call_target="tpu_custom_call" | custom-call | flops 536870912 | bytes 65536 | tf_op jit(solution)/shard_map/pallas_call | solution.py:128
  20.9 0.0 collective-permute-done.6.refs_1_
  20.9 1.2 %collective-permute-done.7.refs_2_ = bf16[128,640]{1,0:T(8,128)(2,1)S(1)} collective-permute-done((bf16[128,640]{1,0:T(8,128)(2,1)S(1)}, bf16[128,640]{1,0:T(8,128)(2,1)S(1)}, u32[]{:S(2)}, u32[]{:S(2)}) %collective-permute-start.7) | collective-permute-done | bytes 163872 | tf_op jit(solution)/shard_map/ppermute | solution.py:289
  22.1 1.6 %collective-permute-done.8.refs_3_ = bf16[128,640]{1,0:T(8,128)(2,1)S(1)} collective-permute-done((bf16[128,640]{1,0:T(8,128)(2,1)S(1)}, bf16[128,640]{1,0:T(8,128)(2,1)S(1)}, u32[]{:S(2)}, u32[]{:S(2)}) %collective-permute-start.8) | collective-permute-done | bytes 163872 | tf_op jit(solution)/shard_map/ppermute | solution.py:289
  23.7 0.4 %shard_map.75 = (f32[320,256]{1,0:T(8,128)S(1)}, bf16[320,256]{1,0:T(8,128)(2,1)S(1)}) custom-call(bf16[512,256]{1,0:T(8,128)(2,1)S(1)} %get-tuple-element.21.attn_ref, bf16[128,640]{1,0:T(8,128)(2,1)S(1)} %get-tuple-element.22.refs_0_, bf16[128,640]{1,0:T(8,128)(2,1)S(1)} %collective-permute-done.6.refs_1_, ...), custom_call_target="tpu_custom_call" | custom-call | flops 268435456 | bytes 65536 | tf_op jit(solution)/shard_map/pallas_call | solution.py:128
  24.1 0.1 collective-permute-start.9
  24.2 0.0 collective-permute-done.4.got_ref
  24.2 2.7 %collective-permute-start.5 = (bf16[128,256]{1,0:T(8,128)(2,1)S(1)}, bf16[128,256]{1,0:T(8,128)(2,1)S(1)}, u32[]{:S(2)}, u32[]{:S(2)}) collective-permute-start(bf16[128,256]{1,0:T(8,128)(2,1)S(1)} %get-tuple-element.20), channel_id=1, source_target_pairs={{0,2},{1,3},{2,0},{3,1},{4,6},{5,7},{6,4},{7,5},{8,10},{9,11},{10,... | collective-permute-start | bytes 196616 | tf_op jit(solution)/shard_map/ppermute | solution.py:289
  26.9 4.2 %collective-permute-done.5.got_ref = bf16[128,256]{1,0:T(8,128)(2,1)S(1)} collective-permute-done((bf16[128,256]{1,0:T(8,128)(2,1)S(1)}, bf16[128,256]{1,0:T(8,128)(2,1)S(1)}, u32[]{:S(2)}, u32[]{:S(2)}) %collective-permute-start.5) | collective-permute-done | bytes 65568 | tf_op jit(solution)/shard_map/ppermute | solution.py:289
  31.1 0.7 %shard_map.73 = bf16[128,256]{1,0:T(8,128)(2,1)S(1)} custom-call(bf16[512,256]{1,0:T(8,128)(2,1)S(1)} %shard_map.69.near_ref, bf16[512,256]{1,0:T(8,128)(2,1)S(1)} %collective-permute-done.3.far_ref, f32[128,256]{1,0:T(8,128)S(1)} %get-tuple-element.15.full_ref, f32[2,128,1024]{2,1,0:T(8,128)S(1)} %get-tuple-element.16.prob_ref, ...), custom_call_target="tpu_custom_call" | custom-call | flops 268435456 | bytes 65536 | tf_op jit(solution)/shard_map/pallas_call | solution.py:128
  31.8 0.6 %copy.7 = bf16[128,256]{1,0:T(8,128)(2,1)} copy(bf16[128,256]{1,0:T(8,128)(2,1)S(1)} %shard_map.73) | data formatting | bytes 131072
  32.4 0.0 collective-permute-done.9.theirs_ref
  32.4 0.9 %shard_map.76 = f32[320,2,128]{2,1,0:T(2,128)} custom-call(f32[320,256]{1,0:T(8,128)S(1)} %get-tuple-element.26.mine_ref, bf16[320,256]{1,0:T(8,128)(2,1)S(1)} %collective-permute-done.9.theirs_ref), custom_call_target="tpu_custom_call" | custom-call | flops 1048576 | bytes 1048576 | tf_op jit(solution)/shard_map/pallas_call | solution.py:375
  (2 shorter events, 0.0 us)
Async XLA Ops:
  0.6 11.9 %copy-start.1 = (bf16[128,2560]{1,0:T(8,128)(2,1)S(1)}, bf16[128,2560]{1,0:T(8,128)(2,1)}, u32[]{:S(2)}) copy-start(bf16[128,2560]{1,0:T(8,128)(2,1)} %grad_ref.3) | copy-start | bytes 1966084
  1.6 6.9 %collective-permute-start = (bf16[128,512]{1,0:T(8,128)(2,1)S(1)}, bf16[128,512]{1,0:T(8,128)(2,1)S(1)}, u32[]{:S(2)}, u32[]{:S(2)}) collective-permute-start(bf16[128,512]{1,0:T(8,128)(2,1)S(1)} %shard_map.68.refs_0_), channel_id=1, source_target_pairs={{0,8},{4,12},{8,0},{12,4},{16,24},{20,28},{24,16},{28,20},{1,9},{5... | collective-permute-start | bytes 393224 | tf_op jit(solution)/shard_map/ppermute | solution.py:289
  4.6 7.8 %collective-permute-start.1 = (bf16[128,512]{1,0:T(8,128)(2,1)S(1)}, bf16[128,512]{1,0:T(8,128)(2,1)S(1)}, u32[]{:S(2)}, u32[]{:S(2)}) collective-permute-start(bf16[128,512]{1,0:T(8,128)(2,1)S(1)} %shard_map.68.refs_0_), channel_id=1, source_target_pairs={{0,16},{4,20},{8,24},{12,28},{16,0},{20,4},{24,8},{28,12},{1,17},{... | collective-permute-start | bytes 393224 | tf_op jit(solution)/shard_map/ppermute | solution.py:289
  6.2 6.3 %collective-permute-start.2 = (bf16[128,512]{1,0:T(8,128)(2,1)S(1)}, bf16[128,512]{1,0:T(8,128)(2,1)S(1)}, u32[]{:S(2)}, u32[]{:S(2)}) collective-permute-start(bf16[128,512]{1,0:T(8,128)(2,1)S(1)} %shard_map.68.refs_0_), channel_id=1, source_target_pairs={{0,24},{4,28},{8,16},{12,20},{16,8},{20,12},{24,0},{28,4},{1,25},{... | collective-permute-start | bytes 393224 | tf_op jit(solution)/shard_map/ppermute | solution.py:289
  12.4 3.7 %copy-start = (bf16[640,8,128]{2,1,0:T(8,128)(2,1)S(1)}, bf16[640,8,128]{2,1,0:T(8,128)(2,1)}, u32[]{:S(2)}) copy-start(bf16[640,8,128]{2,1,0:T(8,128)(2,1)} %weight_ref.1) | copy-start | bytes 3932164
  12.5 6.5 %collective-permute-start.3 = (bf16[512,256]{1,0:T(8,128)(2,1)S(1)}, bf16[512,256]{1,0:T(8,128)(2,1)S(1)}, u32[]{:S(2)}, u32[]{:S(2)}) collective-permute-start(bf16[512,256]{1,0:T(8,128)(2,1)S(1)} %shard_map.69.near_ref), channel_id=1, source_target_pairs={{0,4},{4,0},{8,12},{12,8},{16,20},{20,16},{24,28},{28,24},{1,5},{5... | collective-permute-start | bytes 786440 | tf_op jit(solution)/shard_map/ppermute | solution.py:289
  12.6 6.3 %copy-start.2 = (s32[1024]{0:T(1024)S(1)}, s32[1024]{0:T(1024)}, u32[]{:S(2)}) copy-start(s32[1024]{0:T(1024)} %param.9) | copy-start | bytes 12292
  12.6 8.2 %collective-permute-start.6 = (bf16[128,640]{1,0:T(8,128)(2,1)S(1)}, bf16[128,640]{1,0:T(8,128)(2,1)S(1)}, u32[]{:S(2)}, u32[]{:S(2)}) collective-permute-start(bf16[128,640]{1,0:T(8,128)(2,1)S(1)} %get-tuple-element.23), channel_id=1, source_target_pairs={{0,8},{4,12},{8,0},{12,4},{16,24},{20,28},{24,16},{28,20},{1,9},{5... | collective-permute-start | bytes 491528 | tf_op jit(solution)/shard_map/ppermute | solution.py:289
  13.9 8.2 %collective-permute-start.7 = (bf16[128,640]{1,0:T(8,128)(2,1)S(1)}, bf16[128,640]{1,0:T(8,128)(2,1)S(1)}, u32[]{:S(2)}, u32[]{:S(2)}) collective-permute-start(bf16[128,640]{1,0:T(8,128)(2,1)S(1)} %get-tuple-element.24), channel_id=1, source_target_pairs={{0,16},{4,20},{8,24},{12,28},{16,0},{20,4},{24,8},{28,12},{1,17},{... | collective-permute-start | bytes 491528 | tf_op jit(solution)/shard_map/ppermute | solution.py:289
  14.7 9.0 %collective-permute-start.8 = (bf16[128,640]{1,0:T(8,128)(2,1)S(1)}, bf16[128,640]{1,0:T(8,128)(2,1)S(1)}, u32[]{:S(2)}, u32[]{:S(2)}) collective-permute-start(bf16[128,640]{1,0:T(8,128)(2,1)S(1)} %get-tuple-element.25), channel_id=1, source_target_pairs={{0,24},{4,28},{8,16},{12,20},{16,8},{20,12},{24,0},{28,4},{1,25},{... | collective-permute-start | bytes 491528 | tf_op jit(solution)/shard_map/ppermute | solution.py:289
  17.3 6.9 %collective-permute-start.4 = (bf16[128,512]{1,0:T(8,128)(2,1)S(1)}, bf16[128,512]{1,0:T(8,128)(2,1)S(1)}, u32[]{:S(2)}, u32[]{:S(2)}) collective-permute-start(bf16[128,512]{1,0:T(8,128)(2,1)S(1)} %get-tuple-element.18), channel_id=1, source_target_pairs={{0,1},{1,0},{2,3},{3,2},{4,5},{5,4},{6,7},{7,6},{8,9},{9,8},{10,11... | collective-permute-start | bytes 393224 | tf_op jit(solution)/shard_map/ppermute | solution.py:289
  24.1 8.3 %collective-permute-start.9 = (bf16[320,256]{1,0:T(8,128)(2,1)S(1)}, bf16[320,256]{1,0:T(8,128)(2,1)S(1)}, u32[]{:S(2)}, u32[]{:S(2)}) collective-permute-start(bf16[320,256]{1,0:T(8,128)(2,1)S(1)} %get-tuple-element.27), channel_id=1, source_target_pairs={{0,4},{4,0},{8,12},{12,8},{16,20},{20,16},{24,28},{28,24},{1,5},{5... | collective-permute-start | bytes 491528 | tf_op jit(solution)/shard_map/ppermute | solution.py:289
  24.2 6.9 %collective-permute-start.5 = (bf16[128,256]{1,0:T(8,128)(2,1)S(1)}, bf16[128,256]{1,0:T(8,128)(2,1)S(1)}, u32[]{:S(2)}, u32[]{:S(2)}) collective-permute-start(bf16[128,256]{1,0:T(8,128)(2,1)S(1)} %get-tuple-element.20), channel_id=1, source_target_pairs={{0,2},{1,3},{2,0},{3,1},{4,6},{5,7},{6,4},{7,5},{8,10},{9,11},{10,... | collective-permute-start | bytes 196616 | tf_op jit(solution)/shard_map/ppermute | solution.py:289

commit v5 on v4

--- a/solution.py
+++ b/solution.py
@@ -254,21 +254,44 @@
         out_ref[:, cols] = (acc * HD ** (-0.5)).astype(bf16)
 
 
-def sums_kernel(attn_ref, *refs):
-    grad_refs, (mine_ref, theirs_ref) = refs[:-2], refs[-2:]
+def early_kernel(attn_ref, first_ref, last_ref, acc_ref):
+    rows = first_ref.shape[0]
+    grads = jnp.concatenate([first_ref[...], last_ref[...]], axis=0)
+    attn = jnp.concatenate([attn_ref[:rows, :], attn_ref[-rows:, :]], axis=0)
+    acc_ref[...] = dot(grads, attn, COLS)
+
+
+def late_kernel(own, acc_ref, attn_ref, *refs):
+    grad_refs, (out_ref, sum_ref) = refs[:-2], refs[-2:]
+    rows, half = grad_refs[0].shape[0], out_ref.shape[0]
     low = lax.axis_index("seq") % 2
-    grads = jnp.concatenate([ref[...] for ref in grad_refs], axis=0)
-    sums = dot(grads, attn_ref[...], COLS)
-    half = sums.shape[0] // 2
-    mine_ref[...] = jnp.where(low == 0, sums[:half], sums[half:])
-    theirs = jnp.where(low == 0, sums[half:], sums[:half])
-    theirs_ref[...] = theirs.astype(theirs_ref.dtype)
-
-
-def add_kernel(mine_ref, theirs_ref, out_ref):
-    for h in range(out_ref.shape[1]):
-        cols = slice(h * HD, (h + 1) * HD)
-        out_ref[:, h, :] = mine_ref[:, cols] + theirs_ref[:, cols].astype(f32)
+    side = low if own else 1 - low
+    base = half // 128 * 128
+    size = 2 * half - base
+    cols = pl.ds(pl.multiple_of(side * base, 128), size)
+    grads = jnp.concatenate([ref[:, cols] for ref in grad_refs], axis=0)
+    sum_ref[...] = dot(grads, attn_ref[rows : rows + grads.shape[0], :], COLS)
+    late = sum_ref[pl.ds(pl.multiple_of(side * (half - base), 8), half), :]
+    early = acc_ref[pl.ds(pl.multiple_of(side * half, 8), half), :]
+    out_ref[...] = (early + late).astype(out_ref.dtype)
+
+
+def add_kernel(mine_ref, theirs_ref, query_ref, query_out, out_ref, sum_ref, sems):
+    pieces = sems.shape[0] - 1
+    rows = mine_ref.shape[0] // pieces
+    copies = [pltpu.make_async_copy(query_ref, query_out, sems.at[pieces])]
+    copies[0].start()
+    for piece in range(pieces):
+        span = slice(piece * rows, (piece + 1) * rows)
+        for h in range(sum_ref.shape[1]):
+            cols = slice(h * HD, (h + 1) * HD)
+            sum_ref[span, h, :] = mine_ref[span, cols] + theirs_ref[span, cols].astype(f32)
+        copies.append(pltpu.make_async_copy(sum_ref.at[span], out_ref.at[span], sems.at[piece]))
+        if piece:
+            copies[piece].start()
+    copies[pieces].start()
+    for copy in copies:
+        copy.wait()
 
 
 def narrow_body(queries, keys_values, out_weight, out_grad, positions, seq_size, head_size):
@@ -351,15 +374,25 @@
             ((head_count, tokens_near, 2 * tokens_near), kind) for kind in (f32, bf16)
         ],
     )
-    mine, theirs = vmem_call(
-        sums_kernel,
-        [((span // 2, width), kind) for kind in (f32, bf16)],
-        1 << 28,
-        12,
-        attn,
-        *grads,
-    )
+    (acc,) = vmem_call(early_kernel, [((span, width), f32)], 1 << 27, 6, attn, grads[0], grads[-1])
+    half = span // 2
+    scratch = [((span - half // 128 * 128, width), f32)]
+
+    def late(own, kind):
+        return vmem_call(
+            functools.partial(late_kernel, own),
+            [((half, width), kind)],
+            1 << 27,
+            6,
+            acc,
+            attn,
+            *grads[1:-1],
+            scratch=scratch,
+        )
+
+    (theirs,) = late(False, bf16)
     theirs = move(theirs, "seq", seq_size, 1)
+    (mine,) = late(True, f32)
     (d_query,) = vmem_call(
         query_kernel,
         [((token_count, width), bf16)],
@@ -372,12 +405,16 @@
         kept,
         got,
     )
-    d_out_weight = pl.pallas_call(
+    shape = (span // 2, head_count, HD)
+    d_query, d_out_weight = pl.pallas_call(
         add_kernel,
-        out_shape=jax.ShapeDtypeStruct((span // 2, head_count, HD), f32),
+        out_shape=[pltpu.HBM((token_count, width), bf16), pltpu.HBM(shape, f32)],
+        in_specs=[pl.BlockSpec(memory_space=pltpu.VMEM)] * 3,
+        out_specs=[pl.BlockSpec(memory_space=pltpu.HBM)] * 2,
+        scratch_shapes=[pltpu.VMEM(shape, f32), pltpu.SemaphoreType.DMA((5,))],
         cost_estimate=pl.CostEstimate(flops=1 << 20, bytes_accessed=1 << 20, transcendentals=0),
         compiler_params=pltpu.CompilerParams(vmem_limit_bytes=4 << 20),
-    )(mine, theirs)
+    )(mine, theirs, d_query)
     return (d_query, d_out_weight)
 
 

time: 33.5 us -> 32.8 us (0.979)
  local copies, waits for them, and re-layouts: 0.65 us -> 0.02 us
  waiting for transfers between devices: 13.3 us -> 12.7 us
  Pallas kernels: 6.04 us -> 6.57 us
    unnamed x7 -> x6, local copies, waits for them, and re-layouts: 0.65 us -> 0.02 us
    ppermute x10, waiting for transfers between devices: 13.3 us -> 12.7 us  [move(): return lax.ppermute(array, axis, xor_pairs(size, mask))]
    pallas_call x7 -> x9, Pallas kernels: 4.16 us -> 4.7 us  [vmem_call(): pl.pallas_call(kernel, out_shape=[pltpu.VMEM(shape, dtype) for shape, dty...]
  transfers between devices with their start and end apart: 10 -> 10, of which waited for: 5 -> 4; matrix products, arithmetic and copies ran while one was open for 2% -> 0% of each run, Pallas kernels for 12% -> 14%
where the time goes in v5:
time: 32.8 us; the launch traced here: 32.6 us
  waiting for transfers between devices  12.7 us (39%)
  starting transfers between devices  12.6 us (38%)
  Pallas kernels  6.57 us (20%)
  between operations  0.76 us (2%)
    ppermute x10, waiting for transfers between devices, move(): return lax.ppermute(array, axis, xor_pairs(size, mask))  12.7 us
    ppermute x10, starting transfers between devices, move(): return lax.ppermute(array, axis, xor_pairs(size, mask))  12.6 us
    pallas_call x9, Pallas kernels, vmem_call(): pl.pallas_call(kernel, out_shape=[pltpu.VMEM(shape, dtype) for shape, dty...  4.7 us
    pallas_call x1, Pallas kernels, narrow_body(): pl.pallas_call(pack_kernel, out_shape=pltpu.VMEM((token_count, 2 * HD + w...  0.96 us
    pallas_call x1, Pallas kernels, narrow_body(): pl.pallas_call(add_kernel, out_shape=[pltpu.HBM((token_count, width), bf1...  0.9 us
  transfers between devices with their start and end apart: 10, of which 4 were waited for; matrix products, arithmetic and copies ran while one was open for 0% of the time, Pallas kernels for 14%

profile of v5, /device:TPU:0, one launch (start us, length us, event | category | flops | bytes accessed | tf_op | source)
XLA Modules:
  0.0 32.6 jit_solution(14564487105320669496)
XLA Ops:
  0.6 0.0 copy-start.1
  0.6 1.0 %shard_map.68.refs_0_ = bf16[128,512]{1,0:T(8,128)(2,1)S(1)} custom-call(bf16[2,128,128]{2,1,0:T(8,128)(2,1)} %kv_ref.1, bf16[128,256]{1,0:T(8,128)(2,1)} %query_ref.1), custom_call_target="tpu_custom_call" | custom-call | flops 4294967296 | bytes 262144 | tf_op jit(solution)/shard_map/pallas_call | solution.py:315
  1.6 3.0 %collective-permute-start = (bf16[128,512]{1,0:T(8,128)(2,1)S(1)}, bf16[128,512]{1,0:T(8,128)(2,1)S(1)}, u32[]{:S(2)}, u32[]{:S(2)}) collective-permute-start(bf16[128,512]{1,0:T(8,128)(2,1)S(1)} %shard_map.68.refs_0_), channel_id=1, source_target_pairs={{0,8},{4,12},{8,0},{12,4},{16,24},{20,28},{24,16},{28,20},{1,9},{5... | collective-permute-start | bytes 393224 | tf_op jit(solution)/shard_map/ppermute | solution.py:312
  4.6 1.5 %collective-permute-start.1 = (bf16[128,512]{1,0:T(8,128)(2,1)S(1)}, bf16[128,512]{1,0:T(8,128)(2,1)S(1)}, u32[]{:S(2)}, u32[]{:S(2)}) collective-permute-start(bf16[128,512]{1,0:T(8,128)(2,1)S(1)} %shard_map.68.refs_0_), channel_id=1, source_target_pairs={{0,16},{4,20},{8,24},{12,28},{16,0},{20,4},{24,8},{28,12},{1,17},{... | collective-permute-start | bytes 393224 | tf_op jit(solution)/shard_map/ppermute | solution.py:312
  6.2 0.0 collective-permute-start.2
  6.2 2.3 %collective-permute-done.refs_1_ = bf16[128,512]{1,0:T(8,128)(2,1)S(1)} collective-permute-done((bf16[128,512]{1,0:T(8,128)(2,1)S(1)}, bf16[128,512]{1,0:T(8,128)(2,1)S(1)}, u32[]{:S(2)}, u32[]{:S(2)}) %collective-permute-start) | collective-permute-done | bytes 131104 | tf_op jit(solution)/shard_map/ppermute | solution.py:312
  8.5 3.9 %collective-permute-done.1.refs_2_ = bf16[128,512]{1,0:T(8,128)(2,1)S(1)} collective-permute-done((bf16[128,512]{1,0:T(8,128)(2,1)S(1)}, bf16[128,512]{1,0:T(8,128)(2,1)S(1)}, u32[]{:S(2)}, u32[]{:S(2)}) %collective-permute-start.1) | collective-permute-done | bytes 131104 | tf_op jit(solution)/shard_map/ppermute | solution.py:312
  12.4 0.0 collective-permute-done.2.refs_3_
  12.4 0.0 copy-start
  12.5 0.1 collective-permute-start.3
  12.5 0.0 copy-done.1
  12.5 0.1 shard_map.71
  12.6 0.0 copy-start.2
  12.6 1.5 %collective-permute-start.4 = (bf16[128,640]{1,0:T(8,128)(2,1)S(1)}, bf16[128,640]{1,0:T(8,128)(2,1)S(1)}, u32[]{:S(2)}, u32[]{:S(2)}) collective-permute-start(bf16[128,640]{1,0:T(8,128)(2,1)S(1)} %get-tuple-element.15), channel_id=1, source_target_pairs={{0,24},{4,28},{8,16},{12,20},{16,8},{20,12},{24,0},{28,4},{1,25},{... | collective-permute-start | bytes 491528 | tf_op jit(solution)/shard_map/ppermute | solution.py:312
  14.2 1.5 %collective-permute-start.5 = (bf16[128,640]{1,0:T(8,128)(2,1)S(1)}, bf16[128,640]{1,0:T(8,128)(2,1)S(1)}, u32[]{:S(2)}, u32[]{:S(2)}) collective-permute-start(bf16[128,640]{1,0:T(8,128)(2,1)S(1)} %get-tuple-element.16), channel_id=1, source_target_pairs={{0,8},{4,12},{8,0},{12,4},{16,24},{20,28},{24,16},{28,20},{1,9},{5... | collective-permute-start | bytes 491528 | tf_op jit(solution)/shard_map/ppermute | solution.py:312
  15.7 0.5 %collective-permute-start.6 = (bf16[128,640]{1,0:T(8,128)(2,1)S(1)}, bf16[128,640]{1,0:T(8,128)(2,1)S(1)}, u32[]{:S(2)}, u32[]{:S(2)}) collective-permute-start(bf16[128,640]{1,0:T(8,128)(2,1)S(1)} %get-tuple-element.17), channel_id=1, source_target_pairs={{0,16},{4,20},{8,24},{12,28},{16,0},{20,4},{24,8},{28,12},{1,17},{... | collective-permute-start | bytes 491528 | tf_op jit(solution)/shard_map/ppermute | solution.py:312
  16.2 0.0 copy-done
  16.2 1.1 %shard_map.75 = (f32[128,512]{1,0:T(8,128)S(1)}, bf16[128,512]{1,0:T(8,128)(2,1)S(1)}) custom-call(bf16[128,2560]{1,0:T(8,128)(2,1)S(1)} %copy-done.1, bf16[640,8,128]{2,1,0:T(8,128)(2,1)S(1)} %copy-done), custom_call_target="tpu_custom_call" | custom-call | flops 268435456 | bytes 65536 | tf_op jit(solution)/shard_map/pallas_call | solution.py:128
  17.3 1.6 %collective-permute-start.8 = (bf16[128,512]{1,0:T(8,128)(2,1)S(1)}, bf16[128,512]{1,0:T(8,128)(2,1)S(1)}, u32[]{:S(2)}, u32[]{:S(2)}) collective-permute-start(bf16[128,512]{1,0:T(8,128)(2,1)S(1)} %get-tuple-element.21), channel_id=1, source_target_pairs={{0,1},{1,0},{2,3},{3,2},{4,5},{5,4},{6,7},{7,6},{8,9},{9,8},{10,11... | collective-permute-start | bytes 393224 | tf_op jit(solution)/shard_map/ppermute | solution.py:312
  18.9 0.0 collective-permute-done.3.far_ref
  19.0 0.0 copy-done.2
  19.0 1.9 %shard_map.70 = (bf16[512,256]{1,0:T(8,128)(2,1)S(1)}, f32[128,256]{1,0:T(8,128)S(1)}, f32[2,128,1024]{2,1,0:T(8,128)S(1)}) custom-call(s32[8,128]{1,0:T(8,128)S(1)} %bitcast.1, bf16[512,256]{1,0:T(8,128)(2,1)S(1)} %shard_map.69.near_ref, bf16[512,256]{1,0:T(8,128)(2,1)S(1)} %collective-permute-done.3.far_ref, bf16[128,512]{1,0:T(8,128)(2,1)S(1)} %shard_map.68.refs_0_, ...), custom_call_target="tpu_custom_call" | custom-call | flops 536870912 | bytes 65536 | tf_op jit(solution)/shard_map/pallas_call | solution.py:128
  20.9 0.0 collective-permute-done.4.last_ref
  20.9 0.3 shard_map.72.acc_ref
  21.2 2.6 %collective-permute-done.5.refs_0_ = bf16[128,640]{1,0:T(8,128)(2,1)S(1)} collective-permute-done((bf16[128,640]{1,0:T(8,128)(2,1)S(1)}, bf16[128,640]{1,0:T(8,128)(2,1)S(1)}, u32[]{:S(2)}, u32[]{:S(2)}) %collective-permute-start.5) | collective-permute-done | bytes 163872 | tf_op jit(solution)/shard_map/ppermute | solution.py:312
  23.8 0.0 collective-permute-done.6.refs_1_
  23.8 0.3 shard_map.74
  24.1 0.1 collective-permute-start.7
  24.2 0.0 collective-permute-done.8.got_ref
  24.2 2.7 %collective-permute-start.9 = (bf16[128,256]{1,0:T(8,128)(2,1)S(1)}, bf16[128,256]{1,0:T(8,128)(2,1)S(1)}, u32[]{:S(2)}, u32[]{:S(2)}) collective-permute-start(bf16[128,256]{1,0:T(8,128)(2,1)S(1)} %get-tuple-element.23), channel_id=1, source_target_pairs={{0,2},{1,3},{2,0},{3,1},{4,6},{5,7},{6,4},{7,5},{8,10},{9,11},{10,... | collective-permute-start | bytes 196616 | tf_op jit(solution)/shard_map/ppermute | solution.py:312
  26.9 0.3 shard_map.73.mine_ref
  27.2 3.9 %collective-permute-done.9.got_ref = bf16[128,256]{1,0:T(8,128)(2,1)S(1)} collective-permute-done((bf16[128,256]{1,0:T(8,128)(2,1)S(1)}, bf16[128,256]{1,0:T(8,128)(2,1)S(1)}, u32[]{:S(2)}, u32[]{:S(2)}) %collective-permute-start.9) | collective-permute-done | bytes 65568 | tf_op jit(solution)/shard_map/ppermute | solution.py:312
  31.1 0.7 %shard_map.77.query_ref = bf16[128,256]{1,0:T(8,128)(2,1)S(1)} custom-call(bf16[512,256]{1,0:T(8,128)(2,1)S(1)} %shard_map.69.near_ref, bf16[512,256]{1,0:T(8,128)(2,1)S(1)} %collective-permute-done.3.far_ref, f32[128,256]{1,0:T(8,128)S(1)} %get-tuple-element.18.full_ref, f32[2,128,1024]{2,1,0:T(8,128)S(1)} %get-tuple-element.19.prob_ref, ...), custom_call_target="tpu_custom_call" | custom-call | flops 268435456 | bytes 65536 | tf_op jit(solution)/shard_map/pallas_call | solution.py:128
  31.7 0.0 collective-permute-done.7.theirs_ref
  31.7 0.9 %shard_map.78 = (bf16[128,256]{1,0:T(8,128)(2,1)}, f32[320,2,128]{2,1,0:T(2,128)}) custom-call(f32[320,256]{1,0:T(8,128)S(1)} %shard_map.73.mine_ref, bf16[320,256]{1,0:T(8,128)(2,1)S(1)} %collective-permute-done.7.theirs_ref, bf16[128,256]{1,0:T(8,128)(2,1)S(1)} %shard_map.77.query_ref), custom_call_target="tpu_custom_call" | custom-call | flops 1048576 | bytes 1048576 | tf_op jit(solution)/shard_map/pallas_call | solution.py:409
  (2 shorter events, 0.0 us)
Async XLA Ops:
  0.6 11.9 %copy-start.1 = (bf16[128,2560]{1,0:T(8,128)(2,1)S(1)}, bf16[128,2560]{1,0:T(8,128)(2,1)}, u32[]{:S(2)}) copy-start(bf16[128,2560]{1,0:T(8,128)(2,1)} %grad_ref.3) | copy-start | bytes 1966084
  1.6 6.9 %collective-permute-start = (bf16[128,512]{1,0:T(8,128)(2,1)S(1)}, bf16[128,512]{1,0:T(8,128)(2,1)S(1)}, u32[]{:S(2)}, u32[]{:S(2)}) collective-permute-start(bf16[128,512]{1,0:T(8,128)(2,1)S(1)} %shard_map.68.refs_0_), channel_id=1, source_target_pairs={{0,8},{4,12},{8,0},{12,4},{16,24},{20,28},{24,16},{28,20},{1,9},{5... | collective-permute-start | bytes 393224 | tf_op jit(solution)/shard_map/ppermute | solution.py:312
  4.6 7.8 %collective-permute-start.1 = (bf16[128,512]{1,0:T(8,128)(2,1)S(1)}, bf16[128,512]{1,0:T(8,128)(2,1)S(1)}, u32[]{:S(2)}, u32[]{:S(2)}) collective-permute-start(bf16[128,512]{1,0:T(8,128)(2,1)S(1)} %shard_map.68.refs_0_), channel_id=1, source_target_pairs={{0,16},{4,20},{8,24},{12,28},{16,0},{20,4},{24,8},{28,12},{1,17},{... | collective-permute-start | bytes 393224 | tf_op jit(solution)/shard_map/ppermute | solution.py:312
  6.2 6.3 %collective-permute-start.2 = (bf16[128,512]{1,0:T(8,128)(2,1)S(1)}, bf16[128,512]{1,0:T(8,128)(2,1)S(1)}, u32[]{:S(2)}, u32[]{:S(2)}) collective-permute-start(bf16[128,512]{1,0:T(8,128)(2,1)S(1)} %shard_map.68.refs_0_), channel_id=1, source_target_pairs={{0,24},{4,28},{8,16},{12,20},{16,8},{20,12},{24,0},{28,4},{1,25},{... | collective-permute-start | bytes 393224 | tf_op jit(solution)/shard_map/ppermute | solution.py:312
  12.4 3.7 %copy-start = (bf16[640,8,128]{2,1,0:T(8,128)(2,1)S(1)}, bf16[640,8,128]{2,1,0:T(8,128)(2,1)}, u32[]{:S(2)}) copy-start(bf16[640,8,128]{2,1,0:T(8,128)(2,1)} %weight_ref.1) | copy-start | bytes 3932164
  12.5 6.5 %collective-permute-start.3 = (bf16[512,256]{1,0:T(8,128)(2,1)S(1)}, bf16[512,256]{1,0:T(8,128)(2,1)S(1)}, u32[]{:S(2)}, u32[]{:S(2)}) collective-permute-start(bf16[512,256]{1,0:T(8,128)(2,1)S(1)} %shard_map.69.near_ref), channel_id=1, source_target_pairs={{0,4},{4,0},{8,12},{12,8},{16,20},{20,16},{24,28},{28,24},{1,5},{5... | collective-permute-start | bytes 786440 | tf_op jit(solution)/shard_map/ppermute | solution.py:312
  12.6 6.3 %copy-start.2 = (s32[1024]{0:T(1024)S(1)}, s32[1024]{0:T(1024)}, u32[]{:S(2)}) copy-start(s32[1024]{0:T(1024)} %param.9) | copy-start | bytes 12292
  12.6 8.2 %collective-permute-start.4 = (bf16[128,640]{1,0:T(8,128)(2,1)S(1)}, bf16[128,640]{1,0:T(8,128)(2,1)S(1)}, u32[]{:S(2)}, u32[]{:S(2)}) collective-permute-start(bf16[128,640]{1,0:T(8,128)(2,1)S(1)} %get-tuple-element.15), channel_id=1, source_target_pairs={{0,24},{4,28},{8,16},{12,20},{16,8},{20,12},{24,0},{28,4},{1,25},{... | collective-permute-start | bytes 491528 | tf_op jit(solution)/shard_map/ppermute | solution.py:312
  14.2 9.6 %collective-permute-start.5 = (bf16[128,640]{1,0:T(8,128)(2,1)S(1)}, bf16[128,640]{1,0:T(8,128)(2,1)S(1)}, u32[]{:S(2)}, u32[]{:S(2)}) collective-permute-start(bf16[128,640]{1,0:T(8,128)(2,1)S(1)} %get-tuple-element.16), channel_id=1, source_target_pairs={{0,8},{4,12},{8,0},{12,4},{16,24},{20,28},{24,16},{28,20},{1,9},{5... | collective-permute-start | bytes 491528 | tf_op jit(solution)/shard_map/ppermute | solution.py:312
  15.7 8.1 %collective-permute-start.6 = (bf16[128,640]{1,0:T(8,128)(2,1)S(1)}, bf16[128,640]{1,0:T(8,128)(2,1)S(1)}, u32[]{:S(2)}, u32[]{:S(2)}) collective-permute-start(bf16[128,640]{1,0:T(8,128)(2,1)S(1)} %get-tuple-element.17), channel_id=1, source_target_pairs={{0,16},{4,20},{8,24},{12,28},{16,0},{20,4},{24,8},{28,12},{1,17},{... | collective-permute-start | bytes 491528 | tf_op jit(solution)/shard_map/ppermute | solution.py:312
  17.3 6.9 %collective-permute-start.8 = (bf16[128,512]{1,0:T(8,128)(2,1)S(1)}, bf16[128,512]{1,0:T(8,128)(2,1)S(1)}, u32[]{:S(2)}, u32[]{:S(2)}) collective-permute-start(bf16[128,512]{1,0:T(8,128)(2,1)S(1)} %get-tuple-element.21), channel_id=1, source_target_pairs={{0,1},{1,0},{2,3},{3,2},{4,5},{5,4},{6,7},{7,6},{8,9},{9,8},{10,11... | collective-permute-start | bytes 393224 | tf_op jit(solution)/shard_map/ppermute | solution.py:312
  24.1 7.6 %collective-permute-start.7 = (bf16[320,256]{1,0:T(8,128)(2,1)S(1)}, bf16[320,256]{1,0:T(8,128)(2,1)S(1)}, u32[]{:S(2)}, u32[]{:S(2)}) collective-permute-start(bf16[320,256]{1,0:T(8,128)(2,1)S(1)} %shard_map.74), channel_id=1, source_target_pairs={{0,4},{4,0},{8,12},{12,8},{16,20},{20,16},{24,28},{28,24},{1,5},{5... | collective-permute-start | bytes 491528 | tf_op jit(solution)/shard_map/ppermute | solution.py:312
  24.2 6.9 %collective-permute-start.9 = (bf16[128,256]{1,0:T(8,128)(2,1)S(1)}, bf16[128,256]{1,0:T(8,128)(2,1)S(1)}, u32[]{:S(2)}, u32[]{:S(2)}) collective-permute-start(bf16[128,256]{1,0:T(8,128)(2,1)S(1)} %get-tuple-element.23), channel_id=1, source_target_pairs={{0,2},{1,3},{2,0},{3,1},{4,6},{5,7},{6,4},{7,5},{8,10},{9,11},{10,... | collective-permute-start | bytes 196616 | tf_op jit(solution)/shard_map/ppermute | solution.py:312

commit v6 on v5

--- a/solution.py
+++ b/solution.py
@@ -175,10 +175,13 @@
     per = heads // size
     for out_ref, masks in zip((kept_ref, sent_ref), split_masks(range(size), 1)):
         for place, mask in enumerate(masks):
-            for h in range(per):
-                weight = flat[pl.ds((head ^ mask) * per + h, rows, stride=heads), :].astype(bf16)
-                start = (place * per + h) * HD
-                out_ref[:, start : start + HD] = dot(cols, weight).astype(out_ref.dtype)
+            weights = [
+                flat[pl.ds((head ^ mask) * per + h, rows, stride=heads), :].astype(bf16)
+                for h in range(per)
+            ]
+            span = slice(place * per * HD, (place + 1) * per * HD)
+            product = dot(cols, jnp.concatenate(weights, axis=1))
+            out_ref[:, span] = product.astype(out_ref.dtype)
 
 
 def blend_kernel(width, bit, kept_ref, got_ref, next_ref, sent_ref):

time: 32.8 us -> 32.8 us (level)
  waiting for transfers between devices: 12.7 us -> 13.1 us
  Pallas kernels: 6.57 us -> 6.2 us
    ppermute x10, waiting for transfers between devices: 12.7 us -> 13.1 us  [move(): return lax.ppermute(array, axis, xor_pairs(size, mask))]
    pallas_call x9, Pallas kernels: 4.7 us -> 4.33 us  [vmem_call(): pl.pallas_call(kernel, out_shape=[pltpu.VMEM(shape, dtype) for shape, dty...]
  transfers between devices with their start and end apart: 10 -> 10, of which waited for: 4 -> 5; matrix products, arithmetic and copies ran while one was open for 0% -> 0% of each run, Pallas kernels for 14% -> 13%
where the time goes in v6:
time: 32.8 us; the launch traced here: 32.6 us
  waiting for transfers between devices  13.1 us (40%)
  starting transfers between devices  12.6 us (38%)
  Pallas kernels  6.2 us (19%)
  between operations  0.76 us (2%)
    ppermute x10, waiting for transfers between devices, move(): return lax.ppermute(array, axis, xor_pairs(size, mask))  13.1 us
    ppermute x10, starting transfers between devices, move(): return lax.ppermute(array, axis, xor_pairs(size, mask))  12.6 us
    pallas_call x9, Pallas kernels, vmem_call(): pl.pallas_call(kernel, out_shape=[pltpu.VMEM(shape, dtype) for shape, dty...  4.33 us
    pallas_call x1, Pallas kernels, narrow_body(): pl.pallas_call(pack_kernel, out_shape=pltpu.VMEM((token_count, 2 * HD + w...  0.96 us
    pallas_call x1, Pallas kernels, narrow_body(): pl.pallas_call(add_kernel, out_shape=[pltpu.HBM((token_count, width), bf1...  0.9 us
  transfers between devices with their start and end apart: 10, of which 5 were waited for; matrix products, arithmetic and copies ran while one was open for 0% of the time, Pallas kernels for 13%

profile of v6, /device:TPU:0, one launch (start us, length us, event | category | flops | bytes accessed | tf_op | source)
XLA Modules:
  0.0 32.6 jit_solution(5016705386927398422)
XLA Ops:
  0.6 0.0 copy-start.1
  0.6 1.0 %shard_map.68.refs_0_ = bf16[128,512]{1,0:T(8,128)(2,1)S(1)} custom-call(bf16[2,128,128]{2,1,0:T(8,128)(2,1)} %kv_ref.1, bf16[128,256]{1,0:T(8,128)(2,1)} %query_ref.1), custom_call_target="tpu_custom_call" | custom-call | flops 4294967296 | bytes 262144 | tf_op jit(solution)/shard_map/pallas_call | solution.py:318
  1.6 3.0 %collective-permute-start = (bf16[128,512]{1,0:T(8,128)(2,1)S(1)}, bf16[128,512]{1,0:T(8,128)(2,1)S(1)}, u32[]{:S(2)}, u32[]{:S(2)}) collective-permute-start(bf16[128,512]{1,0:T(8,128)(2,1)S(1)} %shard_map.68.refs_0_), channel_id=1, source_target_pairs={{0,8},{4,12},{8,0},{12,4},{16,24},{20,28},{24,16},{28,20},{1,9},{5... | collective-permute-start | bytes 393224 | tf_op jit(solution)/shard_map/ppermute | solution.py:315
  4.6 1.5 %collective-permute-start.1 = (bf16[128,512]{1,0:T(8,128)(2,1)S(1)}, bf16[128,512]{1,0:T(8,128)(2,1)S(1)}, u32[]{:S(2)}, u32[]{:S(2)}) collective-permute-start(bf16[128,512]{1,0:T(8,128)(2,1)S(1)} %shard_map.68.refs_0_), channel_id=1, source_target_pairs={{0,16},{4,20},{8,24},{12,28},{16,0},{20,4},{24,8},{28,12},{1,17},{... | collective-permute-start | bytes 393224 | tf_op jit(solution)/shard_map/ppermute | solution.py:315
  6.2 0.0 collective-permute-start.2
  6.2 2.3 %collective-permute-done.refs_1_ = bf16[128,512]{1,0:T(8,128)(2,1)S(1)} collective-permute-done((bf16[128,512]{1,0:T(8,128)(2,1)S(1)}, bf16[128,512]{1,0:T(8,128)(2,1)S(1)}, u32[]{:S(2)}, u32[]{:S(2)}) %collective-permute-start) | collective-permute-done | bytes 131104 | tf_op jit(solution)/shard_map/ppermute | solution.py:315
  8.5 3.9 %collective-permute-done.1.refs_2_ = bf16[128,512]{1,0:T(8,128)(2,1)S(1)} collective-permute-done((bf16[128,512]{1,0:T(8,128)(2,1)S(1)}, bf16[128,512]{1,0:T(8,128)(2,1)S(1)}, u32[]{:S(2)}, u32[]{:S(2)}) %collective-permute-start.1) | collective-permute-done | bytes 131104 | tf_op jit(solution)/shard_map/ppermute | solution.py:315
  12.4 0.0 collective-permute-done.2.refs_3_
  12.4 0.0 copy-start
  12.5 0.1 collective-permute-start.3
  12.5 0.0 copy-done.1
  12.5 0.1 shard_map.71
  12.6 0.0 copy-start.2
  12.6 1.5 %collective-permute-start.4 = (bf16[128,640]{1,0:T(8,128)(2,1)S(1)}, bf16[128,640]{1,0:T(8,128)(2,1)S(1)}, u32[]{:S(2)}, u32[]{:S(2)}) collective-permute-start(bf16[128,640]{1,0:T(8,128)(2,1)S(1)} %get-tuple-element.15), channel_id=1, source_target_pairs={{0,24},{4,28},{8,16},{12,20},{16,8},{20,12},{24,0},{28,4},{1,25},{... | collective-permute-start | bytes 491528 | tf_op jit(solution)/shard_map/ppermute | solution.py:315
  14.2 1.5 %collective-permute-start.5 = (bf16[128,640]{1,0:T(8,128)(2,1)S(1)}, bf16[128,640]{1,0:T(8,128)(2,1)S(1)}, u32[]{:S(2)}, u32[]{:S(2)}) collective-permute-start(bf16[128,640]{1,0:T(8,128)(2,1)S(1)} %get-tuple-element.16), channel_id=1, source_target_pairs={{0,8},{4,12},{8,0},{12,4},{16,24},{20,28},{24,16},{28,20},{1,9},{5... | collective-permute-start | bytes 491528 | tf_op jit(solution)/shard_map/ppermute | solution.py:315
  15.7 0.5 %collective-permute-start.6 = (bf16[128,640]{1,0:T(8,128)(2,1)S(1)}, bf16[128,640]{1,0:T(8,128)(2,1)S(1)}, u32[]{:S(2)}, u32[]{:S(2)}) collective-permute-start(bf16[128,640]{1,0:T(8,128)(2,1)S(1)} %get-tuple-element.17), channel_id=1, source_target_pairs={{0,16},{4,20},{8,24},{12,28},{16,0},{20,4},{24,8},{28,12},{1,17},{... | collective-permute-start | bytes 491528 | tf_op jit(solution)/shard_map/ppermute | solution.py:315
  16.2 0.0 copy-done
  16.2 0.7 %shard_map.75 = (f32[128,512]{1,0:T(8,128)S(1)}, bf16[128,512]{1,0:T(8,128)(2,1)S(1)}) custom-call(bf16[128,2560]{1,0:T(8,128)(2,1)S(1)} %copy-done.1, bf16[640,8,128]{2,1,0:T(8,128)(2,1)S(1)} %copy-done), custom_call_target="tpu_custom_call" | custom-call | flops 268435456 | bytes 65536 | tf_op jit(solution)/shard_map/pallas_call | solution.py:128
  16.9 1.6 %collective-permute-start.8 = (bf16[128,512]{1,0:T(8,128)(2,1)S(1)}, bf16[128,512]{1,0:T(8,128)(2,1)S(1)}, u32[]{:S(2)}, u32[]{:S(2)}) collective-permute-start(bf16[128,512]{1,0:T(8,128)(2,1)S(1)} %get-tuple-element.21), channel_id=1, source_target_pairs={{0,1},{1,0},{2,3},{3,2},{4,5},{5,4},{6,7},{7,6},{8,9},{9,8},{10,11... | collective-permute-start | bytes 393224 | tf_op jit(solution)/shard_map/ppermute | solution.py:315
  18.6 0.0 collective-permute-done.3.far_ref
  18.6 0.0 copy-done.2
  18.6 1.9 %shard_map.70 = (bf16[512,256]{1,0:T(8,128)(2,1)S(1)}, f32[128,256]{1,0:T(8,128)S(1)}, f32[2,128,1024]{2,1,0:T(8,128)S(1)}) custom-call(s32[8,128]{1,0:T(8,128)S(1)} %bitcast.1, bf16[512,256]{1,0:T(8,128)(2,1)S(1)} %shard_map.69.near_ref, bf16[512,256]{1,0:T(8,128)(2,1)S(1)} %collective-permute-done.3.far_ref, bf16[128,512]{1,0:T(8,128)(2,1)S(1)} %shard_map.68.refs_0_, ...), custom_call_target="tpu_custom_call" | custom-call | flops 536870912 | bytes 65536 | tf_op jit(solution)/shard_map/pallas_call | solution.py:128
  20.5 0.2 collective-permute-done.4.last_ref
  20.7 0.3 shard_map.72.acc_ref
  21.0 2.8 %collective-permute-done.5.refs_0_ = bf16[128,640]{1,0:T(8,128)(2,1)S(1)} collective-permute-done((bf16[128,640]{1,0:T(8,128)(2,1)S(1)}, bf16[128,640]{1,0:T(8,128)(2,1)S(1)}, u32[]{:S(2)}, u32[]{:S(2)}) %collective-permute-start.5) | collective-permute-done | bytes 163872 | tf_op jit(solution)/shard_map/ppermute | solution.py:315
  23.8 0.0 collective-permute-done.6.refs_1_
  23.8 0.3 shard_map.74
  24.1 0.1 collective-permute-start.7
  24.2 0.0 collective-permute-done.8.got_ref
  24.2 2.7 %collective-permute-start.9 = (bf16[128,256]{1,0:T(8,128)(2,1)S(1)}, bf16[128,256]{1,0:T(8,128)(2,1)S(1)}, u32[]{:S(2)}, u32[]{:S(2)}) collective-permute-start(bf16[128,256]{1,0:T(8,128)(2,1)S(1)} %get-tuple-element.23), channel_id=1, source_target_pairs={{0,2},{1,3},{2,0},{3,1},{4,6},{5,7},{6,4},{7,5},{8,10},{9,11},{10,... | collective-permute-start | bytes 196616 | tf_op jit(solution)/shard_map/ppermute | solution.py:315
  26.9 0.3 shard_map.73.mine_ref
  27.2 3.9 %collective-permute-done.9.got_ref = bf16[128,256]{1,0:T(8,128)(2,1)S(1)} collective-permute-done((bf16[128,256]{1,0:T(8,128)(2,1)S(1)}, bf16[128,256]{1,0:T(8,128)(2,1)S(1)}, u32[]{:S(2)}, u32[]{:S(2)}) %collective-permute-start.9) | collective-permute-done | bytes 65568 | tf_op jit(solution)/shard_map/ppermute | solution.py:315
  31.1 0.7 %shard_map.77.query_ref = bf16[128,256]{1,0:T(8,128)(2,1)S(1)} custom-call(bf16[512,256]{1,0:T(8,128)(2,1)S(1)} %shard_map.69.near_ref, bf16[512,256]{1,0:T(8,128)(2,1)S(1)} %collective-permute-done.3.far_ref, f32[128,256]{1,0:T(8,128)S(1)} %get-tuple-element.18.full_ref, f32[2,128,1024]{2,1,0:T(8,128)S(1)} %get-tuple-element.19.prob_ref, ...), custom_call_target="tpu_custom_call" | custom-call | flops 268435456 | bytes 65536 | tf_op jit(solution)/shard_map/pallas_call | solution.py:128
  31.7 0.0 collective-permute-done.7.theirs_ref
  31.7 0.9 %shard_map.78 = (bf16[128,256]{1,0:T(8,128)(2,1)}, f32[320,2,128]{2,1,0:T(2,128)}) custom-call(f32[320,256]{1,0:T(8,128)S(1)} %shard_map.73.mine_ref, bf16[320,256]{1,0:T(8,128)(2,1)S(1)} %collective-permute-done.7.theirs_ref, bf16[128,256]{1,0:T(8,128)(2,1)S(1)} %shard_map.77.query_ref), custom_call_target="tpu_custom_call" | custom-call | flops 1048576 | bytes 1048576 | tf_op jit(solution)/shard_map/pallas_call | solution.py:412
  (2 shorter events, 0.0 us)
Async XLA Ops:
  0.6 11.9 %copy-start.1 = (bf16[128,2560]{1,0:T(8,128)(2,1)S(1)}, bf16[128,2560]{1,0:T(8,128)(2,1)}, u32[]{:S(2)}) copy-start(bf16[128,2560]{1,0:T(8,128)(2,1)} %grad_ref.3) | copy-start | bytes 1966084
  1.6 6.9 %collective-permute-start = (bf16[128,512]{1,0:T(8,128)(2,1)S(1)}, bf16[128,512]{1,0:T(8,128)(2,1)S(1)}, u32[]{:S(2)}, u32[]{:S(2)}) collective-permute-start(bf16[128,512]{1,0:T(8,128)(2,1)S(1)} %shard_map.68.refs_0_), channel_id=1, source_target_pairs={{0,8},{4,12},{8,0},{12,4},{16,24},{20,28},{24,16},{28,20},{1,9},{5... | collective-permute-start | bytes 393224 | tf_op jit(solution)/shard_map/ppermute | solution.py:315
  4.6 7.8 %collective-permute-start.1 = (bf16[128,512]{1,0:T(8,128)(2,1)S(1)}, bf16[128,512]{1,0:T(8,128)(2,1)S(1)}, u32[]{:S(2)}, u32[]{:S(2)}) collective-permute-start(bf16[128,512]{1,0:T(8,128)(2,1)S(1)} %shard_map.68.refs_0_), channel_id=1, source_target_pairs={{0,16},{4,20},{8,24},{12,28},{16,0},{20,4},{24,8},{28,12},{1,17},{... | collective-permute-start | bytes 393224 | tf_op jit(solution)/shard_map/ppermute | solution.py:315
  6.2 6.3 %collective-permute-start.2 = (bf16[128,512]{1,0:T(8,128)(2,1)S(1)}, bf16[128,512]{1,0:T(8,128)(2,1)S(1)}, u32[]{:S(2)}, u32[]{:S(2)}) collective-permute-start(bf16[128,512]{1,0:T(8,128)(2,1)S(1)} %shard_map.68.refs_0_), channel_id=1, source_target_pairs={{0,24},{4,28},{8,16},{12,20},{16,8},{20,12},{24,0},{28,4},{1,25},{... | collective-permute-start | bytes 393224 | tf_op jit(solution)/shard_map/ppermute | solution.py:315
  12.4 3.7 %copy-start = (bf16[640,8,128]{2,1,0:T(8,128)(2,1)S(1)}, bf16[640,8,128]{2,1,0:T(8,128)(2,1)}, u32[]{:S(2)}) copy-start(bf16[640,8,128]{2,1,0:T(8,128)(2,1)} %weight_ref.1) | copy-start | bytes 3932164
  12.5 6.1 %collective-permute-start.3 = (bf16[512,256]{1,0:T(8,128)(2,1)S(1)}, bf16[512,256]{1,0:T(8,128)(2,1)S(1)}, u32[]{:S(2)}, u32[]{:S(2)}) collective-permute-start(bf16[512,256]{1,0:T(8,128)(2,1)S(1)} %shard_map.69.near_ref), channel_id=1, source_target_pairs={{0,4},{4,0},{8,12},{12,8},{16,20},{20,16},{24,28},{28,24},{1,5},{5... | collective-permute-start | bytes 786440 | tf_op jit(solution)/shard_map/ppermute | solution.py:315
  12.6 6.0 %copy-start.2 = (s32[1024]{0:T(1024)S(1)}, s32[1024]{0:T(1024)}, u32[]{:S(2)}) copy-start(s32[1024]{0:T(1024)} %param.9) | copy-start | bytes 12292
  12.6 8.0 %collective-permute-start.4 = (bf16[128,640]{1,0:T(8,128)(2,1)S(1)}, bf16[128,640]{1,0:T(8,128)(2,1)S(1)}, u32[]{:S(2)}, u32[]{:S(2)}) collective-permute-start(bf16[128,640]{1,0:T(8,128)(2,1)S(1)} %get-tuple-element.15), channel_id=1, source_target_pairs={{0,24},{4,28},{8,16},{12,20},{16,8},{20,12},{24,0},{28,4},{1,25},{... | collective-permute-start | bytes 491528 | tf_op jit(solution)/shard_map/ppermute | solution.py:315
  14.2 9.6 %collective-permute-start.5 = (bf16[128,640]{1,0:T(8,128)(2,1)S(1)}, bf16[128,640]{1,0:T(8,128)(2,1)S(1)}, u32[]{:S(2)}, u32[]{:S(2)}) collective-permute-start(bf16[128,640]{1,0:T(8,128)(2,1)S(1)} %get-tuple-element.16), channel_id=1, source_target_pairs={{0,8},{4,12},{8,0},{12,4},{16,24},{20,28},{24,16},{28,20},{1,9},{5... | collective-permute-start | bytes 491528 | tf_op jit(solution)/shard_map/ppermute | solution.py:315
  15.7 8.1 %collective-permute-start.6 = (bf16[128,640]{1,0:T(8,128)(2,1)S(1)}, bf16[128,640]{1,0:T(8,128)(2,1)S(1)}, u32[]{:S(2)}, u32[]{:S(2)}) collective-permute-start(bf16[128,640]{1,0:T(8,128)(2,1)S(1)} %get-tuple-element.17), channel_id=1, source_target_pairs={{0,16},{4,20},{8,24},{12,28},{16,0},{20,4},{24,8},{28,12},{1,17},{... | collective-permute-start | bytes 491528 | tf_op jit(solution)/shard_map/ppermute | solution.py:315
  16.9 7.2 %collective-permute-start.8 = (bf16[128,512]{1,0:T(8,128)(2,1)S(1)}, bf16[128,512]{1,0:T(8,128)(2,1)S(1)}, u32[]{:S(2)}, u32[]{:S(2)}) collective-permute-start(bf16[128,512]{1,0:T(8,128)(2,1)S(1)} %get-tuple-element.21), channel_id=1, source_target_pairs={{0,1},{1,0},{2,3},{3,2},{4,5},{5,4},{6,7},{7,6},{8,9},{9,8},{10,11... | collective-permute-start | bytes 393224 | tf_op jit(solution)/shard_map/ppermute | solution.py:315
  24.1 7.6 %collective-permute-start.7 = (bf16[320,256]{1,0:T(8,128)(2,1)S(1)}, bf16[320,256]{1,0:T(8,128)(2,1)S(1)}, u32[]{:S(2)}, u32[]{:S(2)}) collective-permute-start(bf16[320,256]{1,0:T(8,128)(2,1)S(1)} %shard_map.74), channel_id=1, source_target_pairs={{0,4},{4,0},{8,12},{12,8},{16,20},{20,16},{24,28},{28,24},{1,5},{5... | collective-permute-start | bytes 491528 | tf_op jit(solution)/shard_map/ppermute | solution.py:315
  24.2 6.9 %collective-permute-start.9 = (bf16[128,256]{1,0:T(8,128)(2,1)S(1)}, bf16[128,256]{1,0:T(8,128)(2,1)S(1)}, u32[]{:S(2)}, u32[]{:S(2)}) collective-permute-start(bf16[128,256]{1,0:T(8,128)(2,1)S(1)} %get-tuple-element.23), channel_id=1, source_target_pairs={{0,2},{1,3},{2,0},{3,1},{4,6},{5,7},{6,4},{7,5},{8,10},{9,11},{10,... | collective-permute-start | bytes 196616 | tf_op jit(solution)/shard_map/ppermute | solution.py:315

commit v7 on v6

--- a/solution.py
+++ b/solution.py
@@ -137,16 +137,21 @@
 
 
 def pack_kernel(kv_ref, query_ref, out_ref, sems):
-    copies = [
-        pltpu.make_async_copy(source, out_ref.at[:, cols], sems.at[index])
+    pieces = sems.shape[1]
+    rows = out_ref.shape[0] // pieces
+    copies = []
+    for piece in range(pieces):
+        span = slice(piece * rows, (piece + 1) * rows)
         for index, (source, cols) in enumerate(
             (
-                (kv_ref.at[0], slice(0, HD)),
-                (kv_ref.at[1], slice(HD, 2 * HD)),
-                (query_ref, slice(2 * HD, out_ref.shape[1])),
+                (kv_ref.at[0, span], slice(0, HD)),
+                (kv_ref.at[1, span], slice(HD, 2 * HD)),
+                (query_ref.at[span], slice(2 * HD, out_ref.shape[1])),
             )
-        )
-    ]
+        ):
+            copies.append(
+                pltpu.make_async_copy(source, out_ref.at[span, cols], sems.at[index, piece])
+            )
     for copy in copies:
         copy.start()
     for copy in copies:
@@ -320,7 +325,7 @@
         out_shape=pltpu.VMEM((token_count, 2 * HD + width), bf16),
         in_specs=[pl.BlockSpec(memory_space=pltpu.HBM)] * 2,
         out_specs=pl.BlockSpec(memory_space=pltpu.VMEM),
-        scratch_shapes=[pltpu.SemaphoreType.DMA((3,))],
+        scratch_shapes=[pltpu.SemaphoreType.DMA((3, 2))],
         cost_estimate=pl.CostEstimate(flops=1 << 32, bytes_accessed=1 << 18, transcendentals=0),
         compiler_params=pltpu.CompilerParams(vmem_limit_bytes=2 << 20),
     )(

time: 32.8 us -> 32.8 us (level)
  no operation moved by 1% of the time
where the time goes in v7:
time: 32.8 us; the launch traced here: 32.6 us
  waiting for transfers between devices  13.1 us (40%)
  starting transfers between devices  12.6 us (38%)
  Pallas kernels  6.19 us (19%)
  between operations  0.76 us (2%)
    ppermute x10, waiting for transfers between devices, move(): return lax.ppermute(array, axis, xor_pairs(size, mask))  13.1 us
    ppermute x10, starting transfers between devices, move(): return lax.ppermute(array, axis, xor_pairs(size, mask))  12.6 us
    pallas_call x9, Pallas kernels, vmem_call(): pl.pallas_call(kernel, out_shape=[pltpu.VMEM(shape, dtype) for shape, dty...  4.33 us
    pallas_call x1, Pallas kernels, narrow_body(): pl.pallas_call(pack_kernel, out_shape=pltpu.VMEM((token_count, 2 * HD + w...  0.96 us
    pallas_call x1, Pallas kernels, narrow_body(): pl.pallas_call(add_kernel, out_shape=[pltpu.HBM((token_count, width), bf1...  0.9 us
  transfers between devices with their start and end apart: 10, of which 5 were waited for; matrix products, arithmetic and copies ran while one was open for 0% of the time, Pallas kernels for 13%

profile of v7, /device:TPU:0, one launch (start us, length us, event | category | flops | bytes accessed | tf_op | source)
XLA Modules:
  0.0 32.6 jit_solution(15457453372711250318)
XLA Ops:
  0.6 0.0 copy-start.1
  0.6 1.0 %shard_map.68.refs_0_ = bf16[128,512]{1,0:T(8,128)(2,1)S(1)} custom-call(bf16[2,128,128]{2,1,0:T(8,128)(2,1)} %kv_ref.1, bf16[128,256]{1,0:T(8,128)(2,1)} %query_ref.1), custom_call_target="tpu_custom_call" | custom-call | flops 4294967296 | bytes 262144 | tf_op jit(solution)/shard_map/pallas_call | solution.py:323
  1.6 3.0 %collective-permute-start = (bf16[128,512]{1,0:T(8,128)(2,1)S(1)}, bf16[128,512]{1,0:T(8,128)(2,1)S(1)}, u32[]{:S(2)}, u32[]{:S(2)}) collective-permute-start(bf16[128,512]{1,0:T(8,128)(2,1)S(1)} %shard_map.68.refs_0_), channel_id=1, source_target_pairs={{0,8},{4,12},{8,0},{12,4},{16,24},{20,28},{24,16},{28,20},{1,9},{5... | collective-permute-start | bytes 393224 | tf_op jit(solution)/shard_map/ppermute | solution.py:320
  4.6 1.5 %collective-permute-start.1 = (bf16[128,512]{1,0:T(8,128)(2,1)S(1)}, bf16[128,512]{1,0:T(8,128)(2,1)S(1)}, u32[]{:S(2)}, u32[]{:S(2)}) collective-permute-start(bf16[128,512]{1,0:T(8,128)(2,1)S(1)} %shard_map.68.refs_0_), channel_id=1, source_target_pairs={{0,16},{4,20},{8,24},{12,28},{16,0},{20,4},{24,8},{28,12},{1,17},{... | collective-permute-start | bytes 393224 | tf_op jit(solution)/shard_map/ppermute | solution.py:320
  6.2 0.0 collective-permute-start.2
  6.2 2.3 %collective-permute-done.refs_1_ = bf16[128,512]{1,0:T(8,128)(2,1)S(1)} collective-permute-done((bf16[128,512]{1,0:T(8,128)(2,1)S(1)}, bf16[128,512]{1,0:T(8,128)(2,1)S(1)}, u32[]{:S(2)}, u32[]{:S(2)}) %collective-permute-start) | collective-permute-done | bytes 131104 | tf_op jit(solution)/shard_map/ppermute | solution.py:320
  8.5 3.9 %collective-permute-done.1.refs_2_ = bf16[128,512]{1,0:T(8,128)(2,1)S(1)} collective-permute-done((bf16[128,512]{1,0:T(8,128)(2,1)S(1)}, bf16[128,512]{1,0:T(8,128)(2,1)S(1)}, u32[]{:S(2)}, u32[]{:S(2)}) %collective-permute-start.1) | collective-permute-done | bytes 131104 | tf_op jit(solution)/shard_map/ppermute | solution.py:320
  12.4 0.0 collective-permute-done.2.refs_3_
  12.4 0.0 copy-start
  12.5 0.1 collective-permute-start.3
  12.5 0.0 copy-done.1
  12.5 0.1 shard_map.71
  12.6 0.0 copy-start.2
  12.6 1.5 %collective-permute-start.4 = (bf16[128,640]{1,0:T(8,128)(2,1)S(1)}, bf16[128,640]{1,0:T(8,128)(2,1)S(1)}, u32[]{:S(2)}, u32[]{:S(2)}) collective-permute-start(bf16[128,640]{1,0:T(8,128)(2,1)S(1)} %get-tuple-element.15), channel_id=1, source_target_pairs={{0,24},{4,28},{8,16},{12,20},{16,8},{20,12},{24,0},{28,4},{1,25},{... | collective-permute-start | bytes 491528 | tf_op jit(solution)/shard_map/ppermute | solution.py:320
  14.2 1.5 %collective-permute-start.5 = (bf16[128,640]{1,0:T(8,128)(2,1)S(1)}, bf16[128,640]{1,0:T(8,128)(2,1)S(1)}, u32[]{:S(2)}, u32[]{:S(2)}) collective-permute-start(bf16[128,640]{1,0:T(8,128)(2,1)S(1)} %get-tuple-element.16), channel_id=1, source_target_pairs={{0,8},{4,12},{8,0},{12,4},{16,24},{20,28},{24,16},{28,20},{1,9},{5... | collective-permute-start | bytes 491528 | tf_op jit(solution)/shard_map/ppermute | solution.py:320
  15.7 0.5 %collective-permute-start.6 = (bf16[128,640]{1,0:T(8,128)(2,1)S(1)}, bf16[128,640]{1,0:T(8,128)(2,1)S(1)}, u32[]{:S(2)}, u32[]{:S(2)}) collective-permute-start(bf16[128,640]{1,0:T(8,128)(2,1)S(1)} %get-tuple-element.17), channel_id=1, source_target_pairs={{0,16},{4,20},{8,24},{12,28},{16,0},{20,4},{24,8},{28,12},{1,17},{... | collective-permute-start | bytes 491528 | tf_op jit(solution)/shard_map/ppermute | solution.py:320
  16.2 0.0 copy-done
  16.2 0.7 %shard_map.75 = (f32[128,512]{1,0:T(8,128)S(1)}, bf16[128,512]{1,0:T(8,128)(2,1)S(1)}) custom-call(bf16[128,2560]{1,0:T(8,128)(2,1)S(1)} %copy-done.1, bf16[640,8,128]{2,1,0:T(8,128)(2,1)S(1)} %copy-done), custom_call_target="tpu_custom_call" | custom-call | flops 268435456 | bytes 65536 | tf_op jit(solution)/shard_map/pallas_call | solution.py:128
  16.9 1.6 %collective-permute-start.8 = (bf16[128,512]{1,0:T(8,128)(2,1)S(1)}, bf16[128,512]{1,0:T(8,128)(2,1)S(1)}, u32[]{:S(2)}, u32[]{:S(2)}) collective-permute-start(bf16[128,512]{1,0:T(8,128)(2,1)S(1)} %get-tuple-element.21), channel_id=1, source_target_pairs={{0,1},{1,0},{2,3},{3,2},{4,5},{5,4},{6,7},{7,6},{8,9},{9,8},{10,11... | collective-permute-start | bytes 393224 | tf_op jit(solution)/shard_map/ppermute | solution.py:320
  18.6 0.0 collective-permute-done.3.far_ref
  18.6 0.0 copy-done.2
  18.6 1.9 %shard_map.70 = (bf16[512,256]{1,0:T(8,128)(2,1)S(1)}, f32[128,256]{1,0:T(8,128)S(1)}, f32[2,128,1024]{2,1,0:T(8,128)S(1)}) custom-call(s32[8,128]{1,0:T(8,128)S(1)} %bitcast.1, bf16[512,256]{1,0:T(8,128)(2,1)S(1)} %shard_map.69.near_ref, bf16[512,256]{1,0:T(8,128)(2,1)S(1)} %collective-permute-done.3.far_ref, bf16[128,512]{1,0:T(8,128)(2,1)S(1)} %shard_map.68.refs_0_, ...), custom_call_target="tpu_custom_call" | custom-call | flops 536870912 | bytes 65536 | tf_op jit(solution)/shard_map/pallas_call | solution.py:128
  20.5 0.2 collective-permute-done.4.last_ref
  20.7 0.3 shard_map.72.acc_ref
  21.0 2.8 %collective-permute-done.5.refs_0_ = bf16[128,640]{1,0:T(8,128)(2,1)S(1)} collective-permute-done((bf16[128,640]{1,0:T(8,128)(2,1)S(1)}, bf16[128,640]{1,0:T(8,128)(2,1)S(1)}, u32[]{:S(2)}, u32[]{:S(2)}) %collective-permute-start.5) | collective-permute-done | bytes 163872 | tf_op jit(solution)/shard_map/ppermute | solution.py:320
  23.8 0.0 collective-permute-done.6.refs_1_
  23.8 0.3 shard_map.74
  24.1 0.1 collective-permute-start.7
  24.2 0.0 collective-permute-done.8.got_ref
  24.2 2.7 %collective-permute-start.9 = (bf16[128,256]{1,0:T(8,128)(2,1)S(1)}, bf16[128,256]{1,0:T(8,128)(2,1)S(1)}, u32[]{:S(2)}, u32[]{:S(2)}) collective-permute-start(bf16[128,256]{1,0:T(8,128)(2,1)S(1)} %get-tuple-element.23), channel_id=1, source_target_pairs={{0,2},{1,3},{2,0},{3,1},{4,6},{5,7},{6,4},{7,5},{8,10},{9,11},{10,... | collective-permute-start | bytes 196616 | tf_op jit(solution)/shard_map/ppermute | solution.py:320
  26.9 0.3 shard_map.73.mine_ref
  27.2 3.9 %collective-permute-done.9.got_ref = bf16[128,256]{1,0:T(8,128)(2,1)S(1)} collective-permute-done((bf16[128,256]{1,0:T(8,128)(2,1)S(1)}, bf16[128,256]{1,0:T(8,128)(2,1)S(1)}, u32[]{:S(2)}, u32[]{:S(2)}) %collective-permute-start.9) | collective-permute-done | bytes 65568 | tf_op jit(solution)/shard_map/ppermute | solution.py:320
  31.1 0.7 %shard_map.77.query_ref = bf16[128,256]{1,0:T(8,128)(2,1)S(1)} custom-call(bf16[512,256]{1,0:T(8,128)(2,1)S(1)} %shard_map.69.near_ref, bf16[512,256]{1,0:T(8,128)(2,1)S(1)} %collective-permute-done.3.far_ref, f32[128,256]{1,0:T(8,128)S(1)} %get-tuple-element.18.full_ref, f32[2,128,1024]{2,1,0:T(8,128)S(1)} %get-tuple-element.19.prob_ref, ...), custom_call_target="tpu_custom_call" | custom-call | flops 268435456 | bytes 65536 | tf_op jit(solution)/shard_map/pallas_call | solution.py:128
  31.7 0.0 collective-permute-done.7.theirs_ref
  31.7 0.9 %shard_map.78 = (bf16[128,256]{1,0:T(8,128)(2,1)}, f32[320,2,128]{2,1,0:T(2,128)}) custom-call(f32[320,256]{1,0:T(8,128)S(1)} %shard_map.73.mine_ref, bf16[320,256]{1,0:T(8,128)(2,1)S(1)} %collective-permute-done.7.theirs_ref, bf16[128,256]{1,0:T(8,128)(2,1)S(1)} %shard_map.77.query_ref), custom_call_target="tpu_custom_call" | custom-call | flops 1048576 | bytes 1048576 | tf_op jit(solution)/shard_map/pallas_call | solution.py:417
  (2 shorter events, 0.0 us)
Async XLA Ops:
  0.6 11.9 %copy-start.1 = (bf16[128,2560]{1,0:T(8,128)(2,1)S(1)}, bf16[128,2560]{1,0:T(8,128)(2,1)}, u32[]{:S(2)}) copy-start(bf16[128,2560]{1,0:T(8,128)(2,1)} %grad_ref.3) | copy-start | bytes 1966084
  1.6 6.9 %collective-permute-start = (bf16[128,512]{1,0:T(8,128)(2,1)S(1)}, bf16[128,512]{1,0:T(8,128)(2,1)S(1)}, u32[]{:S(2)}, u32[]{:S(2)}) collective-permute-start(bf16[128,512]{1,0:T(8,128)(2,1)S(1)} %shard_map.68.refs_0_), channel_id=1, source_target_pairs={{0,8},{4,12},{8,0},{12,4},{16,24},{20,28},{24,16},{28,20},{1,9},{5... | collective-permute-start | bytes 393224 | tf_op jit(solution)/shard_map/ppermute | solution.py:320
  4.6 7.8 %collective-permute-start.1 = (bf16[128,512]{1,0:T(8,128)(2,1)S(1)}, bf16[128,512]{1,0:T(8,128)(2,1)S(1)}, u32[]{:S(2)}, u32[]{:S(2)}) collective-permute-start(bf16[128,512]{1,0:T(8,128)(2,1)S(1)} %shard_map.68.refs_0_), channel_id=1, source_target_pairs={{0,16},{4,20},{8,24},{12,28},{16,0},{20,4},{24,8},{28,12},{1,17},{... | collective-permute-start | bytes 393224 | tf_op jit(solution)/shard_map/ppermute | solution.py:320
  6.2 6.3 %collective-permute-start.2 = (bf16[128,512]{1,0:T(8,128)(2,1)S(1)}, bf16[128,512]{1,0:T(8,128)(2,1)S(1)}, u32[]{:S(2)}, u32[]{:S(2)}) collective-permute-start(bf16[128,512]{1,0:T(8,128)(2,1)S(1)} %shard_map.68.refs_0_), channel_id=1, source_target_pairs={{0,24},{4,28},{8,16},{12,20},{16,8},{20,12},{24,0},{28,4},{1,25},{... | collective-permute-start | bytes 393224 | tf_op jit(solution)/shard_map/ppermute | solution.py:320
  12.4 3.7 %copy-start = (bf16[640,8,128]{2,1,0:T(8,128)(2,1)S(1)}, bf16[640,8,128]{2,1,0:T(8,128)(2,1)}, u32[]{:S(2)}) copy-start(bf16[640,8,128]{2,1,0:T(8,128)(2,1)} %weight_ref.1) | copy-start | bytes 3932164
  12.5 6.1 %collective-permute-start.3 = (bf16[512,256]{1,0:T(8,128)(2,1)S(1)}, bf16[512,256]{1,0:T(8,128)(2,1)S(1)}, u32[]{:S(2)}, u32[]{:S(2)}) collective-permute-start(bf16[512,256]{1,0:T(8,128)(2,1)S(1)} %shard_map.69.near_ref), channel_id=1, source_target_pairs={{0,4},{4,0},{8,12},{12,8},{16,20},{20,16},{24,28},{28,24},{1,5},{5... | collective-permute-start | bytes 786440 | tf_op jit(solution)/shard_map/ppermute | solution.py:320
  12.6 6.0 %copy-start.2 = (s32[1024]{0:T(1024)S(1)}, s32[1024]{0:T(1024)}, u32[]{:S(2)}) copy-start(s32[1024]{0:T(1024)} %param.9) | copy-start | bytes 12292
  12.6 8.0 %collective-permute-start.4 = (bf16[128,640]{1,0:T(8,128)(2,1)S(1)}, bf16[128,640]{1,0:T(8,128)(2,1)S(1)}, u32[]{:S(2)}, u32[]{:S(2)}) collective-permute-start(bf16[128,640]{1,0:T(8,128)(2,1)S(1)} %get-tuple-element.15), channel_id=1, source_target_pairs={{0,24},{4,28},{8,16},{12,20},{16,8},{20,12},{24,0},{28,4},{1,25},{... | collective-permute-start | bytes 491528 | tf_op jit(solution)/shard_map/ppermute | solution.py:320
  14.2 9.6 %collective-permute-start.5 = (bf16[128,640]{1,0:T(8,128)(2,1)S(1)}, bf16[128,640]{1,0:T(8,128)(2,1)S(1)}, u32[]{:S(2)}, u32[]{:S(2)}) collective-permute-start(bf16[128,640]{1,0:T(8,128)(2,1)S(1)} %get-tuple-element.16), channel_id=1, source_target_pairs={{0,8},{4,12},{8,0},{12,4},{16,24},{20,28},{24,16},{28,20},{1,9},{5... | collective-permute-start | bytes 491528 | tf_op jit(solution)/shard_map/ppermute | solution.py:320
  15.7 8.1 %collective-permute-start.6 = (bf16[128,640]{1,0:T(8,128)(2,1)S(1)}, bf16[128,640]{1,0:T(8,128)(2,1)S(1)}, u32[]{:S(2)}, u32[]{:S(2)}) collective-permute-start(bf16[128,640]{1,0:T(8,128)(2,1)S(1)} %get-tuple-element.17), channel_id=1, source_target_pairs={{0,16},{4,20},{8,24},{12,28},{16,0},{20,4},{24,8},{28,12},{1,17},{... | collective-permute-start | bytes 491528 | tf_op jit(solution)/shard_map/ppermute | solution.py:320
  16.9 7.2 %collective-permute-start.8 = (bf16[128,512]{1,0:T(8,128)(2,1)S(1)}, bf16[128,512]{1,0:T(8,128)(2,1)S(1)}, u32[]{:S(2)}, u32[]{:S(2)}) collective-permute-start(bf16[128,512]{1,0:T(8,128)(2,1)S(1)} %get-tuple-element.21), channel_id=1, source_target_pairs={{0,1},{1,0},{2,3},{3,2},{4,5},{5,4},{6,7},{7,6},{8,9},{9,8},{10,11... | collective-permute-start | bytes 393224 | tf_op jit(solution)/shard_map/ppermute | solution.py:320
  24.1 7.6 %collective-permute-start.7 = (bf16[320,256]{1,0:T(8,128)(2,1)S(1)}, bf16[320,256]{1,0:T(8,128)(2,1)S(1)}, u32[]{:S(2)}, u32[]{:S(2)}) collective-permute-start(bf16[320,256]{1,0:T(8,128)(2,1)S(1)} %shard_map.74), channel_id=1, source_target_pairs={{0,4},{4,0},{8,12},{12,8},{16,20},{20,16},{24,28},{28,24},{1,5},{5... | collective-permute-start | bytes 491528 | tf_op jit(solution)/shard_map/ppermute | solution.py:320
  24.2 6.9 %collective-permute-start.9 = (bf16[128,256]{1,0:T(8,128)(2,1)S(1)}, bf16[128,256]{1,0:T(8,128)(2,1)S(1)}, u32[]{:S(2)}, u32[]{:S(2)}) collective-permute-start(bf16[128,256]{1,0:T(8,128)(2,1)S(1)} %get-tuple-element.23), channel_id=1, source_target_pairs={{0,2},{1,3},{2,0},{3,1},{4,6},{5,7},{6,4},{7,5},{8,10},{9,11},{10,... | collective-permute-start | bytes 196616 | tf_op jit(solution)/shard_map/ppermute | solution.py:320
